TPU v7x, 128 devices: a whole 4x4x4 slice. The times are simulated.
128 devices in a mesh: gx: 2 (over core), gy: 4 (over x), gz: 16 (over z, y).
Axes of the slice: x: 4, y: 4, z: 4, core: 2. Of those that a mesh axis runs over, the one named last changes fastest.
Arguments:
- right_side: float32 [96, 192, 768], P('gx', 'gy', 'gz'), may hold values from -6 to 6
- start_guess: float32 [96, 192, 768], P('gx', 'gy', 'gz'), may hold values from -3 to 3
- reaction: float32 [96, 192, 768], P('gx', 'gy', 'gz'), may hold values from 0.0005 to 0.005
Outputs:
- solution_field: float32 [96, 192, 768], P('gx', 'gy', 'gz')
- residual: float32 [96, 192, 768], P('gx', 'gy', 'gz')
All inputs are finite; a program needn't handle non-finite values.
Results may differ from a plain program's by a relative error of at most 0.0003.
Values sent between devices are 32-bit elements.
A program may use at most 128 MiB of HBM per device.

v0:
```python
import jax
import jax.numpy as jnp
from jax import lax
from jax.sharding import PartitionSpec as P

LEVELS = 5
BOTTOM_ITERS = 6


damping = 6.0 / 7.0


def extended(block, sides, width, periodic):
    for axis, dim in sides:
        count = lax.axis_size(axis)
        forward = [(i, i + 1) for i in range(count - 1)]
        if periodic:
            forward.append((count - 1, 0))
        backward = [(target, source) for source, target in forward]
        low = lax.ppermute(
            lax.slice_in_dim(block, block.shape[dim] - width, None, axis=dim), axis, forward
        )
        high = lax.ppermute(lax.slice_in_dim(block, 0, width, axis=dim), axis, backward)
        block = jnp.concatenate([low, block, high], axis=dim)
    return block


def laid_out(parts, dim):
    lengths = list(parts.shape[1:])
    lengths[dim] *= parts.shape[0]
    return jnp.moveaxis(parts, 0, dim).reshape(lengths)


def gather_together(arrays, axis, dims):
    flat = jnp.concatenate([a.reshape(-1) for a in arrays])
    lines, at, outs = lax.all_gather(flat, axis), 0, []
    for a, dim in zip(arrays, dims):
        parts = lines[:, at : at + a.size].reshape(-1, *a.shape)
        outs.append(laid_out(parts, dim))
        at += a.size
    return tuple(outs)


def stencil(padded, values, shifted, factor):
    beside = padded[2:, 1:-1, 1:-1] + padded[:-2, 1:-1, 1:-1]
    beside = beside + padded[1:-1, 2:, 1:-1] + padded[1:-1, :-2, 1:-1]
    beside = beside + padded[1:-1, 1:-1, 2:] + padded[1:-1, 1:-1, :-2]
    return factor * (6.0 * values - beside) + shifted * values


def operate_fine(values, shifted, factor):
    padded = extended(values, (("gx", 0), ("gy", 1), ("gz", 2)), 1, False)
    return stencil(padded, values, shifted, factor)


def operate_coarse(values, shifted, factor):
    padded = extended(values, (("gx", 0), ("gy", 1), ("gz", 2)), 1, False)
    return stencil(padded, values, shifted, factor)


def operate_whole(values, shifted, factor):
    return stencil(jnp.pad(values, 1), values, shifted, factor)


def coarsen(values):
    size_x, size_y, size_z = values.shape
    blocks = values.reshape(size_x // 2, 2, size_y // 2, 2, size_z // 2, 2)
    return jnp.mean(blocks, axis=(1, 3, 5))


def refine(values):
    size_x, size_y, size_z = values.shape
    spread = jnp.broadcast_to(values[:, None, :, None, :, None], (size_x, 2, size_y, 2, size_z, 2))
    return spread.reshape(2 * size_x, 2 * size_y, 2 * size_z)


def solve_whole(source, shifted, factor):
    estimate = jnp.zeros_like(source)
    leftover = source
    direction = source
    norm_now = jnp.sum(leftover * leftover)
    for repeat_index in range(BOTTOM_ITERS):
        applied = operate_whole(direction, shifted, factor)
        step_length = norm_now / jnp.sum(direction * applied)
        estimate = estimate + step_length * direction
        leftover = leftover - step_length * applied
        norm_next = jnp.sum(leftover * leftover)
        direction = leftover + norm_next / norm_now * direction
        norm_now = norm_next
    return estimate


def bottom(source, shifted, factor):
    gathered = (
        lax.all_gather(source, "gx", axis=0, tiled=True),
        lax.all_gather(shifted, "gx", axis=0, tiled=True),
    )
    gathered = gather_together((gathered[0], gathered[1]), "gy", (1, 1))
    gathered = (
        lax.all_gather(gathered[0], "gz", axis=2, tiled=True),
        lax.all_gather(gathered[1], "gz", axis=2, tiled=True),
    )
    answer = solve_whole(gathered[0], gathered[1], factor)
    size_x, size_y, size_z = source.shape
    corner = (
        lax.axis_index("gx") * size_x,
        lax.axis_index("gy") * size_y,
        lax.axis_index("gz") * size_z,
    )
    return lax.dynamic_slice(answer, corner, (size_x, size_y, size_z))


def vcycle_level(source, shifts, depth_index):
    factor = 0.25**depth_index
    shifted = shifts[depth_index]
    if depth_index == LEVELS - 1:
        return bottom(source, shifted, factor)
    operator = operate_fine if depth_index == 0 else operate_coarse
    diagonal = 6.0 * factor + shifted
    estimate = damping * source / diagonal
    estimate = estimate + damping * (source - operator(estimate, shifted, factor)) / diagonal
    leftover = source - operator(estimate, shifted, factor)
    estimate = estimate + refine(vcycle_level(coarsen(leftover), shifts, depth_index + 1))
    for repeat_index in range(2):
        estimate = estimate + damping * (source - operator(estimate, shifted, factor)) / diagonal
    return estimate


def body(right_side, start_guess, reaction):
    shifts = [reaction]
    for depth_index in range(LEVELS - 1):
        shifts.append(coarsen(shifts[-1]))
    start_residual = right_side - operate_fine(start_guess, reaction, 1.0)
    precond = vcycle_level(start_residual, shifts, 0)
    upper = lax.psum(jnp.sum(start_residual * precond), ("gx", "gy", "gz"))
    applied = operate_fine(precond, reaction, 1.0)
    step_length = upper / lax.psum(jnp.sum(precond * applied), ("gx", "gy", "gz"))
    solution_field = start_guess + step_length * precond
    residual = start_residual - step_length * applied
    return (solution_field, residual)


def solution(mesh):
    placed = (P("gx", "gy", "gz"), P("gx", "gy", "gz"), P("gx", "gy", "gz"))
    return jax.shard_map(
        body,
        mesh=mesh,
        in_specs=placed,
        out_specs=(P("gx", "gy", "gz"), P("gx", "gy", "gz")),
        check_vma=False,
    )
```

profile of v0, /device:TPU:1, one launch (start us, length us, event | category | flops | bytes accessed | tf_op | source)
XLA Modules:
  0.0 883.1 jit_solution(6199730012006355169)
XLA Ops:
  28.2 8.1 multiply_divide_fusion
  65.1 9.3 %fusion.43 = f32[48,48,48]{2,1,0:T(8,128)S(1)} fusion(f32[48,48,48]{2,1,0:T(8,128)} %copy-done.3, f32[48,48,48]{2,1,0:T(8,128)S(1)} %get-tuple-element.22, f32[50,50,1]{2,1,0:T(8,128)} %copy.44, f32[50,1,48]{2,1,0:T(1,128)} %copy-done.37, f32[50,1,48]{2,1,0:T(1,128)} %copy-done.43, f32[1,48,48]{2,1,0:T(8,128)} %copy-done.26, f32[1,48,48]{2,1,0:T(8,128)} %copy-done.30, ...), kind=kLoop, calls=%fused_computation.122 | loop fusion | flops 3538944 | bytes 1827104 | tf_op jit(solution)/shard_map/add | solution.py:121
  96.7 5.4 collective-permute-start.17
  102.1 13.7 %reshape.66 = f32[24,2,24,2,24,2]{5,4,3,2,1,0:T(8,128)} reshape(f32[48,48,48]{2,1,0:T(8,128)S(1)} %copy-done) | data formatting | bytes 884736 | tf_op jit(solution)/shard_map/reshape | solution.py:67
  115.8 10.9 %reduce_sum.199 = f32[24,24,24]{2,1,0:T(8,128)} reduce(f32[24,2,24,2,24,2]{5,4,3,2,1,0:T(8,128)} %reshape.66, f32[]{:T(128)} %constant.24.clone.1), dimensions={1,3,5}, to_apply=%region_1.0 | reduce | flops 96768 | bytes 497668 | tf_op jit(solution)/shard_map/reduce_sum | solution.py:68
  131.5 6.9 fusion.32
  138.4 15.3 %reshape.65 = f32[24,2,24,2,24,2]{5,4,3,2,1,0:T(8,128)} reshape(f32[48,48,48]{2,1,0:T(8,128)} %fusion.32) | data formatting | bytes 884736 | tf_op jit(solution)/shard_map/reshape | solution.py:67
  153.7 10.9 %reduce_sum.198 = f32[24,24,24]{2,1,0:T(8,128)} reduce(f32[24,2,24,2,24,2]{5,4,3,2,1,0:T(8,128)} %reshape.65, f32[]{:T(128)} %constant.24.clone.1), dimensions={1,3,5}, to_apply=%region_0.0 | reduce | flops 96768 | bytes 497668 | tf_op jit(solution)/shard_map/reduce_sum | solution.py:68
  185.6 7.2 collective-permute-done.22
  210.5 7.3 collective-permute-start.29
  252.9 6.5 collective-permute-start.35
  272.4 5.1 collective-permute-start.39
  280.9 7.2 collective-permute-start.41
  316.8 7.1 collective-permute-start.47
  345.7 7.6 collective-permute-start.53
  363.3 9.9 %all-reduce.6 = f32[432]{0:T(512)S(1)} all-reduce(f32[432]{0:T(512)S(1)} %maximum_dynamic-update-slice_fusion), channel_id=2, replica_groups=mesh['gx'=2,'gy'=4,'gz'=16] {'gy'}, use_global_device_ids=true, to_apply=%add.6 | all-reduce | flops 432 | bytes 3456
  376.5 32.1 %all_gather.22 = f32[6,12,48]{1,0,2:T(8,128)} all-gather(f32[6,12,3]{1,0,2:T(8,128)S(1)} %copy.50), channel_id=1, replica_groups=mesh['gx'=2,'gy'=4,'gz'=16] {'gz'}, dimensions={2}, use_global_device_ids=true | all-gather | bytes 14688 | tf_op jit(solution)/shard_map/all_gather | solution.py:100
  414.8 17.9 %all_gather.23 = f32[6,12,48]{1,0,2:T(8,128)} all-gather(f32[6,12,3]{1,0,2:T(8,128)S(1)} %copy.54), channel_id=1, replica_groups=mesh['gx'=2,'gy'=4,'gz'=16] {'gz'}, dimensions={2}, use_global_device_ids=true | all-gather | bytes 14688 | tf_op jit(solution)/shard_map/all_gather | solution.py:101
  481.8 14.6 %collective-permute-start.54 = (f32[1,6,6]{2,1,0:T(8,128)S(1)}, f32[1,6,6]{2,1,0:T(8,128)S(1)}, u32[]{:S(2)}, u32[]{:S(2)}) collective-permute-start(f32[1,6,6]{2,1,0:T(8,128)S(1)} %get-tuple-element.130), channel_id=1, source_target_pairs={{64,0},{65,1},{66,2},{67,3},{68,4},{69,5},{70,6},{71,7},{72,8},{73... | collective-permute-start | bytes 440 | tf_op jit(solution)/shard_map/ppermute | solution.py:23
  604.9 5.8 collective-permute-start.83
  610.7 7.2 collective-permute-done.82
  634.2 6.9 collective-permute-start.89
  641.1 7.0 collective-permute-done.88
  649.4 9.7 %broadcast_in_dim.11 = f32[24,2,24,2,24,2]{5,4,3,2,1,0:T(8,128)} broadcast(f32[24,24,24]{2,1,0:T(8,128)S(1)} %fusion.63), dimensions={0,2,4} | broadcast | bytes 497664 | tf_op jit(solution)/shard_map/broadcast_in_dim | solution.py:73
  659.1 17.3 %reshape.79 = f32[48,48,48]{2,1,0:T(8,128)} reshape(f32[24,2,24,2,24,2]{5,4,3,2,1,0:T(8,128)} %broadcast_in_dim.11) | data formatting | bytes 884736 | tf_op jit(solution)/shard_map/reshape | solution.py:74
  700.2 7.5 collective-permute-start.95
  712.5 6.2 fusion.24
  739.7 6.5 collective-permute-start.101
  749.6 9.3 %fusion.13 = f32[48,48,48]{2,1,0:T(8,128)S(1)} fusion(f32[48,48,48]{2,1,0:T(8,128)} %copy-done.4, f32[48,48,48]{2,1,0:T(8,128)S(1)} %get-tuple-element.22, f32[50,50,1]{2,1,0:T(8,128)} %copy.73, f32[50,1,48]{2,1,0:T(1,128)} %copy-done.39, f32[50,1,48]{2,1,0:T(1,128)} %copy-done.45, f32[1,48,48]{2,1,0:T(8,128)} %copy-done.28, f32[1,48,48]{2,1,0:T(8,128)} %copy-done.32, ...), kind=kLoop, calls=%fused_computation.38 | loop fusion | flops 3538944 | bytes 1827104 | tf_op jit(solution)/shard_map/add | solution.py:125
  781.2 7.7 collective-permute-start.107
  793.8 7.7 multiply_reduce_fusion
  801.5 76.6 %all-reduce.7 = (f32[]{:T(128)}, f32[]{:T(128)}) all-reduce(f32[]{:T(128)} %get-tuple-element.3, f32[]{:T(128)} %get-tuple-element.2), channel_id=1, replica_groups=mesh['gx'=2,'gy'=4,'gz'=16] {'gx','gy','gz'}, use_global_device_ids=true, to_apply=%region_21.22 | all-reduce | flops 2 | bytes 16 | tf_op jit(solution)/shard_map/psum | solution.py:135
  (476 shorter events, 485.2 us)
Async XLA Ops:
  54.1 7.6 collective-permute-start.10
  92.9 33.8 %collective-permute-start.16 = (f32[50,50,1]{1,2,0:T(1,128)}, f32[50,50,1]{1,2,0:T(1,128)}, u32[]{:S(2)}, u32[]{:S(2)}) collective-permute-start(f32[50,50,1]{1,2,0:T(1,128)} %copy.45), channel_id=1, source_target_pairs={{1,0},{2,1},{3,2},{4,3},{5,4},{6,5},{7,6},{8,7},{9,8},{10,9},{11,1... | collective-permute-start | bytes 30008 | tf_op jit(solution)/shard_map/ppermute | solution.py:23
  96.7 32.4 %collective-permute-start.17 = (f32[50,50,1]{1,2,0:T(1,128)}, f32[50,50,1]{1,2,0:T(1,128)}, u32[]{:S(2)}, u32[]{:S(2)}) collective-permute-start(f32[50,50,1]{1,2,0:T(1,128)} %copy.47), channel_id=1, source_target_pairs={{0,1},{1,2},{2,3},{3,4},{4,5},{5,6},{6,7},{7,8},{8,9},{9,10},{10,1... | collective-permute-start | bytes 30008 | tf_op jit(solution)/shard_map/ppermute | solution.py:20
  179.9 13.0 %collective-permute-start.22 = (f32[26,26,1]{2,1,0:T(8,128)S(1)}, f32[26,26,1]{2,1,0:T(8,128)S(1)}, u32[]{:S(2)}, u32[]{:S(2)}) collective-permute-start(f32[26,26,1]{2,1,0:T(8,128)S(1)} %get-tuple-element.65), channel_id=1, source_target_pairs={{1,0},{2,1},{3,2},{4,3},{5,4},{6,5},{7,6},{8,7},{9,8},{10,9},{11,1... | collective-permute-start | bytes 8120 | tf_op jit(solution)/shard_map/ppermute | solution.py:23
  181.2 12.6 %collective-permute-start.23 = (f32[26,26,1]{2,1,0:T(8,128)S(1)}, f32[26,26,1]{2,1,0:T(8,128)S(1)}, u32[]{:S(2)}, u32[]{:S(2)}) collective-permute-start(f32[26,26,1]{2,1,0:T(8,128)S(1)} %get-tuple-element.66), channel_id=1, source_target_pairs={{0,1},{1,2},{2,3},{3,4},{4,5},{5,6},{6,7},{7,8},{8,9},{9,10},{10,1... | collective-permute-start | bytes 8120 | tf_op jit(solution)/shard_map/ppermute | solution.py:20
  209.2 16.2 %collective-permute-start.28 = (f32[26,26,1]{2,1,0:T(8,128)}, f32[26,26,1]{2,1,0:T(8,128)}, u32[]{:S(2)}, u32[]{:S(2)}) collective-permute-start(f32[26,26,1]{2,1,0:T(8,128)} %get-tuple-element.63), channel_id=1, source_target_pairs={{1,0},{2,1},{3,2},{4,3},{5,4},{6,5},{7,6},{8,7},{9,8},{10,9},{11,1... | collective-permute-start | bytes 8120 | tf_op jit(solution)/shard_map/ppermute | solution.py:23
  210.5 14.9 %collective-permute-start.29 = (f32[26,26,1]{2,1,0:T(8,128)}, f32[26,26,1]{2,1,0:T(8,128)}, u32[]{:S(2)}, u32[]{:S(2)}) collective-permute-start(f32[26,26,1]{2,1,0:T(8,128)} %get-tuple-element.64), channel_id=1, source_target_pairs={{0,1},{1,2},{2,3},{3,4},{4,5},{5,6},{6,7},{7,8},{8,9},{9,10},{10,1... | collective-permute-start | bytes 8120 | tf_op jit(solution)/shard_map/ppermute | solution.py:20
  251.6 8.3 collective-permute-start.34
  252.9 8.3 collective-permute-start.35
  279.6 12.1 %collective-permute-start.40 = (f32[14,14,1]{2,1,0:T(8,128)}, f32[14,14,1]{2,1,0:T(8,128)}, u32[]{:S(2)}, u32[]{:S(2)}) collective-permute-start(f32[14,14,1]{2,1,0:T(8,128)} %get-tuple-element.93), channel_id=1, source_target_pairs={{1,0},{2,1},{3,2},{4,3},{5,4},{6,5},{7,6},{8,7},{9,8},{10,9},{11,1... | collective-permute-start | bytes 2360 | tf_op jit(solution)/shard_map/ppermute | solution.py:23
  280.9 10.9 %collective-permute-start.41 = (f32[14,14,1]{2,1,0:T(8,128)}, f32[14,14,1]{2,1,0:T(8,128)}, u32[]{:S(2)}, u32[]{:S(2)}) collective-permute-start(f32[14,14,1]{2,1,0:T(8,128)} %get-tuple-element.94), channel_id=1, source_target_pairs={{0,1},{1,2},{2,3},{3,4},{4,5},{5,6},{6,7},{7,8},{8,9},{9,10},{10,1... | collective-permute-start | bytes 2360 | tf_op jit(solution)/shard_map/ppermute | solution.py:20
  306.8 7.2 collective-permute-start.44
  315.5 9.1 %collective-permute-start.46 = (f32[8,8,1]{2,1,0:T(8,128)}, f32[8,8,1]{2,1,0:T(8,128)}, u32[]{:S(2)}, u32[]{:S(2)}) collective-permute-start(f32[8,8,1]{2,1,0:T(8,128)} %get-tuple-element.123), channel_id=1, source_target_pairs={{1,0},{2,1},{3,2},{4,3},{5,4},{6,5},{7,6},{8,7},{9,8},{10,9},{11,1... | collective-permute-start | bytes 776 | tf_op jit(solution)/shard_map/ppermute | solution.py:23
  316.8 7.8 collective-permute-start.47
  334.1 8.9 %collective-permute-start.50 = (f32[8,1,6]{2,1,0:T(1,128)}, f32[8,1,6]{2,1,0:T(1,128)}, u32[]{:S(2)}, u32[]{:S(2)}) collective-permute-start(f32[8,1,6]{2,1,0:T(1,128)} %get-tuple-element.122), channel_id=1, source_target_pairs={{16,0},{32,16},{48,32},{17,1},{33,17},{49,33},{18,2},{34,18},{50,3... | collective-permute-start | bytes 584 | tf_op jit(solution)/shard_map/ppermute | solution.py:23
  335.4 7.6 collective-permute-start.51
  344.4 11.7 %collective-permute-start.52 = (f32[8,8,1]{2,1,0:T(8,128)}, f32[8,8,1]{2,1,0:T(8,128)}, u32[]{:S(2)}, u32[]{:S(2)}) collective-permute-start(f32[8,8,1]{2,1,0:T(8,128)} %get-tuple-element.119), channel_id=1, source_target_pairs={{1,0},{2,1},{3,2},{4,3},{5,4},{6,5},{7,6},{8,7},{9,8},{10,9},{11,1... | collective-permute-start | bytes 776 | tf_op jit(solution)/shard_map/ppermute | solution.py:23
  345.7 10.5 %collective-permute-start.53 = (f32[8,8,1]{2,1,0:T(8,128)}, f32[8,8,1]{2,1,0:T(8,128)}, u32[]{:S(2)}, u32[]{:S(2)}) collective-permute-start(f32[8,8,1]{2,1,0:T(8,128)} %get-tuple-element.120), channel_id=1, source_target_pairs={{0,1},{1,2},{2,3},{3,4},{4,5},{5,6},{6,7},{7,8},{8,9},{9,10},{10,1... | collective-permute-start | bytes 776 | tf_op jit(solution)/shard_map/ppermute | solution.py:20
  481.8 15.9 %collective-permute-start.54 = (f32[1,6,6]{2,1,0:T(8,128)S(1)}, f32[1,6,6]{2,1,0:T(8,128)S(1)}, u32[]{:S(2)}, u32[]{:S(2)}) collective-permute-start(f32[1,6,6]{2,1,0:T(8,128)S(1)} %get-tuple-element.130), channel_id=1, source_target_pairs={{64,0},{65,1},{66,2},{67,3},{68,4},{69,5},{70,6},{71,7},{72,8},{73... | collective-permute-start | bytes 440 | tf_op jit(solution)/shard_map/ppermute | solution.py:23
  552.1 6.4 collective-permute-start.70
  573.6 6.6 collective-permute-start.76
  574.9 6.5 collective-permute-start.77
  603.6 14.3 %collective-permute-start.82 = (f32[26,26,1]{2,1,0:T(8,128)S(1)}, f32[26,26,1]{2,1,0:T(8,128)S(1)}, u32[]{:S(2)}, u32[]{:S(2)}) collective-permute-start(f32[26,26,1]{2,1,0:T(8,128)S(1)} %get-tuple-element.61), channel_id=1, source_target_pairs={{1,0},{2,1},{3,2},{4,3},{5,4},{6,5},{7,6},{8,7},{9,8},{10,9},{11,1... | collective-permute-start | bytes 8120 | tf_op jit(solution)/shard_map/ppermute | solution.py:23
  604.9 13.9 %collective-permute-start.83 = (f32[26,26,1]{2,1,0:T(8,128)S(1)}, f32[26,26,1]{2,1,0:T(8,128)S(1)}, u32[]{:S(2)}, u32[]{:S(2)}) collective-permute-start(f32[26,26,1]{2,1,0:T(8,128)S(1)} %get-tuple-element.62), channel_id=1, source_target_pairs={{0,1},{1,2},{2,3},{3,4},{4,5},{5,6},{6,7},{7,8},{8,9},{9,10},{10,1... | collective-permute-start | bytes 8120 | tf_op jit(solution)/shard_map/ppermute | solution.py:20
  632.9 15.2 %collective-permute-start.88 = (f32[26,26,1]{2,1,0:T(8,128)S(1)}, f32[26,26,1]{2,1,0:T(8,128)S(1)}, u32[]{:S(2)}, u32[]{:S(2)}) collective-permute-start(f32[26,26,1]{2,1,0:T(8,128)S(1)} %get-tuple-element.59), channel_id=1, source_target_pairs={{1,0},{2,1},{3,2},{4,3},{5,4},{6,5},{7,6},{8,7},{9,8},{10,9},{11,1... | collective-permute-start | bytes 8120 | tf_op jit(solution)/shard_map/ppermute | solution.py:23
  634.2 14.8 %collective-permute-start.89 = (f32[26,26,1]{2,1,0:T(8,128)S(1)}, f32[26,26,1]{2,1,0:T(8,128)S(1)}, u32[]{:S(2)}, u32[]{:S(2)}) collective-permute-start(f32[26,26,1]{2,1,0:T(8,128)S(1)} %get-tuple-element.60), channel_id=1, source_target_pairs={{0,1},{1,2},{2,3},{3,4},{4,5},{5,6},{6,7},{7,8},{8,9},{9,10},{10,1... | collective-permute-start | bytes 8120 | tf_op jit(solution)/shard_map/ppermute | solution.py:20
  696.4 11.3 %collective-permute-start.94 = (f32[50,50,1]{1,2,0:T(1,128)}, f32[50,50,1]{1,2,0:T(1,128)}, u32[]{:S(2)}, u32[]{:S(2)}) collective-permute-start(f32[50,50,1]{1,2,0:T(1,128)} %copy.66), channel_id=1, source_target_pairs={{1,0},{2,1},{3,2},{4,3},{5,4},{6,5},{7,6},{8,7},{9,8},{10,9},{11,1... | collective-permute-start | bytes 30008 | tf_op jit(solution)/shard_map/ppermute | solution.py:23
  700.2 9.9 %collective-permute-start.95 = (f32[50,50,1]{1,2,0:T(1,128)}, f32[50,50,1]{1,2,0:T(1,128)}, u32[]{:S(2)}, u32[]{:S(2)}) collective-permute-start(f32[50,50,1]{1,2,0:T(1,128)} %copy.68), channel_id=1, source_target_pairs={{0,1},{1,2},{2,3},{3,4},{4,5},{5,6},{6,7},{7,8},{8,9},{9,10},{10,1... | collective-permute-start | bytes 30008 | tf_op jit(solution)/shard_map/ppermute | solution.py:20
  736.5 9.7 %collective-permute-start.100 = (f32[50,50,1]{1,2,0:T(1,128)S(1)}, f32[50,50,1]{1,2,0:T(1,128)S(1)}, u32[]{:S(2)}, u32[]{:S(2)}) collective-permute-start(f32[50,50,1]{1,2,0:T(1,128)S(1)} %copy.70), channel_id=1, source_target_pairs={{1,0},{2,1},{3,2},{4,3},{5,4},{6,5},{7,6},{8,7},{9,8},{10,9},{11,1... | collective-permute-start | bytes 30008 | tf_op jit(solution)/shard_map/ppermute | solution.py:23
  739.7 8.2 collective-permute-start.101
  777.4 11.5 %collective-permute-start.106 = (f32[50,50,1]{1,2,0:T(1,128)}, f32[50,50,1]{1,2,0:T(1,128)}, u32[]{:S(2)}, u32[]{:S(2)}) collective-permute-start(f32[50,50,1]{1,2,0:T(1,128)} %copy.74), channel_id=1, source_target_pairs={{1,0},{2,1},{3,2},{4,3},{5,4},{6,5},{7,6},{8,7},{9,8},{10,9},{11,1... | collective-permute-start | bytes 30008 | tf_op jit(solution)/shard_map/ppermute | solution.py:23
  781.2 10.2 %collective-permute-start.107 = (f32[50,50,1]{1,2,0:T(1,128)}, f32[50,50,1]{1,2,0:T(1,128)}, u32[]{:S(2)}, u32[]{:S(2)}) collective-permute-start(f32[50,50,1]{1,2,0:T(1,128)} %copy.76), channel_id=1, source_target_pairs={{0,1},{1,2},{2,3},{3,4},{4,5},{5,6},{6,7},{7,8},{8,9},{9,10},{10,1... | collective-permute-start | bytes 30008 | tf_op jit(solution)/shard_map/ppermute | solution.py:20
  (127 other events, 749.6 us)
where the time goes:
time: 898 us; the launch traced here: 883 us
  starting transfers between devices  332 us (37%)
  local copies, waits for them, and re-layouts  172 us (19%)
  other arithmetic  144 us (16%)
  blocking collectives  140 us (16%)
  waiting for transfers between devices  74.2 us (8%)
  between operations  19.6 us (2%)
    ppermute x54, starting transfers between devices, extended(): lax.ppermute(lax.slice_in_dim(block, block.shape[dim] - width, None, axis...  211 us
    ppermute x54, starting transfers between devices, extended(): lax.ppermute(lax.slice_in_dim(block, 0, width, axis=dim), axis, backward)  121 us
    psum x1, blocking collectives, body(): upper = lax.psum(jnp.sum(start_residual * precond), ('gx', 'gy', 'gz'))  76.6 us
    ppermute x54, waiting for transfers between devices, extended(): lax.ppermute(lax.slice_in_dim(block, block.shape[dim] - width, None, axis...  51 us
    reshape x5, local copies, waits for them, and re-layouts, coarsen(): blocks = values.reshape(size_x // 2, 2, size_y // 2, 2, size_z // 2, 2)  36.5 us
    reduce_sum x8, other arithmetic, coarsen(): return jnp.mean(blocks, axis=(1, 3, 5))  34.2 us
    all_gather x1, blocking collectives, bottom(): lax.all_gather(gathered[0], 'gz', axis=2, tiled=True)  32.1 us
    add x12, other arithmetic, vcycle_level(): estimate + damping * (source - operator(estimate, shifted, factor)) / dia...  30 us
  transfers between devices with their start and end apart: 108, of which 47 were waited for; matrix products, arithmetic and copies ran while one was open for 7% of the time, Pallas kernels for 0%

commit v1 on v0

v1 whole, which is shorter than its diff:
```python
import functools

import jax
import jax.numpy as jnp
from jax import lax
from jax.experimental import pallas as pl
from jax.experimental.pallas import tpu as pltpu
from jax.sharding import PartitionSpec as P

MESH = pl.DeviceIdType.MESH
F32 = jnp.float32
BF16 = jnp.bfloat16
DAMP = 6.0 / 7.0
GUARD = 8
BOTTOM_ITERS = 6


class Geo:
    def __init__(self, nx, ny, nz, halo, rows, y0, depth):
        self.nx, self.ny, self.nz, self.halo, self.R, self.y0 = nx, ny, nz, halo, rows, y0
        self.factor = 0.25**depth
        self.total = 2 * GUARD + (nx + 2 * halo) * rows

    def row(self, x, y):
        return GUARD + (self.halo + x) * self.R + self.y0 + y


L0 = Geo(24, 48, 48, 4, 56, 4, 0)
L1 = Geo(12, 24, 24, 6, 40, 8, 1)
L2 = Geo(6, 12, 12, 5, 24, 6, 2)
FACTOR3 = 0.25**3
FACTOR4 = 0.25**4


def lanes(rows):
    return lax.broadcasted_iota(jnp.int32, (rows, 128), 1)


def iota2(shape, dim):
    return lax.broadcasted_iota(jnp.int32, shape, dim)


def roll(v, shift):
    shift = shift % 128
    return v if shift == 0 else pltpu.roll(v, shift, 1)


def split3(a):
    hi = a.astype(BF16)
    rest = a - hi.astype(F32)
    mid = rest.astype(BF16)
    low = (rest - mid.astype(F32)).astype(BF16)
    return hi, mid, low


def mm(a, b):
    parts = split3(a)
    out = [jnp.dot(p, b, preferred_element_type=F32) for p in parts]
    return out[0] + (out[1] + out[2])


def beside_of(ref, r, R):
    c = ref[pl.ds(r, R), :]
    b = ref[pl.ds(r + R, R), :] + ref[pl.ds(r - R, R), :]
    b = b + (ref[pl.ds(r + 1, R), :] + ref[pl.ds(r - 1, R), :])
    b = b + (roll(c, 1) + roll(c, -1))
    return c, b


def image_of(ref, s_ref, g, r):
    c, b = beside_of(ref, r, g.R)
    return c, g.factor * (6.0 * c - b) + s_ref[pl.ds(r, g.R), :] * c


def planes(g, a, b, body):
    def step(i, carry):
        body(pl.multiple_of(GUARD + i * g.R, 8), i)
        return carry

    lax.fori_loop(g.halo + a, g.halo + b, step, 0)


def inverse(s, factor):
    return jnp.where(s > 0.0, DAMP / (6.0 * factor + s), 0.0)


def relax(g, src, dst, f, s, inv, a, b):
    def body(r, i):
        c, image = image_of(src, s, g, r)
        at = pl.ds(r, g.R)
        dst[at, :] = c + inv[at, :] * (f[at, :] - image)

    planes(g, a, b, body)


def first(g, dst, f, inv, a, b):
    def body(r, i):
        at = pl.ds(r, g.R)
        dst[at, :] = inv[at, :] * f[at, :]

    planes(g, a, b, body)


def leftover(g, src, dst, f, s, a, b):
    def body(r, i):
        c, image = image_of(src, s, g, r)
        at = pl.ds(r, g.R)
        dst[at, :] = f[at, :] - image

    planes(g, a, b, body)


def restrict(src, gs, dst, gd, x0, x1, y0, count, matrix, tmp):
    step = -(-count // 8) * 8
    for x in range(x0, x1):
        r = gs.row(2 * x, 2 * y0)
        t = src[pl.ds(r, count, stride=2), :] + src[pl.ds(r + 1, count, stride=2), :]
        r = r + gs.R
        t = t + (src[pl.ds(r, count, stride=2), :] + src[pl.ds(r + 1, count, stride=2), :])
        tmp[pl.ds((x - x0) * step, count), :] = t
    for x in range(x0, x1):
        out = mm(tmp[pl.ds((x - x0) * step, step), :], matrix[...])
        dst[pl.ds(gd.row(x, y0), count), :] = out[0:count]


def prolong(src, gc, dst, gf, x0, x1, y0, count, matrix, tmp):
    for x in range(x0, x1):
        o = (x - x0) * 56
        u = mm(src[pl.ds(gc.row(x, y0), count), :], matrix[...])
        tmp[pl.ds(o, count, stride=2), :] = u
        tmp[pl.ds(o + 1, count, stride=2), :] = u
    for x in range(x0, x1):
        o = (x - x0) * 56
        v = tmp[pl.ds(o, 2 * count), :]
        for k in range(2):
            at = pl.ds(gf.row(2 * x + k, 2 * y0), 2 * count)
            dst[at, :] = dst[at, :] + v


class Item:
    def __init__(self, geo, w, diamond):
        self.g, self.w, self.diamond = geo, w, diamond
        self.slots = 64 // w
        self.wz = w - 1 if diamond else w
        self.wd = w - 2 if diamond else w
        self.ztiles = -(-(geo.nx + 2 * self.wz) // self.slots)

    def wy(self, d):
        return self.w - d if self.diamond else self.w


class Plan:
    def __init__(self, items):
        self.items = items
        self.yrows = sum(it.g.nx + 2 * it.wy(d) for it in items for d in range(1, it.w + 1))
        self.yrows = -(-self.yrows // 8) * 8
        self.zrows = sum(it.ztiles * it.g.ny for it in items)
        self.zrows = -(-self.zrows // 8) * 8
        self.drows = max(it.g.nx + 2 * it.wd for it in items)
        self.drows = -(-self.drows // 8) * 8
        assert sum(it.w * it.w for it in items) <= 64

    def scratch(self):
        x = [pltpu.VMEM((it.w * it.g.R, 128), F32) for it in self.items]
        return x + [
            pltpu.VMEM((2, self.yrows, 128), F32),
            pltpu.VMEM((2, self.yrows, 128), F32),
            pltpu.VMEM((2, self.zrows, 128), F32),
            pltpu.VMEM((2, self.zrows, 128), F32),
            pltpu.VMEM((4, self.drows, 128), F32),
            pltpu.VMEM((4, self.drows, 128), F32),
            pltpu.SemaphoreType.DMA((11,)),
            pltpu.SemaphoreType.DMA((11,)),
        ]


class Exchange:
    def __init__(self, plan, refs, scratch, place):
        n = len(plan.items)
        self.plan, self.refs, self.place = plan, refs, place
        self.xr = scratch[:n]
        self.ys, self.yr, self.zs, self.zr, self.ds, self.dr, self.ss, self.rs = scratch[n:]
        gx, gy, gz = place.me
        self.x_copies = []
        for k, it in enumerate(plan.items):
            g = it.g
            start = jnp.where(gx == 0, g.nx - it.w, 0)
            r = pl.multiple_of(GUARD + (g.halo + start) * g.R, 8)
            self.x_copies.append(
                self.copy(refs[k].at[pl.ds(r, it.w * g.R), :], self.xr[k], k, (1 - gx, gy, gz))
            )
        self.copies = []
        for d in range(2):
            self.copies.append(self.copy(self.ys.at[d], self.yr.at[d], 3 + d, place.beside(0, 1 - 2 * d, 0)))
            self.copies.append(self.copy(self.zs.at[d], self.zr.at[d], 5 + d, place.beside(0, 0, 1 - 2 * d)))
            for e in range(2):
                self.copies.append(
                    self.copy(
                        self.ds.at[2 * d + e], self.dr.at[2 * d + e], 7 + 2 * d + e,
                        place.beside(0, 1 - 2 * d, 1 - 2 * e),
                    )
                )

    def copy(self, src, dst, k, peer):
        return pltpu.make_async_remote_copy(
            src_ref=src, dst_ref=dst, send_sem=self.ss.at[k], recv_sem=self.rs.at[k],
            device_id=peer, device_id_type=MESH,
        )

    def x_send(self):
        for c in self.x_copies:
            c.start()

    def x_fill(self):
        for c in self.x_copies:
            c.wait()
        m0, m1 = self.place.x_masks
        for k, it in enumerate(self.plan.items):
            g, w, ref = it.g, it.w, self.refs[k]
            upper = lanes(g.R) >= 64
            for j in range(w):
                got = self.xr[k][pl.ds(j * g.R, g.R), :]
                top = ref[pl.ds(GUARD + (g.halo + g.nx - w + j) * g.R, g.R), :]
                low = ref[pl.ds(GUARD + (g.halo + j) * g.R, g.R), :]
                ref[pl.ds(GUARD + (g.halo - w + j) * g.R, g.R), :] = roll(jnp.where(upper, got * m1, top), 64)
                ref[pl.ds(GUARD + (g.halo + g.nx + j) * g.R, g.R), :] = roll(jnp.where(upper, low, got * m0), 64)

    def pack_send(self):
        yo, zo, co = 0, 0, 0
        corner = [None] * 4
        for k, it in enumerate(self.plan.items):
            g, w, ref = it.g, it.w, self.refs[k]
            for d in range(1, w + 1):
                n = g.nx + 2 * it.wy(d)
                for e, y in enumerate((g.ny - d, d - 1)):
                    self.ys[e, pl.ds(yo, n), :] = ref[pl.ds(g.row(-it.wy(d), y), n, stride=g.R), :]
                yo += n
            lane = lanes(self.plan.drows) & 63
            for d in range(1, w + 1):
                at = co + (d - 1) * w
                pick = (lane >= at) & (lane < at + w)
                for e, y in enumerate((g.ny - d, d - 1)):
                    n = g.nx + 2 * it.wd
                    v = ref[pl.ds(g.row(-it.wd, y), n, stride=g.R), :]
                    if n < self.plan.drows:
                        v = jnp.concatenate([v, jnp.zeros((self.plan.drows - n, 128), F32)], axis=0)
                    for q, z in enumerate((g.nz - w, 0)):
                        moved = roll(v, at - z)
                        old = corner[2 * e + q]
                        corner[2 * e + q] = moved if old is None else jnp.where(pick, moved, old)
            co += w * w
            lane = lanes(g.ny) & 63
            count = g.nx + 2 * it.wz
            for t in range(it.ztiles):
                acc = [None, None]
                for j in range(min(it.slots, count - t * it.slots)):
                    x = t * it.slots + j - it.wz
                    v = ref[pl.ds(g.row(x, 0), g.ny), :]
                    pick = (lane >= j * w) & (lane < j * w + w)
                    for q, z in enumerate((g.nz - w, 0)):
                        moved = roll(v, j * w - z)
                        acc[q] = moved if j == 0 else jnp.where(pick, moved, acc[q])
                for q in range(2):
                    self.zs[q, pl.ds(zo, g.ny), :] = acc[q]
                zo += g.ny
        for q in range(4):
            self.ds[q] = corner[q]
        for c in self.copies:
            c.start()

    def unpack(self):
        for c in self.copies:
            c.wait()
        my, mz = self.place.y_masks, self.place.z_masks
        yo, zo, co = 0, 0, 0
        for k, it in enumerate(self.plan.items):
            g, w, ref = it.g, it.w, self.refs[k]
            for d in range(1, w + 1):
                n = g.nx + 2 * it.wy(d)
                for e, y in enumerate((-d, g.ny + d - 1)):
                    ref[pl.ds(g.row(-it.wy(d), y), n, stride=g.R), :] = self.yr[e, pl.ds(yo, n), :] * my[e]
                yo += n
            n = g.nx + 2 * it.wd
            lane = lanes(n) & 63
            into = (lane >= 64 - w, (lane >= g.nz) & (lane < g.nz + w))
            for d in range(1, w + 1):
                at = co + (d - 1) * w
                for e, y in enumerate((-d, g.ny + d - 1)):
                    rows = pl.ds(g.row(-it.wd, y), n, stride=g.R)
                    v = ref[rows, :]
                    for q, z in enumerate((-w, g.nz)):
                        got = self.dr[2 * e + q, pl.ds(0, n), :] * (my[e] * mz[q])
                        v = jnp.where(into[q], roll(got, z - at), v)
                    ref[rows, :] = v
            co += w * w
            lane = lanes(g.ny) & 63
            into = (lane >= 64 - w, (lane >= g.nz) & (lane < g.nz + w))
            count = g.nx + 2 * it.wz
            for t in range(it.ztiles):
                got = [self.zr[q, pl.ds(zo, g.ny), :] * mz[q] for q in range(2)]
                for j in range(min(it.slots, count - t * it.slots)):
                    x = t * it.slots + j - it.wz
                    rows = pl.ds(g.row(x, 0), g.ny)
                    v = ref[rows, :]
                    for q, z in enumerate((-w, g.nz)):
                        v = jnp.where(into[q], roll(got[q], z - j * w), v)
                    ref[rows, :] = v
                zo += g.ny


class Place:
    def __init__(self, sizes):
        self.sizes = sizes
        self.me = tuple(lax.axis_index(a) for a in ("gx", "gy", "gz"))
        gx, gy, gz = self.me
        one = lambda c: jnp.where(c, 1.0, 0.0).astype(F32)
        self.x_masks = (one(gx == 0), one(gx == 1))
        self.y_masks = (one(gy > 0), one(gy < sizes[1] - 1))
        self.z_masks = (one(gz > 0), one(gz < sizes[2] - 1))

    def beside(self, dx, dy, dz):
        return tuple(
            lax.rem(m + d % n, n) if d % n else m for m, d, n in zip(self.me, (dx, dy, dz), self.sizes)
        )


class Gather:
    def __init__(self, place, scratch):
        self.place = place
        self.mine, self.got, self.sum, self.s1, self.r1, self.s2, self.r2 = scratch
        n = place.sizes
        self.near = [(a, b) for a in range(n[0]) for b in range(n[1])][1:]

    def first_copies(self):
        n = self.place.sizes
        out = []
        for a, b in self.near:
            k = a * n[1] + b
            out.append(
                pltpu.make_async_remote_copy(
                    src_ref=self.mine, dst_ref=self.got.at[k], send_sem=self.s1.at[k], recv_sem=self.r1.at[k],
                    device_id=self.place.beside(a, b, 0), device_id_type=MESH,
                )
            )
        return out

    def second_copies(self, target):
        out = []
        for c in range(1, self.place.sizes[2]):
            out.append(
                pltpu.make_async_remote_copy(
                    src_ref=self.sum, dst_ref=target(c), send_sem=self.s2.at[c], recv_sem=self.r2.at[c],
                    device_id=self.place.beside(0, 0, c), device_id_type=MESH,
                )
            )
        return out

    def send(self):
        for c in self.first_copies():
            c.start()

    def relay(self, target):
        for c in self.first_copies():
            c.wait()
        total = self.mine[...]
        n = self.place.sizes
        for a, b in self.near:
            total = total + self.got[a * n[1] + b]
        self.sum[...] = total
        for c in self.second_copies(target):
            c.start()
        return total

    def finish(self, target):
        for c in self.second_copies(target):
            c.wait()


def gather_scratch(sizes, rows):
    near = sizes[0] * sizes[1]
    return [
        pltpu.VMEM((rows, 128), F32),
        pltpu.VMEM((near, rows, 128), F32),
        pltpu.VMEM((rows, 128), F32),
        pltpu.SemaphoreType.DMA((near,)),
        pltpu.SemaphoreType.DMA((near,)),
        pltpu.SemaphoreType.DMA((sizes[2],)),
        pltpu.SemaphoreType.DMA((sizes[2],)),
    ]


def to_level3(src, mine, square, turned, place):
    g = L2
    gx, gy, gz = place.me
    for i in range(3):
        r = g.row(2 * i, 0)
        t = src[pl.ds(r, 6, stride=2), :] + src[pl.ds(r + 1, 6, stride=2), :]
        r = r + g.R
        t = t + (src[pl.ds(r, 6, stride=2), :] + src[pl.ds(r + 1, 6, stride=2), :])
        square[pl.ds(8 * i, 6), :] = t
    turned[...] = jnp.transpose(square[...])
    a = turned[pl.ds(0, 8, stride=2), :] + turned[pl.ds(1, 8, stride=2), :]
    b = turned[pl.ds(64, 8, stride=2), :] + turned[pl.ds(65, 8, stride=2), :]
    a = (a + roll(b, 64)) * 0.125
    r = iota2((128, 384), 0)
    l = iota2((128, 384), 1)
    x = 6 * gx + 3 * (r >> 6) + ((r & 63) >> 3)
    y = 6 * gy + (r & 7)
    hit = (x == (l >> 5)) & (y == (l & 31)) & ((r & 7) < 6) & ((r & 63) < 24)
    out = mm(a, jnp.where(hit, 1.0, 0.0).astype(BF16))
    for k in range(3):
        mine[pl.ds(k, 6, stride=4), :] = out[0:6, 128 * k : 128 * k + 128]


def image3(ref, s_ref, r, n):
    lane = lanes(n)
    c = ref[pl.ds(r, n), :]
    b = ref[pl.ds(r + 4, n), :] + ref[pl.ds(r - 4, n), :]
    b = b + (roll(c, 1) + roll(c, -1))
    b = b + roll(jnp.where(lane < 32, ref[pl.ds(r + 1, n), :], c), -32)
    b = b + roll(jnp.where(lane >= 96, ref[pl.ds(r - 1, n), :], c), 32)
    return c, FACTOR3 * (6.0 * c - b) + s_ref[pl.ds(r, n), :] * c


def chunks3(rows, body):
    n = 48

    def step(i, carry):
        body(pl.multiple_of(GUARD + i * n, 8), n)
        return carry

    lax.fori_loop(0, rows // n, step, 0)


def match4(k, shape, coarse_dim, ny):
    c = iota2(shape, coarse_dim)
    l = iota2(shape, 1 - coarse_dim)
    return ((c >> 4) == 2 * k + (l >> 6)) & ((c & 15) == ((l & 31) >> 1)) & ((l & 31) < ny)


def restrict4(src, n, ny):
    total = None
    for k in range(3):
        t = src[pl.ds(GUARD + k, n, stride=8), :] + src[pl.ds(GUARD + k + 4, n, stride=8), :]
        part = mm(t, jnp.where(match4(k, (128, 128), 1, ny), 0.125, 0.0).astype(BF16))
        total = part if total is None else total + part
    return total


def dot_all(a, b):
    return jnp.sum(jnp.sum(a * b, axis=0, keepdims=True), axis=1, keepdims=True)


def bottom(source, s4, p4, n, ny):
    estimate = jnp.zeros_like(source)
    left = source
    direction = source
    now = dot_all(left, left)
    shifted = s4[...]
    for it in range(BOTTOM_ITERS):
        p4[pl.ds(GUARD, n), :] = direction
        b = p4[pl.ds(GUARD + 1, n), :] + p4[pl.ds(GUARD - 1, n), :]
        b = b + (roll(direction, 1) + roll(direction, -1))
        b = b + (roll(direction, 16) + roll(direction, -16))
        inside = (lanes(n) < 96) & ((lanes(n) & 15) < ny)
        image = FACTOR4 * (6.0 * direction - jnp.where(inside, b, 0.0)) + shifted * direction
        step = now / dot_all(direction, image)
        estimate = estimate + step * direction
        if it < BOTTOM_ITERS - 1:
            left = left - step * image
            after = dot_all(left, left)
            direction = left + (after / now) * direction
            now = after
    return estimate


PLAN_A = Plan([Item(L0, 3, True), Item(L0, 2, True), Item(L0, 2, True)])
PLAN_S = Plan([Item(L1, 6, False), Item(L2, 5, False)])
PLAN_B = Plan([Item(L1, 6, False)])
PLAN_C = Plan([Item(L0, 3, True)])
PLAN_D = Plan([Item(L2, 5, False)])
PLANS = (PLAN_A, PLAN_S, PLAN_B, PLAN_C, PLAN_D)


def kernel(sizes, counts, right_ref, guess_ref, react_ref, field_ref, resid_ref, *scratch):
    scratch = list(scratch)

    def take(n):
        out = scratch[:n]
        del scratch[:n]
        return out

    guess, right, react, r0, inv0, ea0, eb0, left0 = take(8)
    f1, s1, inv1, ea1, eb1, left1 = take(6)
    f2, s2, inv2, ea2, eb2, left2 = take(6)
    f3, s3, inv3, ea3, eb3, left3 = take(6)
    s4, p4, down_m, up_m, tmp, square, turned, spread, slab = take(9)
    scr = [take(n) for n in counts]
    place = Place(sizes)
    gx, gy, gz = place.me
    n3, n4, ny3 = 24 * sizes[2], 3 * sizes[2], 6 * sizes[1]

    peers = {(a, b, 0) for a in range(sizes[0]) for b in range(sizes[1])}
    peers |= {(0, 0, c) for c in range(sizes[2])}
    peers |= {(0, b % sizes[1], c % sizes[2]) for b in (1, -1) for c in (1, -1)}
    peers = sorted(peers - {(0, 0, 0)})
    barrier = pltpu.get_barrier_semaphore()

    def clear(ref):
        n = ref.shape[0]

        def step(i, carry):
            ref[pl.ds(pl.multiple_of(i * 8, 8), 8), :] = jnp.zeros((8, 128), F32)
            return carry

        lax.fori_loop(0, n // 8, step, 0)

    clear(f3)
    clear(s3)
    for p in peers:
        pl.semaphore_signal(barrier, inc=1, device_id=place.beside(*p), device_id_type=MESH)
    for ref in (guess, right, react, r0, inv0, ea0, eb0, left0, f1, s1, inv1, ea1, eb1, left1):
        clear(ref)
    for ref in (f2, s2, inv2, ea2, eb2, left2, inv3, ea3, eb3, left3, p4, square, tmp):
        clear(ref)
    spread[...] = jnp.zeros_like(spread)

    def load(i, carry):
        r = L0.row(i, 0)
        for src, dst in ((guess_ref, guess), (right_ref, right), (react_ref, react)):
            dst[pl.ds(r, 48), 0:48] = src[i]
            dst[pl.ds(r, 48), 64:112] = src[i + 24]
        return carry

    lax.fori_loop(0, 24, load, 0)

    a = iota2((128, 128), 0)
    b = iota2((128, 128), 1)
    signed = lambda v: ((v + 8) & 63) - 8
    base = lambda v: ((v + 8) & 127) & 64
    zb = signed(b)
    hit = ((a == ((base(b) + 2 * zb) & 127)) | (a == ((base(b) + 2 * zb + 1) & 127))) & (zb >= -8) & (zb < 24)
    down_m[...] = jnp.where(hit, 0.125, 0.0).astype(BF16)
    hit = a == ((base(b) + (zb >> 1)) & 127)
    up_m[...] = jnp.where(hit, 1.0, 0.0).astype(BF16)

    ex_a = Exchange(PLAN_A, (guess, right, react), scr[0], place)
    ex_s = Exchange(PLAN_S, (s1, s2), scr[1], place)
    ex_b = Exchange(PLAN_B, (f1,), scr[2], place)
    ex_c = Exchange(PLAN_C, (eb0,), scr[3], place)
    ex_d = Exchange(PLAN_D, (f2,), scr[4], place)
    ga_s = Gather(place, scr[5])
    ga_f = Gather(place, scr[6])
    ga_r = Gather(place, scr[7])
    reduced = scr[8][0]

    def slot(ref):
        return lambda c: ref.at[pl.ds(pl.multiple_of(GUARD + 24 * gz, 8), 24), :]

    pl.semaphore_wait(barrier, len(peers))
    ex_a.x_send()

    restrict(react, L0, s1, L1, 0, 12, 0, 24, down_m, tmp)
    restrict(s1, L1, s2, L2, 0, 6, 0, 12, down_m, tmp)
    ex_s.x_send()
    ga_s.mine[...] = jnp.zeros((24, 128), F32)
    ga_f.mine[...] = jnp.zeros((24, 128), F32)
    to_level3(s2, ga_s.mine, square, turned, place)

    ex_a.x_fill()
    ex_a.pack_send()
    ga_s.send()
    ex_s.x_fill()
    ex_s.pack_send()
    s3[pl.ds(pl.multiple_of(GUARD + 24 * gz, 8), 24), :] = ga_s.relay(slot(s3))
    ex_a.unpack()

    def start(r, i):
        at = pl.ds(r, L0.R)
        c, image = image_of(guess, react, L0, r)
        res = right[at, :] - image
        inv = inverse(react[at, :], 1.0)
        r0[at, :] = res
        inv0[at, :] = inv
        ea0[at, :] = inv * res

    planes(L0, -2, 26, start)
    relax(L0, ea0, eb0, r0, react, inv0, -1, 25)
    leftover(L0, eb0, left0, r0, react, 0, 24)
    restrict(left0, L0, f1, L1, 0, 12, 0, 24, down_m, tmp)
    ex_b.x_send()
    ex_c.x_send()
    ex_b.x_fill()
    ex_b.pack_send()

    ex_s.unpack()

    def inverse_of(g, s, inv):
        def body(r, i):
            at = pl.ds(r, g.R)
            inv[at, :] = inverse(s[at, :], g.factor)

        planes(g, -g.halo, g.nx + g.halo, body)

    inverse_of(L1, s1, inv1)
    inverse_of(L2, s2, inv2)
    ex_c.x_fill()
    ex_c.pack_send()

    ex_b.unpack()
    first(L1, ea1, f1, inv1, -6, 18)
    relax(L1, ea1, eb1, f1, s1, inv1, -5, 17)
    leftover(L1, eb1, left1, f1, s1, -4, 16)
    restrict(left1, L1, f2, L2, -2, 8, -2, 16, down_m, tmp)
    first(L2, ea2, f2, inv2, -2, 8)
    relax(L2, ea2, eb2, f2, s2, inv2, -1, 7)
    leftover(L2, eb2, left2, f2, s2, 0, 6)
    to_level3(left2, ga_f.mine, square, turned, place)
    ga_f.send()
    ex_d.x_send()

    ga_s.finish(slot(s3))

    def inverse3(r, n):
        inv3[pl.ds(r, n), :] = inverse(s3[pl.ds(r, n), :], FACTOR3)

    chunks3(n3, inverse3)
    s4[...] = restrict4(s3, n4, ny3)
    ex_d.x_fill()
    ex_d.pack_send()

    f3[pl.ds(pl.multiple_of(GUARD + 24 * gz, 8), 24), :] = ga_f.relay(slot(f3))
    ex_d.unpack()
    first(L2, ea2, f2, inv2, -5, 11)
    relax(L2, ea2, eb2, f2, s2, inv2, -4, 10)
    ex_c.unpack()
    ga_f.finish(slot(f3))

    def relax3(src, dst):
        def body(r, n):
            c, image = image3(src, s3, r, n)
            at = pl.ds(r, n)
            dst[at, :] = c + inv3[at, :] * (f3[at, :] - image)

        chunks3(n3, body)

    def first3(r, n):
        ea3[pl.ds(r, n), :] = inv3[pl.ds(r, n), :] * f3[pl.ds(r, n), :]

    def left_3(r, n):
        c, image = image3(eb3, s3, r, n)
        left3[pl.ds(r, n), :] = f3[pl.ds(r, n), :] - image

    chunks3(n3, first3)
    relax3(ea3, eb3)
    chunks3(n3, left_3)
    e4 = bottom(restrict4(left3, n4, ny3), s4, p4, n4, ny3 // 2)
    for k in range(3):
        u = mm(e4, jnp.where(match4(k, (128, 128), 0, ny3), 1.0, 0.0).astype(BF16))
        for q in (k, k + 4):
            at = pl.ds(GUARD + q, n4, stride=8)
            eb3[at, :] = eb3[at, :] + u
    relax3(eb3, ea3)
    relax3(ea3, eb3)

    slab[...] = eb3[pl.ds(pl.multiple_of(24 * gz, 8), 40), :]
    for k in range(3):
        v = slab[pl.ds(k, 10, stride=4), :]
        for h in range(2):
            for q in range(2):
                spread[k, pl.ds(64 * h + q, 10, stride=2), :] = v
    wide = [jnp.concatenate(p, axis=1) for p in zip(*[split3(spread[k]) for k in range(3)])]
    coarse = []
    for h in range(2):
        r = iota2((112, 384), 0)
        l = iota2((112, 384), 1)
        hit = (6 * gx + 3 * h + (r >> 4) - 2 == (l >> 5)) & (6 * gy + (r & 15) - 2 == (l & 31)) & ((r & 15) < 10)
        pick = jnp.where(hit, 1.0, 0.0).astype(BF16)
        parts = [
            lax.dot_general(pick, p, (((1,), (1,)), ((), ())), preferred_element_type=F32) for p in wide
        ]
        coarse.append(parts[0] + (parts[1] + parts[2]))
    fine = roll(jnp.where(lanes(112) < 64, coarse[0], coarse[1]), -4)
    for i in range(7):
        u = fine[16 * i : 16 * i + 10]
        tmp[pl.ds(24 * i, 10, stride=2), :] = u
        tmp[pl.ds(24 * i + 1, 10, stride=2), :] = u
    for i in range(7):
        v = tmp[pl.ds(24 * i, 20), :]
        for q in range(2):
            at = pl.ds(L2.row(2 * (i - 2) + q, -4), 20)
            eb2[at, :] = eb2[at, :] + v
    relax(L2, eb2, ea2, f2, s2, inv2, -3, 9)
    relax(L2, ea2, eb2, f2, s2, inv2, -2, 8)
    prolong(eb2, L2, eb1, L1, -2, 8, -2, 16, up_m, tmp)
    relax(L1, eb1, ea1, f1, s1, inv1, -3, 15)
    relax(L1, ea1, eb1, f1, s1, inv1, -2, 14)
    prolong(eb1, L1, eb0, L0, -2, 14, -2, 28, up_m, tmp)
    relax(L0, eb0, ea0, r0, react, inv0, -2, 26)
    relax(L0, ea0, eb0, r0, react, inv0, -1, 25)

    row = iota2((L0.R, 128), 0)
    inside = ((lanes(L0.R) & 63) < 48) & (row >= L0.y0) & (row < L0.y0 + 48)

    def last(i, sums):
        r = pl.multiple_of(GUARD + (L0.halo + i) * L0.R, 8)
        at = pl.ds(r, L0.R)
        c, image = image_of(eb0, react, L0, r)
        left0[at, :] = image
        upper = jnp.where(inside, c * r0[at, :], 0.0)
        lower = jnp.where(inside, c * image, 0.0)
        return sums[0] + upper, sums[1] + lower

    zero = jnp.zeros((L0.R, 128), F32)
    upper, lower = lax.fori_loop(0, 24, last, (zero, zero))
    upper = jnp.sum(upper, axis=0, keepdims=True)
    lower = jnp.sum(lower, axis=0, keepdims=True)
    half = lanes(1) < 64
    ga_r.mine[...] = jnp.where(half, upper + roll(upper, 64), lower + roll(lower, 64))
    ga_r.send()
    own = ga_r.relay(lambda c: reduced.at[c])
    ga_r.finish(lambda c: reduced.at[c])
    total = own
    for c in range(1, sizes[2]):
        total = total + reduced[c]
    upper = jnp.sum(jnp.where(half, total, 0.0), axis=1, keepdims=True)
    lower = jnp.sum(jnp.where(half, 0.0, total), axis=1, keepdims=True)
    step = upper / lower

    def store(i, carry):
        at = pl.ds(L0.row(i, 0), 48)
        e = eb0[at, :]
        v = guess[at, :] + step * e
        field_ref[i] = v[:, 0:48]
        field_ref[i + 24] = roll(v, 64)[:, 0:48]
        v = r0[at, :] - step * left0[at, :]
        resid_ref[i] = v[:, 0:48]
        resid_ref[i + 24] = roll(v, 64)[:, 0:48]
        return carry

    lax.fori_loop(0, 24, store, 0)


def solution(mesh):
    sizes = tuple(mesh.shape[a] for a in ("gx", "gy", "gz"))
    n3, n4 = 24 * sizes[2] + 2 * GUARD, 3 * sizes[2]
    scratch = [pltpu.VMEM((L0.total, 128), F32)] * 8
    scratch += [pltpu.VMEM((L1.total, 128), F32)] * 6
    scratch += [pltpu.VMEM((L2.total, 128), F32)] * 6
    scratch += [pltpu.VMEM((n3, 128), F32)] * 6
    scratch += [pltpu.VMEM((n4, 128), F32), pltpu.VMEM((n4 + 2 * GUARD, 128), F32)]
    scratch += [pltpu.VMEM((128, 128), BF16)] * 2 + [pltpu.VMEM((16 * 56, 128), F32)]
    scratch += [pltpu.VMEM((128, 128), F32)] * 2
    scratch += [pltpu.VMEM((3, 128, 128), F32), pltpu.VMEM((40, 128), F32)]
    groups = [p.scratch() for p in PLANS] + [gather_scratch(sizes, 24)] * 2 + [gather_scratch(sizes, 1)]
    groups += [[pltpu.VMEM((sizes[2], 1, 128), F32)]]
    for g in groups:
        scratch += g
    counts = tuple(len(g) for g in groups)
    vmem = pl.BlockSpec(memory_space=pltpu.VMEM)

    def body(right_side, start_guess, reaction):
        shape = jax.ShapeDtypeStruct(right_side.shape, F32)
        return tuple(
            pl.pallas_call(
                functools.partial(kernel, sizes, counts),
                out_shape=[shape, shape],
                in_specs=[vmem] * 3,
                out_specs=[vmem] * 2,
                scratch_shapes=scratch,
                compiler_params=pltpu.CompilerParams(collective_id=0, has_side_effects=True),
            )(right_side, start_guess, reaction)
        )

    placed = P("gx", "gy", "gz")
    return jax.shard_map(
        body, mesh=mesh, in_specs=(placed,) * 3, out_specs=(placed,) * 2, check_vma=False
    )
```

time: 898 us -> 107 us (0.12); the launches traced: 883 us -> 107 us
  starting transfers between devices: 332 us -> 0 us
  local copies, waits for them, and re-layouts: 172 us -> 3.47 us
  other arithmetic: 144 us -> 0 us
  blocking collectives: 140 us -> 0 us
  Pallas kernels: 0 us -> 103 us
  waiting for transfers between devices: 74.2 us -> 0 us
  between operations: 19.6 us -> 0.65 us
    ppermute x108 -> x0, starting transfers between devices: 332 us -> none  [the longest x54 211 us: extended(): lax.ppermute(lax.slice_in_dim(block, block.shape[dim] - width, None, axis...]
    pallas_call x0 -> x1, Pallas kernels: none -> 103 us  [body(): pl.pallas_call(functools.partial(kernel, sizes, counts), out_shape=[shape...]
    psum x1 -> x0, blocking collectives: 76.6 us -> none  [body(): upper = lax.psum(jnp.sum(start_residual * precond), ('gx', 'gy', 'gz'))]
    ppermute x108 -> x0, waiting for transfers between devices: 74.2 us -> none  [the longest x54 51 us: extended(): lax.ppermute(lax.slice_in_dim(block, block.shape[dim] - width, None, axis...]
    reshape x15 -> x0, local copies, waits for them, and re-layouts: 65.4 us -> none  [the longest x5 36.5 us: coarsen(): blocks = values.reshape(size_x // 2, 2, size_y // 2, 2, size_z // 2, 2)]
    reduce_sum x21 -> x0, other arithmetic: 64.9 us -> none  [the longest x8 34.2 us: coarsen(): return jnp.mean(blocks, axis=(1, 3, 5))]
    all_gather x4 -> x0, blocking collectives: 54 us -> none  [the longest x1 32.1 us: bottom(): lax.all_gather(gathered[0], 'gz', axis=2, tiled=True)]
    slice x50 -> x0, local copies, waits for them, and re-layouts: 42.3 us -> none  [the longest x25 29.7 us: extended(): lax.slice_in_dim(block, 0, width, axis=dim)]
  transfers between devices with their start and end apart: 108 -> 0, of which waited for: 47 -> 0; matrix products, arithmetic and copies ran while one was open for 7% -> 0% of each run, Pallas kernels for 0% -> 0%
where the time goes in v1:
time: 107 us
  Pallas kernels  103 us (96%)
  local copies, waits for them, and re-layouts  3.47 us (3%)
    pallas_call x1, Pallas kernels, body(): pl.pallas_call(functools.partial(kernel, sizes, counts), out_shape=[shape...  103 us
    unnamed x4, local copies, waits for them, and re-layouts  3.47 us

profile of v1, /device:TPU:1, one launch (start us, length us, event | category | flops | bytes accessed | tf_op | source)
XLA Modules:
  0.0 106.7 jit_solution(3926464930829427612)
XLA Ops:
  0.6 102.6 %shard_map.50 = (f32[48,48,48]{2,1,0:T(8,128)}, f32[48,48,48]{2,1,0:T(8,128)}) custom-call(f32[48,48,48]{2,1,0:T(8,128)} %right_ref.1, f32[48,48,48]{2,1,0:T(8,128)} %guess_ref.1, f32[48,48,48]{2,1,0:T(8,128)} %react_ref.1), custom_call_target="tpu_custom_call" | custom-call | tf_op jit(solution)/shard_map/pallas_call | solution.py:765
  103.2 0.0 copy-start
  103.2 2.5 %copy.7 = f32[48,48,48]{2,1,0:T(8,128)} copy(f32[48,48,48]{2,1,0:T(8,128)} %get-tuple-element.4) | data formatting | bytes 884736
  105.7 0.0 copy-done
  105.7 1.0 copy.8
Async XLA Ops:
  103.2 2.5 %copy-start = (f32[48,48,48]{2,1,0:T(8,128)S(1)}, f32[48,48,48]{2,1,0:T(8,128)}, u32[]{:S(2)}) copy-start(f32[48,48,48]{2,1,0:T(8,128)} %get-tuple-element.5) | copy-start | bytes 1327108

commit v2 on v1

--- a/solution.py
+++ b/solution.py
@@ -16,18 +16,19 @@
 
 
 class Geo:
-    def __init__(self, nx, ny, nz, halo, rows, y0, depth):
+    def __init__(self, nx, ny, nz, halo, rows, y0, depth, unroll):
         self.nx, self.ny, self.nz, self.halo, self.R, self.y0 = nx, ny, nz, halo, rows, y0
         self.factor = 0.25**depth
+        self.unroll = unroll
         self.total = 2 * GUARD + (nx + 2 * halo) * rows
 
     def row(self, x, y):
         return GUARD + (self.halo + x) * self.R + self.y0 + y
 
 
-L0 = Geo(24, 48, 48, 4, 56, 4, 0)
-L1 = Geo(12, 24, 24, 6, 40, 8, 1)
-L2 = Geo(6, 12, 12, 5, 24, 6, 2)
+L0 = Geo(24, 48, 48, 4, 56, 4, 0, 4)
+L1 = Geo(12, 24, 24, 6, 40, 8, 1, 6)
+L2 = Geo(6, 12, 12, 5, 24, 6, 2, 8)
 FACTOR3 = 0.25**3
 FACTOR4 = 0.25**4
 
@@ -73,11 +74,31 @@
 
 
 def planes(g, a, b, body):
-    def step(i, carry):
-        body(pl.multiple_of(GUARD + i * g.R, 8), i)
-        return carry
-
-    lax.fori_loop(g.halo + a, g.halo + b, step, 0)
+    unroll = g.unroll
+
+    def group(start, count):
+        todo = []
+        for k in range(count):
+            r = start + k * g.R
+            r = r if isinstance(r, int) else pl.multiple_of(r, 8)
+            todo.append((r, body(r)))
+        for r, pairs in todo:
+            for ref, value in pairs:
+                ref[pl.ds(r, g.R), :] = value
+
+    trips = (b - a) // unroll
+    origin = GUARD + (g.halo + a) * g.R
+    if trips == 1:
+        group(origin, unroll)
+    elif trips:
+
+        def step(i, carry):
+            group(pl.multiple_of(origin + i * (unroll * g.R), 8), unroll)
+            return carry
+
+        lax.fori_loop(0, trips, step, 0)
+    if (b - a) % unroll:
+        group(origin + trips * unroll * g.R, (b - a) % unroll)
 
 
 def inverse(s, factor):
@@ -85,27 +106,26 @@
 
 
 def relax(g, src, dst, f, s, inv, a, b):
-    def body(r, i):
+    def body(r):
         c, image = image_of(src, s, g, r)
         at = pl.ds(r, g.R)
-        dst[at, :] = c + inv[at, :] * (f[at, :] - image)
+        return [(dst, c + inv[at, :] * (f[at, :] - image))]
 
     planes(g, a, b, body)
 
 
 def first(g, dst, f, inv, a, b):
-    def body(r, i):
+    def body(r):
         at = pl.ds(r, g.R)
-        dst[at, :] = inv[at, :] * f[at, :]
+        return [(dst, inv[at, :] * f[at, :])]
 
     planes(g, a, b, body)
 
 
 def leftover(g, src, dst, f, s, a, b):
-    def body(r, i):
+    def body(r):
         c, image = image_of(src, s, g, r)
-        at = pl.ds(r, g.R)
-        dst[at, :] = f[at, :] - image
+        return [(dst, f[pl.ds(r, g.R), :] - image)]
 
     planes(g, a, b, body)
 
@@ -138,25 +158,29 @@
 
 
 class Item:
-    def __init__(self, geo, w, diamond):
-        self.g, self.w, self.diamond = geo, w, diamond
-        self.slots = 64 // w
-        self.wz = w - 1 if diamond else w
-        self.wd = w - 2 if diamond else w
-        self.ztiles = -(-(geo.nx + 2 * self.wz) // self.slots)
-
-    def wy(self, d):
-        return self.w - d if self.diamond else self.w
+    def __init__(self, geo, w):
+        self.g, self.w = geo, w
 
 
 class Plan:
     def __init__(self, items):
         self.items = items
-        self.yrows = sum(it.g.nx + 2 * it.wy(d) for it in items for d in range(1, it.w + 1))
+        self.yrows = sum(it.g.nx * it.w for it in items)
         self.yrows = -(-self.yrows // 8) * 8
-        self.zrows = sum(it.ztiles * it.g.ny for it in items)
+        self.tiles = []
+        for k, it in enumerate(items):
+            for x in range(it.g.nx):
+                for t in self.tiles:
+                    if t[0] is it.g and t[1] + it.w <= 64:
+                        break
+                else:
+                    t = [it.g, 0, []]
+                    self.tiles.append(t)
+                t[2].append((k, x, t[1]))
+                t[1] += it.w
+        self.zrows = sum(t[0].ny for t in self.tiles)
         self.zrows = -(-self.zrows // 8) * 8
-        self.drows = max(it.g.nx + 2 * it.wd for it in items)
+        self.drows = max(it.g.nx for it in items)
         self.drows = -(-self.drows // 8) * 8
         assert sum(it.w * it.w for it in items) <= 64
 
@@ -189,17 +213,18 @@
             self.x_copies.append(
                 self.copy(refs[k].at[pl.ds(r, it.w * g.R), :], self.xr[k], k, (1 - gx, gy, gz))
             )
-        self.copies = []
+        self.y_copies, self.z_copies, self.d_copies = [], [], []
         for d in range(2):
-            self.copies.append(self.copy(self.ys.at[d], self.yr.at[d], 3 + d, place.beside(0, 1 - 2 * d, 0)))
-            self.copies.append(self.copy(self.zs.at[d], self.zr.at[d], 5 + d, place.beside(0, 0, 1 - 2 * d)))
+            self.y_copies.append(self.copy(self.ys.at[d], self.yr.at[d], 3 + d, place.beside(0, 1 - 2 * d, 0)))
+            self.z_copies.append(self.copy(self.zs.at[d], self.zr.at[d], 5 + d, place.beside(0, 0, 1 - 2 * d)))
             for e in range(2):
-                self.copies.append(
+                self.d_copies.append(
                     self.copy(
                         self.ds.at[2 * d + e], self.dr.at[2 * d + e], 7 + 2 * d + e,
                         place.beside(0, 1 - 2 * d, 1 - 2 * e),
                     )
                 )
+        self.copies = self.y_copies + self.z_copies + self.d_copies
 
     def copy(self, src, dst, k, peer):
         return pltpu.make_async_remote_copy(
@@ -217,7 +242,7 @@
         m0, m1 = self.place.x_masks
         for k, it in enumerate(self.plan.items):
             g, w, ref = it.g, it.w, self.refs[k]
-            upper = lanes(g.R) >= 64
+            upper = ((lanes(g.R) + 8) & 127) >= 64
             for j in range(w):
                 got = self.xr[k][pl.ds(j * g.R, g.R), :]
                 top = ref[pl.ds(GUARD + (g.halo + g.nx - w + j) * g.R, g.R), :]
@@ -226,86 +251,77 @@
                 ref[pl.ds(GUARD + (g.halo + g.nx + j) * g.R, g.R), :] = roll(jnp.where(upper, low, got * m0), 64)
 
     def pack_send(self):
-        yo, zo, co = 0, 0, 0
+        zo = 0
+        for g, _, slots in self.plan.tiles:
+            lane = lanes(g.ny) & 63
+            acc = [None, None]
+            for k, x, at in slots:
+                w = self.plan.items[k].w
+                v = self.refs[k][pl.ds(g.row(x, 0), g.ny), :]
+                for q, z in enumerate((g.nz - w, 0)):
+                    moved = roll(v, at - z)
+                    acc[q] = moved if acc[q] is None else jnp.where(lane >= at, moved, acc[q])
+            for q in range(2):
+                self.zs[q, pl.ds(zo, g.ny), :] = acc[q]
+            zo += g.ny
+        for c in self.z_copies:
+            c.start()
+        yo, co = 0, 0
         corner = [None] * 4
         for k, it in enumerate(self.plan.items):
             g, w, ref = it.g, it.w, self.refs[k]
-            for d in range(1, w + 1):
-                n = g.nx + 2 * it.wy(d)
-                for e, y in enumerate((g.ny - d, d - 1)):
-                    self.ys[e, pl.ds(yo, n), :] = ref[pl.ds(g.row(-it.wy(d), y), n, stride=g.R), :]
-                yo += n
+            n = g.nx
             lane = lanes(self.plan.drows) & 63
             for d in range(1, w + 1):
                 at = co + (d - 1) * w
-                pick = (lane >= at) & (lane < at + w)
                 for e, y in enumerate((g.ny - d, d - 1)):
-                    n = g.nx + 2 * it.wd
-                    v = ref[pl.ds(g.row(-it.wd, y), n, stride=g.R), :]
+                    v = ref[pl.ds(g.row(0, y), n, stride=g.R), :]
+                    self.ys[e, pl.ds(yo, n), :] = v
                     if n < self.plan.drows:
                         v = jnp.concatenate([v, jnp.zeros((self.plan.drows - n, 128), F32)], axis=0)
                     for q, z in enumerate((g.nz - w, 0)):
                         moved = roll(v, at - z)
                         old = corner[2 * e + q]
-                        corner[2 * e + q] = moved if old is None else jnp.where(pick, moved, old)
+                        corner[2 * e + q] = moved if old is None else jnp.where(lane >= at, moved, old)
+                yo += n
             co += w * w
-            lane = lanes(g.ny) & 63
-            count = g.nx + 2 * it.wz
-            for t in range(it.ztiles):
-                acc = [None, None]
-                for j in range(min(it.slots, count - t * it.slots)):
-                    x = t * it.slots + j - it.wz
-                    v = ref[pl.ds(g.row(x, 0), g.ny), :]
-                    pick = (lane >= j * w) & (lane < j * w + w)
-                    for q, z in enumerate((g.nz - w, 0)):
-                        moved = roll(v, j * w - z)
-                        acc[q] = moved if j == 0 else jnp.where(pick, moved, acc[q])
-                for q in range(2):
-                    self.zs[q, pl.ds(zo, g.ny), :] = acc[q]
-                zo += g.ny
         for q in range(4):
             self.ds[q] = corner[q]
-        for c in self.copies:
+        for c in self.d_copies + self.y_copies:
             c.start()
 
     def unpack(self):
+        my, mz = self.place.y_masks, self.place.z_masks
         for c in self.copies:
             c.wait()
-        my, mz = self.place.y_masks, self.place.z_masks
-        yo, zo, co = 0, 0, 0
+        zo = 0
+        for g, _, slots in self.plan.tiles:
+            lane = lanes(g.ny) & 63
+            got = [self.zr[q, pl.ds(zo, g.ny), :] * mz[q] for q in range(2)]
+            for k, x, at in slots:
+                w = self.plan.items[k].w
+                rows = pl.ds(g.row(x, 0), g.ny)
+                v = self.refs[k][rows, :]
+                v = jnp.where(lane >= 64 - w, roll(got[0], -w - at), v)
+                v = jnp.where((lane >= g.nz) & (lane < g.nz + w), roll(got[1], g.nz - at), v)
+                self.refs[k][rows, :] = v
+            zo += g.ny
+        yo, co = 0, 0
         for k, it in enumerate(self.plan.items):
             g, w, ref = it.g, it.w, self.refs[k]
-            for d in range(1, w + 1):
-                n = g.nx + 2 * it.wy(d)
-                for e, y in enumerate((-d, g.ny + d - 1)):
-                    ref[pl.ds(g.row(-it.wy(d), y), n, stride=g.R), :] = self.yr[e, pl.ds(yo, n), :] * my[e]
-                yo += n
-            n = g.nx + 2 * it.wd
+            n = g.nx
             lane = lanes(n) & 63
             into = (lane >= 64 - w, (lane >= g.nz) & (lane < g.nz + w))
             for d in range(1, w + 1):
                 at = co + (d - 1) * w
                 for e, y in enumerate((-d, g.ny + d - 1)):
-                    rows = pl.ds(g.row(-it.wd, y), n, stride=g.R)
-                    v = ref[rows, :]
+                    v = self.yr[e, pl.ds(yo, n), :]
                     for q, z in enumerate((-w, g.nz)):
-                        got = self.dr[2 * e + q, pl.ds(0, n), :] * (my[e] * mz[q])
+                        got = self.dr[2 * e + q, pl.ds(0, n), :] * mz[q]
                         v = jnp.where(into[q], roll(got, z - at), v)
-                    ref[rows, :] = v
+                    ref[pl.ds(g.row(0, y), n, stride=g.R), :] = v * my[e]
+                yo += n
             co += w * w
-            lane = lanes(g.ny) & 63
-            into = (lane >= 64 - w, (lane >= g.nz) & (lane < g.nz + w))
-            count = g.nx + 2 * it.wz
-            for t in range(it.ztiles):
-                got = [self.zr[q, pl.ds(zo, g.ny), :] * mz[q] for q in range(2)]
-                for j in range(min(it.slots, count - t * it.slots)):
-                    x = t * it.slots + j - it.wz
-                    rows = pl.ds(g.row(x, 0), g.ny)
-                    v = ref[rows, :]
-                    for q, z in enumerate((-w, g.nz)):
-                        v = jnp.where(into[q], roll(got[q], z - j * w), v)
-                    ref[rows, :] = v
-                zo += g.ny
 
 
 class Place:
@@ -422,11 +438,12 @@
     return c, FACTOR3 * (6.0 * c - b) + s_ref[pl.ds(r, n), :] * c
 
 
-def chunks3(rows, body):
-    n = 48
+def chunks3(rows, ref, body):
+    n = min(rows, 192)
 
     def step(i, carry):
-        body(pl.multiple_of(GUARD + i * n, 8), n)
+        r = pl.multiple_of(GUARD + i * n, 8)
+        ref[pl.ds(r, n), :] = body(r, n)
         return carry
 
     lax.fori_loop(0, rows // n, step, 0)
@@ -474,15 +491,15 @@
     return estimate
 
 
-PLAN_A = Plan([Item(L0, 3, True), Item(L0, 2, True), Item(L0, 2, True)])
-PLAN_S = Plan([Item(L1, 6, False), Item(L2, 5, False)])
-PLAN_B = Plan([Item(L1, 6, False)])
-PLAN_C = Plan([Item(L0, 3, True)])
-PLAN_D = Plan([Item(L2, 5, False)])
+PLAN_A = Plan([Item(L0, 3), Item(L0, 2), Item(L0, 2)])
+PLAN_S = Plan([Item(L1, 6), Item(L2, 5)])
+PLAN_B = Plan([Item(L1, 6)])
+PLAN_C = Plan([Item(L0, 3)])
+PLAN_D = Plan([Item(L2, 5)])
 PLANS = (PLAN_A, PLAN_S, PLAN_B, PLAN_C, PLAN_D)
 
 
-def kernel(sizes, counts, right_ref, guess_ref, react_ref, field_ref, resid_ref, *scratch):
+def kernel(sizes, counts, right_in, guess_in, react_in, guess, r0, eb0, left0, step_out, *scratch):
     scratch = list(scratch)
 
     def take(n):
@@ -490,7 +507,9 @@
         del scratch[:n]
         return out
 
-    guess, right, react, r0, inv0, ea0, eb0, left0 = take(8)
+    raw = take(3)
+    (in_sems,) = take(1)
+    right, react, inv0, ea0 = take(4)
     f1, s1, inv1, ea1, eb1, left1 = take(6)
     f2, s2, inv2, ea2, eb2, left2 = take(6)
     f3, s3, inv3, ea3, eb3, left3 = take(6)
@@ -500,39 +519,49 @@
     gx, gy, gz = place.me
     n3, n4, ny3 = 24 * sizes[2], 3 * sizes[2], 6 * sizes[1]
 
+    loads = [
+        pltpu.make_async_copy(src, dst, in_sems.at[k])
+        for k, (src, dst) in enumerate(zip((guess_in, right_in, react_in), raw))
+    ]
+    for c in loads:
+        c.start()
+
+    def clear(ref):
+        n = ref.shape[0]
+        size = next(k for k in (128, 122 * 8, 80, 8) if n % k == 0) if n > 128 else n
+        size = {1808: 904, 976: 488}.get(n, size)
+
+        def step(i, carry):
+            ref[pl.ds(pl.multiple_of(i * size, 8), size), :] = jnp.zeros((size, 128), F32)
+            return carry
+
+        lax.fori_loop(0, n // size, step, 0)
+
+    clear(f3)
+    clear(s3)
     peers = {(a, b, 0) for a in range(sizes[0]) for b in range(sizes[1])}
     peers |= {(0, 0, c) for c in range(sizes[2])}
     peers |= {(0, b % sizes[1], c % sizes[2]) for b in (1, -1) for c in (1, -1)}
     peers = sorted(peers - {(0, 0, 0)})
     barrier = pltpu.get_barrier_semaphore()
-
-    def clear(ref):
-        n = ref.shape[0]
-
-        def step(i, carry):
-            ref[pl.ds(pl.multiple_of(i * 8, 8), 8), :] = jnp.zeros((8, 128), F32)
-            return carry
-
-        lax.fori_loop(0, n // 8, step, 0)
-
-    clear(f3)
-    clear(s3)
     for p in peers:
         pl.semaphore_signal(barrier, inc=1, device_id=place.beside(*p), device_id_type=MESH)
-    for ref in (guess, right, react, r0, inv0, ea0, eb0, left0, f1, s1, inv1, ea1, eb1, left1):
-        clear(ref)
-    for ref in (f2, s2, inv2, ea2, eb2, left2, inv3, ea3, eb3, left3, p4, square, tmp):
+    for ref in (guess, right, react, f1, s1, ea1, eb1, f2, s2, ea2, eb2, ea3, eb3, p4, square):
         clear(ref)
     spread[...] = jnp.zeros_like(spread)
 
+    for c in loads:
+        c.wait()
+
     def load(i, carry):
-        r = L0.row(i, 0)
-        for src, dst in ((guess_ref, guess), (right_ref, right), (react_ref, react)):
-            dst[pl.ds(r, 48), 0:48] = src[i]
-            dst[pl.ds(r, 48), 64:112] = src[i + 24]
+        for src, dst in zip(raw, (guess, right, react)):
+            for k in range(2):
+                r = GUARD + (L0.halo + 2 * i + k) * L0.R + L0.y0
+                dst[pl.ds(r, 48), 0:48] = src[2 * i + k]
+                dst[pl.ds(r, 48), 64:112] = src[2 * i + k + 24]
         return carry
 
-    lax.fori_loop(0, 24, load, 0)
+    lax.fori_loop(0, 12, load, 0)
 
     a = iota2((128, 128), 0)
     b = iota2((128, 128), 1)
@@ -558,58 +587,51 @@
         return lambda c: ref.at[pl.ds(pl.multiple_of(GUARD + 24 * gz, 8), 24), :]
 
     pl.semaphore_wait(barrier, len(peers))
-    ex_a.x_send()
+    ex_a.pack_send()
 
     restrict(react, L0, s1, L1, 0, 12, 0, 24, down_m, tmp)
     restrict(s1, L1, s2, L2, 0, 6, 0, 12, down_m, tmp)
-    ex_s.x_send()
+    ex_s.pack_send()
     ga_s.mine[...] = jnp.zeros((24, 128), F32)
     ga_f.mine[...] = jnp.zeros((24, 128), F32)
     to_level3(s2, ga_s.mine, square, turned, place)
-
-    ex_a.x_fill()
-    ex_a.pack_send()
     ga_s.send()
-    ex_s.x_fill()
-    ex_s.pack_send()
-    s3[pl.ds(pl.multiple_of(GUARD + 24 * gz, 8), 24), :] = ga_s.relay(slot(s3))
-    ex_a.unpack()
-
-    def start(r, i):
+
+    def start(r):
         at = pl.ds(r, L0.R)
         c, image = image_of(guess, react, L0, r)
         res = right[at, :] - image
         inv = inverse(react[at, :], 1.0)
-        r0[at, :] = res
-        inv0[at, :] = inv
-        ea0[at, :] = inv * res
-
-    planes(L0, -2, 26, start)
+        return [(r0, res), (inv0, inv), (ea0, inv * res)]
+
+    ex_a.unpack()
+    ex_a.x_send()
+    planes(L0, 1, 23, start)
+    ex_a.x_fill()
+    planes(L0, -2, 1, start)
+    planes(L0, 23, 26, start)
     relax(L0, ea0, eb0, r0, react, inv0, -1, 25)
     leftover(L0, eb0, left0, r0, react, 0, 24)
     restrict(left0, L0, f1, L1, 0, 12, 0, 24, down_m, tmp)
+    ex_b.pack_send()
+
+    ex_s.unpack()
+    ex_s.x_send()
+    ex_c.pack_send()
+    ex_s.x_fill()
+    for g, sh, inv in ((L1, s1, inv1), (L2, s2, inv2)):
+        planes(g, -g.halo, g.nx + g.halo, lambda r: [(inv, inverse(sh[pl.ds(r, g.R), :], g.factor))])
+    s3[pl.ds(pl.multiple_of(GUARD + 24 * gz, 8), 24), :] = ga_s.relay(slot(s3))
+
+    ex_b.unpack()
     ex_b.x_send()
-    ex_c.x_send()
+    first(L1, ea1, f1, inv1, 0, 12)
+    relax(L1, ea1, eb1, f1, s1, inv1, 1, 11)
     ex_b.x_fill()
-    ex_b.pack_send()
-
-    ex_s.unpack()
-
-    def inverse_of(g, s, inv):
-        def body(r, i):
-            at = pl.ds(r, g.R)
-            inv[at, :] = inverse(s[at, :], g.factor)
-
-        planes(g, -g.halo, g.nx + g.halo, body)
-
-    inverse_of(L1, s1, inv1)
-    inverse_of(L2, s2, inv2)
-    ex_c.x_fill()
-    ex_c.pack_send()
-
-    ex_b.unpack()
-    first(L1, ea1, f1, inv1, -6, 18)
-    relax(L1, ea1, eb1, f1, s1, inv1, -5, 17)
+    first(L1, ea1, f1, inv1, -6, 0)
+    first(L1, ea1, f1, inv1, 12, 18)
+    relax(L1, ea1, eb1, f1, s1, inv1, -5, 1)
+    relax(L1, ea1, eb1, f1, s1, inv1, 11, 17)
     leftover(L1, eb1, left1, f1, s1, -4, 16)
     restrict(left1, L1, f2, L2, -2, 8, -2, 16, down_m, tmp)
     first(L2, ea2, f2, inv2, -2, 8)
@@ -617,43 +639,34 @@
     leftover(L2, eb2, left2, f2, s2, 0, 6)
     to_level3(left2, ga_f.mine, square, turned, place)
     ga_f.send()
-    ex_d.x_send()
-
+    ex_d.pack_send()
+
+    ex_c.unpack()
+    ex_c.x_send()
     ga_s.finish(slot(s3))
-
-    def inverse3(r, n):
-        inv3[pl.ds(r, n), :] = inverse(s3[pl.ds(r, n), :], FACTOR3)
-
-    chunks3(n3, inverse3)
+    chunks3(n3, inv3, lambda r, n: inverse(s3[pl.ds(r, n), :], FACTOR3))
     s4[...] = restrict4(s3, n4, ny3)
-    ex_d.x_fill()
-    ex_d.pack_send()
 
     f3[pl.ds(pl.multiple_of(GUARD + 24 * gz, 8), 24), :] = ga_f.relay(slot(f3))
     ex_d.unpack()
+    ex_d.x_send()
+    ex_c.x_fill()
+    ex_d.x_fill()
     first(L2, ea2, f2, inv2, -5, 11)
     relax(L2, ea2, eb2, f2, s2, inv2, -4, 10)
-    ex_c.unpack()
     ga_f.finish(slot(f3))
 
     def relax3(src, dst):
         def body(r, n):
             c, image = image3(src, s3, r, n)
             at = pl.ds(r, n)
-            dst[at, :] = c + inv3[at, :] * (f3[at, :] - image)
-
-        chunks3(n3, body)
-
-    def first3(r, n):
-        ea3[pl.ds(r, n), :] = inv3[pl.ds(r, n), :] * f3[pl.ds(r, n), :]
-
-    def left_3(r, n):
-        c, image = image3(eb3, s3, r, n)
-        left3[pl.ds(r, n), :] = f3[pl.ds(r, n), :] - image
-
-    chunks3(n3, first3)
+            return c + inv3[at, :] * (f3[at, :] - image)
+
+        chunks3(n3, dst, body)
+
+    chunks3(n3, ea3, lambda r, n: inv3[pl.ds(r, n), :] * f3[pl.ds(r, n), :])
     relax3(ea3, eb3)
-    chunks3(n3, left_3)
+    chunks3(n3, left3, lambda r, n: f3[pl.ds(r, n), :] - image3(eb3, s3, r, n)[1])
     e4 = bottom(restrict4(left3, n4, ny3), s4, p4, n4, ny3 // 2)
     for k in range(3):
         u = mm(e4, jnp.where(match4(k, (128, 128), 0, ny3), 1.0, 0.0).astype(BF16))
@@ -703,16 +716,20 @@
     inside = ((lanes(L0.R) & 63) < 48) & (row >= L0.y0) & (row < L0.y0 + 48)
 
     def last(i, sums):
-        r = pl.multiple_of(GUARD + (L0.halo + i) * L0.R, 8)
-        at = pl.ds(r, L0.R)
-        c, image = image_of(eb0, react, L0, r)
-        left0[at, :] = image
-        upper = jnp.where(inside, c * r0[at, :], 0.0)
-        lower = jnp.where(inside, c * image, 0.0)
-        return sums[0] + upper, sums[1] + lower
+        upper, lower = sums
+        images = []
+        for k in range(4):
+            r = pl.multiple_of(GUARD + (L0.halo + 4 * i + k) * L0.R, 8)
+            c, image = image_of(eb0, react, L0, r)
+            images.append((r, image))
+            upper = upper + jnp.where(inside, c * r0[pl.ds(r, L0.R), :], 0.0)
+            lower = lower + jnp.where(inside, c * image, 0.0)
+        for r, image in images:
+            left0[pl.ds(r, L0.R), :] = image
+        return upper, lower
 
     zero = jnp.zeros((L0.R, 128), F32)
-    upper, lower = lax.fori_loop(0, 24, last, (zero, zero))
+    upper, lower = lax.fori_loop(0, 6, last, (zero, zero))
     upper = jnp.sum(upper, axis=0, keepdims=True)
     lower = jnp.sum(lower, axis=0, keepdims=True)
     half = lanes(1) < 64
@@ -725,26 +742,43 @@
         total = total + reduced[c]
     upper = jnp.sum(jnp.where(half, total, 0.0), axis=1, keepdims=True)
     lower = jnp.sum(jnp.where(half, 0.0, total), axis=1, keepdims=True)
-    step = upper / lower
-
-    def store(i, carry):
-        at = pl.ds(L0.row(i, 0), 48)
-        e = eb0[at, :]
-        v = guess[at, :] + step * e
-        field_ref[i] = v[:, 0:48]
-        field_ref[i + 24] = roll(v, 64)[:, 0:48]
-        v = r0[at, :] - step * left0[at, :]
-        resid_ref[i] = v[:, 0:48]
-        resid_ref[i + 24] = roll(v, 64)[:, 0:48]
-        return carry
-
-    lax.fori_loop(0, 24, store, 0)
+    step_out[...] = jnp.broadcast_to(upper / lower, (8, 128))
+
+
+def finish(guess, r0, eb0, left0, step_ref, field_out, resid_out, field, resid, sems):
+    step = step_ref[0:1, :]
+    copies = []
+    parts, size = 4, 6
+    for p in range(parts):
+        def body(i, carry):
+            for k in range(2):
+                x = p * size + 2 * i + k
+                at = pl.ds(GUARD + (L0.halo + x) * L0.R + L0.y0, 48)
+                e = eb0[at, :]
+                v = guess[at, :] + step * e
+                field[x] = v[:, 0:48]
+                field[x + 24] = roll(v, 64)[:, 0:48]
+                v = r0[at, :] - step * left0[at, :]
+                resid[x] = v[:, 0:48]
+                resid[x + 24] = roll(v, 64)[:, 0:48]
+            return carry
+
+        lax.fori_loop(0, size // 2, body, 0)
+        for q, (src, dst) in enumerate(((field, field_out), (resid, resid_out))):
+            for h in range(2):
+                at = pl.ds(p * size + 24 * h, size)
+                c = pltpu.make_async_copy(src.at[at], dst.at[at], sems.at[4 * p + 2 * q + h])
+                c.start()
+                copies.append(c)
+    for c in copies:
+        c.wait()
 
 
 def solution(mesh):
     sizes = tuple(mesh.shape[a] for a in ("gx", "gy", "gz"))
     n3, n4 = 24 * sizes[2] + 2 * GUARD, 3 * sizes[2]
-    scratch = [pltpu.VMEM((L0.total, 128), F32)] * 8
+    scratch = [pltpu.VMEM((48, 48, 48), F32)] * 3 + [pltpu.SemaphoreType.DMA((3,))]
+    scratch += [pltpu.VMEM((L0.total, 128), F32)] * 4
     scratch += [pltpu.VMEM((L1.total, 128), F32)] * 6
     scratch += [pltpu.VMEM((L2.total, 128), F32)] * 6
     scratch += [pltpu.VMEM((n3, 128), F32)] * 6
@@ -759,17 +793,30 @@
     counts = tuple(len(g) for g in groups)
     vmem = pl.BlockSpec(memory_space=pltpu.VMEM)
 
+    anywhere = pl.BlockSpec(memory_space=pl.ANY)
+
     def body(right_side, start_guess, reaction):
+        whole = pltpu.VMEM((L0.total, 128), F32)
+        parts = pl.pallas_call(
+            functools.partial(kernel, sizes, counts),
+            out_shape=[whole] * 4 + [pltpu.VMEM((8, 128), F32)],
+            in_specs=[anywhere] * 3,
+            out_specs=[vmem] * 5,
+            scratch_shapes=scratch,
+            compiler_params=pltpu.CompilerParams(
+                collective_id=0, has_side_effects=True, vmem_limit_bytes=60 * 2**20
+            ),
+        )(right_side, start_guess, reaction)
         shape = jax.ShapeDtypeStruct(right_side.shape, F32)
         return tuple(
             pl.pallas_call(
-                functools.partial(kernel, sizes, counts),
+                finish,
                 out_shape=[shape, shape],
-                in_specs=[vmem] * 3,
-                out_specs=[vmem] * 2,
-                scratch_shapes=scratch,
-                compiler_params=pltpu.CompilerParams(collective_id=0, has_side_effects=True),
-            )(right_side, start_guess, reaction)
+                in_specs=[vmem] * 5,
+                out_specs=[anywhere] * 2,
+                scratch_shapes=[pltpu.VMEM(right_side.shape, F32)] * 2 + [pltpu.SemaphoreType.DMA((16,))],
+                compiler_params=pltpu.CompilerParams(vmem_limit_bytes=16 * 2**20),
+            )(*parts)
         )
 
     placed = P("gx", "gy", "gz")

time: 107 us -> 61.4 us (0.57)
  Pallas kernels: 103 us -> 60.4 us
  local copies, waits for them, and re-layouts: 3.47 us -> 0 us
    pallas_call x1 -> x2, Pallas kernels: 103 us -> 60.4 us  [the longest x1 58.3 us: body(): pl.pallas_call(functools.partial(kernel, sizes, counts), out_shape=[whole...]
    unnamed x4 -> x0, local copies, waits for them, and re-layouts: 3.47 us -> none
where the time goes in v2:
time: 61.4 us; the launch traced here: 61 us
  Pallas kernels  60.4 us (98%)
  between operations  0.64 us (1%)
    pallas_call x1, Pallas kernels, body(): pl.pallas_call(functools.partial(kernel, sizes, counts), out_shape=[whole...  58.3 us
    pallas_call x1, Pallas kernels, body(): pl.pallas_call(finish, out_shape=[shape, shape], in_specs=[vmem] * 5, out...  2.11 us

profile of v2, /device:TPU:1, one launch (start us, length us, event | category | flops | bytes accessed | tf_op | source)
XLA Modules:
  0.0 61.0 jit_solution(16013871654311069286)
XLA Ops:
  0.6 58.3 %shard_map.50 = (f32[1808,128]{1,0:T(8,128)S(1)}, f32[1808,128]{1,0:T(8,128)S(1)}, f32[1808,128]{1,0:T(8,128)S(1)}, f32[1808,128]{1,0:T(8,128)S(1)}, f32[8,128]{1,0:T(8,128)S(1)}) custom-call(f32[48,48,48]{2,1,0:T(8,128)} %right_in.1, f32[48,48,48]{2,1,0:T(8,128)} %guess_in.1, f32[48,48,48]{2,1,0:T(8,128)} %react_in.1), custom_call_target="tpu_custom_call" | custom-call | tf_op jit(solution)/shard_map/pallas_call | solution.py:800
  58.9 2.1 %shard_map.51 = (f32[48,48,48]{2,1,0:T(8,128)}, f32[48,48,48]{2,1,0:T(8,128)}) custom-call(f32[1808,128]{1,0:T(8,128)S(1)} %get-tuple-element.7.guess, f32[1808,128]{1,0:T(8,128)S(1)} %get-tuple-element.8.r0, f32[1808,128]{1,0:T(8,128)S(1)} %get-tuple-element.9.eb0, f32[1808,128]{1,0:T(8,128)S(1)} %get-tuple-element.10.left0, ...), custom_call_target="tpu_custom_call" | custom-call | tf_op jit(solution)/shard_map/pallas_call | solution.py:812

commit v3 on v2

--- a/solution.py
+++ b/solution.py
@@ -184,47 +184,48 @@
         self.drows = -(-self.drows // 8) * 8
         assert sum(it.w * it.w for it in items) <= 64
 
+        self.z0 = [0, self.zrows]
+        self.d0 = [2 * self.zrows + q * self.drows for q in range(4)]
+        self.y0 = [2 * self.zrows + 4 * self.drows + q * self.yrows for q in range(2)]
+        self.total = 2 * (self.zrows + self.yrows) + 4 * self.drows
+        self.xtotal = sum(it.w * it.g.R for it in items)
+
     def scratch(self):
-        x = [pltpu.VMEM((it.w * it.g.R, 128), F32) for it in self.items]
-        return x + [
-            pltpu.VMEM((2, self.yrows, 128), F32),
-            pltpu.VMEM((2, self.yrows, 128), F32),
-            pltpu.VMEM((2, self.zrows, 128), F32),
-            pltpu.VMEM((2, self.zrows, 128), F32),
-            pltpu.VMEM((4, self.drows, 128), F32),
-            pltpu.VMEM((4, self.drows, 128), F32),
-            pltpu.SemaphoreType.DMA((11,)),
-            pltpu.SemaphoreType.DMA((11,)),
+        return [
+            pltpu.VMEM((self.xtotal, 128), F32),
+            pltpu.VMEM((self.total, 128), F32),
+            pltpu.VMEM((self.total, 128), F32),
+            pltpu.SemaphoreType.DMA((2,)),
+            pltpu.SemaphoreType.DMA((2,)),
         ]
 
 
 class Exchange:
     def __init__(self, plan, refs, scratch, place):
-        n = len(plan.items)
         self.plan, self.refs, self.place = plan, refs, place
-        self.xr = scratch[:n]
-        self.ys, self.yr, self.zs, self.zr, self.ds, self.dr, self.ss, self.rs = scratch[n:]
+        self.xr, self.sent, self.got, self.ss, self.rs = scratch
         gx, gy, gz = place.me
+        self.partner = (1 - gx, gy, gz)
         self.x_copies = []
+        o = 0
         for k, it in enumerate(plan.items):
             g = it.g
             start = jnp.where(gx == 0, g.nx - it.w, 0)
             r = pl.multiple_of(GUARD + (g.halo + start) * g.R, 8)
-            self.x_copies.append(
-                self.copy(refs[k].at[pl.ds(r, it.w * g.R), :], self.xr[k], k, (1 - gx, gy, gz))
-            )
+            n = it.w * g.R
+            self.x_copies.append(self.copy(refs[k].at[pl.ds(r, n), :], self.xr.at[pl.ds(o, n), :], 0, self.partner))
+            o += n
         self.y_copies, self.z_copies, self.d_copies = [], [], []
         for d in range(2):
-            self.y_copies.append(self.copy(self.ys.at[d], self.yr.at[d], 3 + d, place.beside(0, 1 - 2 * d, 0)))
-            self.z_copies.append(self.copy(self.zs.at[d], self.zr.at[d], 5 + d, place.beside(0, 0, 1 - 2 * d)))
+            self.y_copies.append(self.segment(plan.y0[d], plan.yrows, place.beside(0, 1 - 2 * d, 0)))
+            self.z_copies.append(self.segment(plan.z0[d], plan.zrows, place.beside(0, 0, 1 - 2 * d)))
             for e in range(2):
                 self.d_copies.append(
-                    self.copy(
-                        self.ds.at[2 * d + e], self.dr.at[2 * d + e], 7 + 2 * d + e,
-                        place.beside(0, 1 - 2 * d, 1 - 2 * e),
-                    )
+                    self.segment(plan.d0[2 * d + e], plan.drows, place.beside(0, 1 - 2 * d, 1 - 2 * e))
                 )
-        self.copies = self.y_copies + self.z_copies + self.d_copies
+
+    def segment(self, start, n, peer):
+        return self.copy(self.sent.at[pl.ds(start, n), :], self.got.at[pl.ds(start, n), :], 1, peer)
 
     def copy(self, src, dst, k, peer):
         return pltpu.make_async_remote_copy(
@@ -237,20 +238,30 @@
             c.start()
 
     def x_fill(self):
-        for c in self.x_copies:
-            c.wait()
+        self.copy(self.xr, self.xr, 0, self.partner).wait()
         m0, m1 = self.place.x_masks
+        o = 0
         for k, it in enumerate(self.plan.items):
             g, w, ref = it.g, it.w, self.refs[k]
             upper = ((lanes(g.R) + 8) & 127) >= 64
             for j in range(w):
-                got = self.xr[k][pl.ds(j * g.R, g.R), :]
+                got = self.xr[pl.ds(o + j * g.R, g.R), :]
                 top = ref[pl.ds(GUARD + (g.halo + g.nx - w + j) * g.R, g.R), :]
                 low = ref[pl.ds(GUARD + (g.halo + j) * g.R, g.R), :]
                 ref[pl.ds(GUARD + (g.halo - w + j) * g.R, g.R), :] = roll(jnp.where(upper, got * m1, top), 64)
                 ref[pl.ds(GUARD + (g.halo + g.nx + j) * g.R, g.R), :] = roll(jnp.where(upper, low, got * m0), 64)
+            o += w * g.R
 
     def pack_send(self):
+        self.pack(True)
+        for c in self.d_copies + self.y_copies:
+            c.start()
+
+    def send(self):
+        for c in self.z_copies + self.d_copies + self.y_copies:
+            c.start()
+
+    def pack(self, early=False):
         zo = 0
         for g, _, slots in self.plan.tiles:
             lane = lanes(g.ny) & 63
@@ -262,10 +273,11 @@
                     moved = roll(v, at - z)
                     acc[q] = moved if acc[q] is None else jnp.where(lane >= at, moved, acc[q])
             for q in range(2):
-                self.zs[q, pl.ds(zo, g.ny), :] = acc[q]
+                self.sent[pl.ds(self.plan.z0[q] + zo, g.ny), :] = acc[q]
             zo += g.ny
-        for c in self.z_copies:
-            c.start()
+        if early:
+            for c in self.z_copies:
+                c.start()
         yo, co = 0, 0
         corner = [None] * 4
         for k, it in enumerate(self.plan.items):
@@ -276,7 +288,7 @@
                 at = co + (d - 1) * w
                 for e, y in enumerate((g.ny - d, d - 1)):
                     v = ref[pl.ds(g.row(0, y), n, stride=g.R), :]
-                    self.ys[e, pl.ds(yo, n), :] = v
+                    self.sent[pl.ds(self.plan.y0[e] + yo, n), :] = v
                     if n < self.plan.drows:
                         v = jnp.concatenate([v, jnp.zeros((self.plan.drows - n, 128), F32)], axis=0)
                     for q, z in enumerate((g.nz - w, 0)):
@@ -286,18 +298,15 @@
                 yo += n
             co += w * w
         for q in range(4):
-            self.ds[q] = corner[q]
-        for c in self.d_copies + self.y_copies:
-            c.start()
+            self.sent[pl.ds(self.plan.d0[q], self.plan.drows), :] = corner[q]
 
     def unpack(self):
         my, mz = self.place.y_masks, self.place.z_masks
-        for c in self.copies:
-            c.wait()
+        self.copy(self.sent, self.got, 1, self.partner).wait()
         zo = 0
         for g, _, slots in self.plan.tiles:
             lane = lanes(g.ny) & 63
-            got = [self.zr[q, pl.ds(zo, g.ny), :] * mz[q] for q in range(2)]
+            got = [self.got[pl.ds(self.plan.z0[q] + zo, g.ny), :] * mz[q] for q in range(2)]
             for k, x, at in slots:
                 w = self.plan.items[k].w
                 rows = pl.ds(g.row(x, 0), g.ny)
@@ -315,9 +324,9 @@
             for d in range(1, w + 1):
                 at = co + (d - 1) * w
                 for e, y in enumerate((-d, g.ny + d - 1)):
-                    v = self.yr[e, pl.ds(yo, n), :]
+                    v = self.got[pl.ds(self.plan.y0[e] + yo, n), :]
                     for q, z in enumerate((-w, g.nz)):
-                        got = self.dr[2 * e + q, pl.ds(0, n), :] * mz[q]
+                        got = self.got[pl.ds(self.plan.d0[2 * e + q], n), :] * mz[q]
                         v = jnp.where(into[q], roll(got, z - at), v)
                     ref[pl.ds(g.row(0, y), n, stride=g.R), :] = v * my[e]
                 yo += n
@@ -341,67 +350,47 @@
 
 
 class Gather:
-    def __init__(self, place, scratch):
-        self.place = place
-        self.mine, self.got, self.sum, self.s1, self.r1, self.s2, self.r2 = scratch
+    rows = 24
+
+    def __init__(self, place, scratch, whole):
+        self.place, self.whole = place, whole
+        self.mine, self.got, self.sum, self.ss, self.rs = scratch
         n = place.sizes
         self.near = [(a, b) for a in range(n[0]) for b in range(n[1])][1:]
-
-    def first_copies(self):
-        n = self.place.sizes
-        out = []
-        for a, b in self.near:
-            k = a * n[1] + b
-            out.append(
-                pltpu.make_async_remote_copy(
-                    src_ref=self.mine, dst_ref=self.got.at[k], send_sem=self.s1.at[k], recv_sem=self.r1.at[k],
-                    device_id=self.place.beside(a, b, 0), device_id_type=MESH,
-                )
-            )
-        return out
-
-    def second_copies(self, target):
-        out = []
+        self.at = pl.ds(pl.multiple_of(GUARD + self.rows * place.me[2], 8), self.rows)
+
+    def copy(self, src, dst, k, peer):
+        return pltpu.make_async_remote_copy(
+            src_ref=src, dst_ref=dst, send_sem=self.ss.at[k], recv_sem=self.rs.at[k],
+            device_id=peer, device_id_type=MESH,
+        )
+
+    def send(self):
+        for k, (a, b) in enumerate(self.near):
+            self.copy(self.mine, self.got.at[k], 0, self.place.beside(a, b, 0)).start()
+
+    def relay(self):
+        self.copy(self.got, self.got, 0, self.place.beside(1, 0, 0)).wait()
+        total = self.mine[...]
+        for k in range(len(self.near)):
+            total = total + self.got[k]
+        self.sum[...] = total
         for c in range(1, self.place.sizes[2]):
-            out.append(
-                pltpu.make_async_remote_copy(
-                    src_ref=self.sum, dst_ref=target(c), send_sem=self.s2.at[c], recv_sem=self.r2.at[c],
-                    device_id=self.place.beside(0, 0, c), device_id_type=MESH,
-                )
-            )
-        return out
-
-    def send(self):
-        for c in self.first_copies():
-            c.start()
-
-    def relay(self, target):
-        for c in self.first_copies():
-            c.wait()
-        total = self.mine[...]
-        n = self.place.sizes
-        for a, b in self.near:
-            total = total + self.got[a * n[1] + b]
-        self.sum[...] = total
-        for c in self.second_copies(target):
-            c.start()
-        return total
-
-    def finish(self, target):
-        for c in self.second_copies(target):
-            c.wait()
-
-
-def gather_scratch(sizes, rows):
-    near = sizes[0] * sizes[1]
+            self.copy(self.sum, self.whole.at[self.at, :], 1, self.place.beside(0, 0, c)).start()
+        self.whole[self.at, :] = total
+
+    def finish(self):
+        most = self.whole.at[pl.ds(GUARD, self.rows * (self.place.sizes[2] - 1)), :]
+        self.copy(most, most, 1, self.place.beside(1, 0, 0)).wait()
+
+
+def gather_scratch(sizes):
     return [
-        pltpu.VMEM((rows, 128), F32),
-        pltpu.VMEM((near, rows, 128), F32),
-        pltpu.VMEM((rows, 128), F32),
-        pltpu.SemaphoreType.DMA((near,)),
-        pltpu.SemaphoreType.DMA((near,)),
-        pltpu.SemaphoreType.DMA((sizes[2],)),
-        pltpu.SemaphoreType.DMA((sizes[2],)),
+        pltpu.VMEM((24, 128), F32),
+        pltpu.VMEM((sizes[0] * sizes[1] - 1, 24, 128), F32),
+        pltpu.VMEM((24, 128), F32),
+        pltpu.SemaphoreType.DMA((2,)),
+        pltpu.SemaphoreType.DMA((2,)),
     ]
 
 
@@ -471,23 +460,28 @@
 def bottom(source, s4, p4, n, ny):
     estimate = jnp.zeros_like(source)
     left = source
-    direction = source
-    now = dot_all(left, left)
-    shifted = s4[...]
+    inside = (lanes(n) < 96) & ((lanes(n) & 15) < ny)
+    shifted = 6.0 * FACTOR4 + s4[...]
     for it in range(BOTTOM_ITERS):
-        p4[pl.ds(GUARD, n), :] = direction
+        p4[pl.ds(GUARD, n), :] = left
         b = p4[pl.ds(GUARD + 1, n), :] + p4[pl.ds(GUARD - 1, n), :]
-        b = b + (roll(direction, 1) + roll(direction, -1))
-        b = b + (roll(direction, 16) + roll(direction, -16))
-        inside = (lanes(n) < 96) & ((lanes(n) & 15) < ny)
-        image = FACTOR4 * (6.0 * direction - jnp.where(inside, b, 0.0)) + shifted * direction
-        step = now / dot_all(direction, image)
+        b = b + (roll(left, 1) + roll(left, -1))
+        b = b + (roll(left, 16) + roll(left, -16))
+        image = shifted * left - FACTOR4 * jnp.where(inside, b, 0.0)
+        now = dot_all(left, left)
+        bent = dot_all(left, image)
+        if it == 0:
+            step = now / bent
+            direction, turned = left, image
+        else:
+            ratio = now / before
+            step = now / (bent - ratio * now / step)
+            direction = left + ratio * direction
+            turned = image + ratio * turned
+        before = now
         estimate = estimate + step * direction
         if it < BOTTOM_ITERS - 1:
-            left = left - step * image
-            after = dot_all(left, left)
-            direction = left + (after / now) * direction
-            now = after
+            left = left - step * turned
     return estimate
 
 
@@ -497,6 +491,11 @@
 PLAN_C = Plan([Item(L0, 3)])
 PLAN_D = Plan([Item(L2, 5)])
 PLANS = (PLAN_A, PLAN_S, PLAN_B, PLAN_C, PLAN_D)
+
+
+def far(p, sizes):
+    ring = lambda d, n: min(d % n, -d % n)
+    return p[0] + ring(p[1], sizes[1]) + ring(p[2], 4) + ring(p[2] // 4, 4)
 
 
 def kernel(sizes, counts, right_in, guess_in, react_in, guess, r0, eb0, left0, step_out, *scratch):
@@ -519,12 +518,11 @@
     gx, gy, gz = place.me
     n3, n4, ny3 = 24 * sizes[2], 3 * sizes[2], 6 * sizes[1]
 
-    loads = [
-        pltpu.make_async_copy(src, dst, in_sems.at[k])
-        for k, (src, dst) in enumerate(zip((guess_in, right_in, react_in), raw))
-    ]
-    for c in loads:
-        c.start()
+    inputs = (guess_in, right_in, react_in)
+    for k in range(3):
+        for q in range(4):
+            at = pl.ds(12 * q, 12)
+            pltpu.make_async_copy(inputs[k].at[at], raw[k].at[at], in_sems.at[k]).start()
 
     def clear(ref):
         n = ref.shape[0]
@@ -537,31 +535,17 @@
 
         lax.fori_loop(0, n // size, step, 0)
 
-    clear(f3)
-    clear(s3)
-    peers = {(a, b, 0) for a in range(sizes[0]) for b in range(sizes[1])}
-    peers |= {(0, 0, c) for c in range(sizes[2])}
-    peers |= {(0, b % sizes[1], c % sizes[2]) for b in (1, -1) for c in (1, -1)}
-    peers = sorted(peers - {(0, 0, 0)})
+    peers = [(a, b, c) for a in range(sizes[0]) for b in range(sizes[1]) for c in range(sizes[2])][1:]
+    peers.sort(key=lambda p: -far(p, sizes))
     barrier = pltpu.get_barrier_semaphore()
     for p in peers:
         pl.semaphore_signal(barrier, inc=1, device_id=place.beside(*p), device_id_type=MESH)
     for ref in (guess, right, react, f1, s1, ea1, eb1, f2, s2, ea2, eb2, ea3, eb3, p4, square):
         clear(ref)
     spread[...] = jnp.zeros_like(spread)
-
-    for c in loads:
-        c.wait()
-
-    def load(i, carry):
-        for src, dst in zip(raw, (guess, right, react)):
-            for k in range(2):
-                r = GUARD + (L0.halo + 2 * i + k) * L0.R + L0.y0
-                dst[pl.ds(r, 48), 0:48] = src[2 * i + k]
-                dst[pl.ds(r, 48), 64:112] = src[2 * i + k + 24]
-        return carry
-
-    lax.fori_loop(0, 12, load, 0)
+    for ref in (f3, s3):
+        for r in (0, GUARD + n3):
+            ref[pl.ds(r, GUARD), :] = jnp.zeros((GUARD, 128), F32)
 
     a = iota2((128, 128), 0)
     b = iota2((128, 128), 1)
@@ -573,21 +557,30 @@
     hit = a == ((base(b) + (zb >> 1)) & 127)
     up_m[...] = jnp.where(hit, 1.0, 0.0).astype(BF16)
 
+    for k, dst in enumerate((guess, right, react)):
+        pltpu.make_async_copy(inputs[k], raw[k], in_sems.at[k]).wait()
+
+        def load(i, carry):
+            for q in range(4):
+                r = GUARD + (L0.halo + 4 * i + q) * L0.R + L0.y0
+                dst[pl.ds(r, 48), 0:48] = raw[k][4 * i + q]
+                dst[pl.ds(r, 48), 64:112] = raw[k][4 * i + q + 24]
+            return carry
+
+        lax.fori_loop(0, 6, load, 0)
+
     ex_a = Exchange(PLAN_A, (guess, right, react), scr[0], place)
     ex_s = Exchange(PLAN_S, (s1, s2), scr[1], place)
     ex_b = Exchange(PLAN_B, (f1,), scr[2], place)
     ex_c = Exchange(PLAN_C, (eb0,), scr[3], place)
     ex_d = Exchange(PLAN_D, (f2,), scr[4], place)
-    ga_s = Gather(place, scr[5])
-    ga_f = Gather(place, scr[6])
-    ga_r = Gather(place, scr[7])
-    reduced = scr[8][0]
-
-    def slot(ref):
-        return lambda c: ref.at[pl.ds(pl.multiple_of(GUARD + 24 * gz, 8), 24), :]
-
+    ga_s = Gather(place, scr[5], s3)
+    ga_f = Gather(place, scr[6], f3)
+    reduced, red_send, red_recv = scr[7]
+
+    ex_a.pack()
     pl.semaphore_wait(barrier, len(peers))
-    ex_a.pack_send()
+    ex_a.send()
 
     restrict(react, L0, s1, L1, 0, 12, 0, 24, down_m, tmp)
     restrict(s1, L1, s2, L2, 0, 6, 0, 12, down_m, tmp)
@@ -621,7 +614,7 @@
     ex_s.x_fill()
     for g, sh, inv in ((L1, s1, inv1), (L2, s2, inv2)):
         planes(g, -g.halo, g.nx + g.halo, lambda r: [(inv, inverse(sh[pl.ds(r, g.R), :], g.factor))])
-    s3[pl.ds(pl.multiple_of(GUARD + 24 * gz, 8), 24), :] = ga_s.relay(slot(s3))
+    ga_s.relay()
 
     ex_b.unpack()
     ex_b.x_send()
@@ -643,18 +636,18 @@
 
     ex_c.unpack()
     ex_c.x_send()
-    ga_s.finish(slot(s3))
+    ga_s.finish()
     chunks3(n3, inv3, lambda r, n: inverse(s3[pl.ds(r, n), :], FACTOR3))
     s4[...] = restrict4(s3, n4, ny3)
 
-    f3[pl.ds(pl.multiple_of(GUARD + 24 * gz, 8), 24), :] = ga_f.relay(slot(f3))
+    ga_f.relay()
     ex_d.unpack()
     ex_d.x_send()
     ex_c.x_fill()
     ex_d.x_fill()
     first(L2, ea2, f2, inv2, -5, 11)
     relax(L2, ea2, eb2, f2, s2, inv2, -4, 10)
-    ga_f.finish(slot(f3))
+    ga_f.finish()
 
     def relax3(src, dst):
         def body(r, n):
@@ -733,13 +726,26 @@
     upper = jnp.sum(upper, axis=0, keepdims=True)
     lower = jnp.sum(lower, axis=0, keepdims=True)
     half = lanes(1) < 64
-    ga_r.mine[...] = jnp.where(half, upper + roll(upper, 64), lower + roll(lower, 64))
-    ga_r.send()
-    own = ga_r.relay(lambda c: reduced.at[c])
-    ga_r.finish(lambda c: reduced.at[c])
-    total = own
-    for c in range(1, sizes[2]):
-        total = total + reduced[c]
+    number = (gx * sizes[1] + gy) * sizes[2] + gz
+    reduced[number] = jnp.where(half, upper + roll(upper, 64), lower + roll(lower, 64))
+    own = reduced.at[number]
+
+    def summed(src, dst, p):
+        return pltpu.make_async_remote_copy(
+            src_ref=src, dst_ref=dst, send_sem=red_send.at[0], recv_sem=red_recv.at[0],
+            device_id=place.beside(*p), device_id_type=MESH,
+        )
+
+    for p in peers:
+        summed(own, own, p).start()
+    most = reduced.at[pl.ds(0, len(peers))]
+    summed(most, most, peers[0]).wait()
+    sums = [reduced[k] for k in range(8)]
+    for k in range(8, len(peers) + 1):
+        sums[k % 8] = sums[k % 8] + reduced[k]
+    while len(sums) > 1:
+        sums = [x + y for x, y in zip(sums[::2], sums[1::2])]
+    total = sums[0]
     upper = jnp.sum(jnp.where(half, total, 0.0), axis=1, keepdims=True)
     lower = jnp.sum(jnp.where(half, 0.0, total), axis=1, keepdims=True)
     step_out[...] = jnp.broadcast_to(upper / lower, (8, 128))
@@ -786,8 +792,9 @@
     scratch += [pltpu.VMEM((128, 128), BF16)] * 2 + [pltpu.VMEM((16 * 56, 128), F32)]
     scratch += [pltpu.VMEM((128, 128), F32)] * 2
     scratch += [pltpu.VMEM((3, 128, 128), F32), pltpu.VMEM((40, 128), F32)]
-    groups = [p.scratch() for p in PLANS] + [gather_scratch(sizes, 24)] * 2 + [gather_scratch(sizes, 1)]
-    groups += [[pltpu.VMEM((sizes[2], 1, 128), F32)]]
+    groups = [p.scratch() for p in PLANS] + [gather_scratch(sizes)] * 2
+    devices = sizes[0] * sizes[1] * sizes[2]
+    groups += [[pltpu.VMEM((devices, 1, 128), F32)] + [pltpu.SemaphoreType.DMA((1,))] * 2]
     for g in groups:
         scratch += g
     counts = tuple(len(g) for g in groups)

time: 61.4 us -> 57.8 us (0.941)
  Pallas kernels: 60.4 us -> 57 us
    pallas_call x1, Pallas kernels: 58.3 us -> 54.9 us  [body(): pl.pallas_call(functools.partial(kernel, sizes, counts), out_shape=[whole...]
where the time goes in v3:
time: 57.8 us; the launch traced here: 57.7 us
  Pallas kernels  57 us (99%)
  between operations  0.64 us (1%)
    pallas_call x1, Pallas kernels, body(): pl.pallas_call(functools.partial(kernel, sizes, counts), out_shape=[whole...  54.9 us
    pallas_call x1, Pallas kernels, body(): pl.pallas_call(finish, out_shape=[shape, shape], in_specs=[vmem] * 5, out...  2.11 us

profile of v3, /device:TPU:1, one launch (start us, length us, event | category | flops | bytes accessed | tf_op | source)
XLA Modules:
  0.0 57.7 jit_solution(15834217088889135981)
XLA Ops:
  0.6 54.9 %shard_map.50 = (f32[1808,128]{1,0:T(8,128)S(1)}, f32[1808,128]{1,0:T(8,128)S(1)}, f32[1808,128]{1,0:T(8,128)S(1)}, f32[1808,128]{1,0:T(8,128)S(1)}, f32[8,128]{1,0:T(8,128)S(1)}) custom-call(f32[48,48,48]{2,1,0:T(8,128)} %right_in.1, f32[48,48,48]{2,1,0:T(8,128)} %guess_in.1, f32[48,48,48]{2,1,0:T(8,128)} %react_in.1), custom_call_target="tpu_custom_call" | custom-call | tf_op jit(solution)/shard_map/pallas_call | solution.py:807
  55.6 2.1 %shard_map.51 = (f32[48,48,48]{2,1,0:T(8,128)}, f32[48,48,48]{2,1,0:T(8,128)}) custom-call(f32[1808,128]{1,0:T(8,128)S(1)} %get-tuple-element.7.guess, f32[1808,128]{1,0:T(8,128)S(1)} %get-tuple-element.8.r0, f32[1808,128]{1,0:T(8,128)S(1)} %get-tuple-element.9.eb0, f32[1808,128]{1,0:T(8,128)S(1)} %get-tuple-element.10.left0, ...), custom_call_target="tpu_custom_call" | custom-call | tf_op jit(solution)/shard_map/pallas_call | solution.py:819

commit v4 on v3

--- a/solution.py
+++ b/solution.py
@@ -26,9 +26,9 @@
         return GUARD + (self.halo + x) * self.R + self.y0 + y
 
 
-L0 = Geo(24, 48, 48, 4, 56, 4, 0, 4)
-L1 = Geo(12, 24, 24, 6, 40, 8, 1, 6)
-L2 = Geo(6, 12, 12, 5, 24, 6, 2, 8)
+L0 = Geo(24, 48, 48, 4, 56, 4, 0, 28)
+L1 = Geo(12, 24, 24, 6, 40, 8, 1, 24)
+L2 = Geo(6, 12, 12, 5, 24, 6, 2, 16)
 FACTOR3 = 0.25**3
 FACTOR4 = 0.25**4
 
@@ -39,6 +39,12 @@
 
 def iota2(shape, dim):
     return lax.broadcasted_iota(jnp.int32, shape, dim)
+
+
+def tree(terms):
+    while len(terms) > 1:
+        terms = [sum(terms[k + 1 : k + 2], terms[k]) for k in range(0, len(terms), 2)]
+    return terms[0]
 
 
 def roll(v, shift):
@@ -215,17 +221,25 @@
             n = it.w * g.R
             self.x_copies.append(self.copy(refs[k].at[pl.ds(r, n), :], self.xr.at[pl.ds(o, n), :], 0, self.partner))
             o += n
+        at = {}
+        for d in range(2):
+            at[1 - 2 * d, 0] = plan.y0[d]
+            at[0, 1 - 2 * d] = plan.z0[d]
+            for e in range(2):
+                at[1 - 2 * d, 1 - 2 * e] = plan.d0[2 * d + e]
         self.y_copies, self.z_copies, self.d_copies = [], [], []
-        for d in range(2):
-            self.y_copies.append(self.segment(plan.y0[d], plan.yrows, place.beside(0, 1 - 2 * d, 0)))
-            self.z_copies.append(self.segment(plan.z0[d], plan.zrows, place.beside(0, 0, 1 - 2 * d)))
-            for e in range(2):
-                self.d_copies.append(
-                    self.segment(plan.d0[2 * d + e], plan.drows, place.beside(0, 1 - 2 * d, 1 - 2 * e))
-                )
-
-    def segment(self, start, n, peer):
-        return self.copy(self.sent.at[pl.ds(start, n), :], self.got.at[pl.ds(start, n), :], 1, peer)
+        for d in (1, -1):
+            self.y_copies.append(self.segment(at, d, 0, plan.yrows))
+            self.z_copies.append(self.segment(at, 0, d, plan.zrows))
+            for e in (1, -1):
+                self.d_copies.append(self.segment(at, d, e, plan.drows))
+
+    def segment(self, at, dy, dz, n):
+        there = self.place.exists(dy, dz)
+        peer = self.place.beside(0, dy, dz)
+        peer = tuple(jnp.where(there, p, q) for p, q in zip(peer, self.partner))
+        target = pl.multiple_of(jnp.where(there, at[dy, dz], at[-dy, -dz]), 8)
+        return self.copy(self.sent.at[pl.ds(at[dy, dz], n), :], self.got.at[pl.ds(target, n), :], 1, peer)
 
     def copy(self, src, dst, k, peer):
         return pltpu.make_async_remote_copy(
@@ -343,6 +357,11 @@
         self.y_masks = (one(gy > 0), one(gy < sizes[1] - 1))
         self.z_masks = (one(gz > 0), one(gz < sizes[2] - 1))
 
+    def exists(self, dy, dz):
+        gx, gy, gz = self.me
+        y, z = gy + dy, gz + dz
+        return (y >= 0) & (y < self.sizes[1]) & (z >= 0) & (z < self.sizes[2])
+
     def beside(self, dx, dy, dz):
         return tuple(
             lax.rem(m + d % n, n) if d % n else m for m, d, n in zip(self.me, (dx, dy, dz), self.sizes)
@@ -428,7 +447,7 @@
 
 
 def chunks3(rows, ref, body):
-    n = min(rows, 192)
+    n = min(rows, 384)
 
     def step(i, carry):
         r = pl.multiple_of(GUARD + i * n, 8)
@@ -560,14 +579,9 @@
     for k, dst in enumerate((guess, right, react)):
         pltpu.make_async_copy(inputs[k], raw[k], in_sems.at[k]).wait()
 
-        def load(i, carry):
-            for q in range(4):
-                r = GUARD + (L0.halo + 4 * i + q) * L0.R + L0.y0
-                dst[pl.ds(r, 48), 0:48] = raw[k][4 * i + q]
-                dst[pl.ds(r, 48), 64:112] = raw[k][4 * i + q + 24]
-            return carry
-
-        lax.fori_loop(0, 6, load, 0)
+        for i in range(24):
+            dst[pl.ds(L0.row(i, 0), 48), 0:48] = raw[k][i]
+            dst[pl.ds(L0.row(i, 0), 48), 64:112] = raw[k][i + 24]
 
     ex_a = Exchange(PLAN_A, (guess, right, react), scr[0], place)
     ex_s = Exchange(PLAN_S, (s1, s2), scr[1], place)
@@ -708,21 +722,15 @@
     row = iota2((L0.R, 128), 0)
     inside = ((lanes(L0.R) & 63) < 48) & (row >= L0.y0) & (row < L0.y0 + 48)
 
-    def last(i, sums):
-        upper, lower = sums
-        images = []
-        for k in range(4):
-            r = pl.multiple_of(GUARD + (L0.halo + 4 * i + k) * L0.R, 8)
-            c, image = image_of(eb0, react, L0, r)
-            images.append((r, image))
-            upper = upper + jnp.where(inside, c * r0[pl.ds(r, L0.R), :], 0.0)
-            lower = lower + jnp.where(inside, c * image, 0.0)
-        for r, image in images:
-            left0[pl.ds(r, L0.R), :] = image
-        return upper, lower
-
-    zero = jnp.zeros((L0.R, 128), F32)
-    upper, lower = lax.fori_loop(0, 6, last, (zero, zero))
+    upper, lower = [], []
+    for i in range(24):
+        r = GUARD + (L0.halo + i) * L0.R
+        c, image = image_of(eb0, react, L0, r)
+        left0[pl.ds(r, L0.R), :] = image
+        upper.append(c * r0[pl.ds(r, L0.R), :])
+        lower.append(c * image)
+    upper = jnp.where(inside, tree(upper), 0.0)
+    lower = jnp.where(inside, tree(lower), 0.0)
     upper = jnp.sum(upper, axis=0, keepdims=True)
     lower = jnp.sum(lower, axis=0, keepdims=True)
     half = lanes(1) < 64
@@ -743,9 +751,7 @@
     sums = [reduced[k] for k in range(8)]
     for k in range(8, len(peers) + 1):
         sums[k % 8] = sums[k % 8] + reduced[k]
-    while len(sums) > 1:
-        sums = [x + y for x, y in zip(sums[::2], sums[1::2])]
-    total = sums[0]
+    total = tree(sums)
     upper = jnp.sum(jnp.where(half, total, 0.0), axis=1, keepdims=True)
     lower = jnp.sum(jnp.where(half, 0.0, total), axis=1, keepdims=True)
     step_out[...] = jnp.broadcast_to(upper / lower, (8, 128))
@@ -756,20 +762,14 @@
     copies = []
     parts, size = 4, 6
     for p in range(parts):
-        def body(i, carry):
-            for k in range(2):
-                x = p * size + 2 * i + k
-                at = pl.ds(GUARD + (L0.halo + x) * L0.R + L0.y0, 48)
-                e = eb0[at, :]
-                v = guess[at, :] + step * e
-                field[x] = v[:, 0:48]
-                field[x + 24] = roll(v, 64)[:, 0:48]
-                v = r0[at, :] - step * left0[at, :]
-                resid[x] = v[:, 0:48]
-                resid[x + 24] = roll(v, 64)[:, 0:48]
-            return carry
-
-        lax.fori_loop(0, size // 2, body, 0)
+        for x in range(p * size, p * size + size):
+            at = pl.ds(L0.row(x, 0), 48)
+            v = guess[at, :] + step * eb0[at, :]
+            field[x] = v[:, 0:48]
+            field[x + 24] = roll(v, 64)[:, 0:48]
+            v = r0[at, :] - step * left0[at, :]
+            resid[x] = v[:, 0:48]
+            resid[x + 24] = roll(v, 64)[:, 0:48]
         for q, (src, dst) in enumerate(((field, field_out), (resid, resid_out))):
             for h in range(2):
                 at = pl.ds(p * size + 24 * h, size)

time: 57.8 us -> 50.4 us (0.87)
  Pallas kernels: 57 us -> 49.7 us
    pallas_call x1, Pallas kernels: 54.9 us -> 48 us  [body(): pl.pallas_call(functools.partial(kernel, sizes, counts), out_shape=[whole...]
where the time goes in v4:
time: 50.4 us; the launch traced here: 50.3 us
  Pallas kernels  49.7 us (99%)
  between operations  0.64 us (1%)
    pallas_call x1, Pallas kernels, body(): pl.pallas_call(functools.partial(kernel, sizes, counts), out_shape=[whole...  48 us
    pallas_call x1, Pallas kernels, body(): pl.pallas_call(finish, out_shape=[shape, shape], in_specs=[vmem] * 5, out...  1.68 us

profile of v4, /device:TPU:1, one launch (start us, length us, event | category | flops | bytes accessed | tf_op | source)
XLA Modules:
  0.0 50.3 jit_solution(18280070654922372033)
XLA Ops:
  0.6 48.0 %shard_map.50 = (f32[1808,128]{1,0:T(8,128)S(1)}, f32[1808,128]{1,0:T(8,128)S(1)}, f32[1808,128]{1,0:T(8,128)S(1)}, f32[1808,128]{1,0:T(8,128)S(1)}, f32[8,128]{1,0:T(8,128)S(1)}) custom-call(f32[48,48,48]{2,1,0:T(8,128)} %right_in.1, f32[48,48,48]{2,1,0:T(8,128)} %guess_in.1, f32[48,48,48]{2,1,0:T(8,128)} %react_in.1), custom_call_target="tpu_custom_call" | custom-call | tf_op jit(solution)/shard_map/pallas_call | solution.py:807
  48.6 1.7 %shard_map.51 = (f32[48,48,48]{2,1,0:T(8,128)}, f32[48,48,48]{2,1,0:T(8,128)}) custom-call(f32[1808,128]{1,0:T(8,128)S(1)} %get-tuple-element.7.guess, f32[1808,128]{1,0:T(8,128)S(1)} %get-tuple-element.8.r0, f32[1808,128]{1,0:T(8,128)S(1)} %get-tuple-element.9.eb0, f32[1808,128]{1,0:T(8,128)S(1)} %get-tuple-element.10.left0, ...), custom_call_target="tpu_custom_call" | custom-call | tf_op jit(solution)/shard_map/pallas_call | solution.py:819

commit v5 on v4

--- a/solution.py
+++ b/solution.py
@@ -12,6 +12,7 @@
 BF16 = jnp.bfloat16
 DAMP = 6.0 / 7.0
 GUARD = 8
+GUARD3 = 16
 BOTTOM_ITERS = 6
 
 
@@ -52,18 +53,14 @@
     return v if shift == 0 else pltpu.roll(v, shift, 1)
 
 
-def split3(a):
+def split(a):
     hi = a.astype(BF16)
-    rest = a - hi.astype(F32)
-    mid = rest.astype(BF16)
-    low = (rest - mid.astype(F32)).astype(BF16)
-    return hi, mid, low
+    return hi, (a - hi.astype(F32)).astype(BF16)
 
 
 def mm(a, b):
-    parts = split3(a)
-    out = [jnp.dot(p, b, preferred_element_type=F32) for p in parts]
-    return out[0] + (out[1] + out[2])
+    hi, low = split(a)
+    return jnp.dot(hi, b, preferred_element_type=F32) + jnp.dot(low, b, preferred_element_type=F32)
 
 
 def beside_of(ref, r, R):
@@ -317,18 +314,6 @@
     def unpack(self):
         my, mz = self.place.y_masks, self.place.z_masks
         self.copy(self.sent, self.got, 1, self.partner).wait()
-        zo = 0
-        for g, _, slots in self.plan.tiles:
-            lane = lanes(g.ny) & 63
-            got = [self.got[pl.ds(self.plan.z0[q] + zo, g.ny), :] * mz[q] for q in range(2)]
-            for k, x, at in slots:
-                w = self.plan.items[k].w
-                rows = pl.ds(g.row(x, 0), g.ny)
-                v = self.refs[k][rows, :]
-                v = jnp.where(lane >= 64 - w, roll(got[0], -w - at), v)
-                v = jnp.where((lane >= g.nz) & (lane < g.nz + w), roll(got[1], g.nz - at), v)
-                self.refs[k][rows, :] = v
-            zo += g.ny
         yo, co = 0, 0
         for k, it in enumerate(self.plan.items):
             g, w, ref = it.g, it.w, self.refs[k]
@@ -345,6 +330,27 @@
                     ref[pl.ds(g.row(0, y), n, stride=g.R), :] = v * my[e]
                 yo += n
             co += w * w
+        self.unpack_z(True)
+
+    def unpack_rest(self):
+        self.unpack_z(False)
+
+    def unpack_z(self, edge):
+        mz = self.place.z_masks
+        zo = 0
+        for g, _, slots in self.plan.tiles:
+            lane = lanes(g.ny) & 63
+            got = [self.got[pl.ds(self.plan.z0[q] + zo, g.ny), :] * mz[q] for q in range(2)]
+            for k, x, at in slots:
+                w = self.plan.items[k].w
+                if (x < w or x >= g.nx - w) != edge:
+                    continue
+                rows = pl.ds(g.row(x, 0), g.ny)
+                v = self.refs[k][rows, :]
+                v = jnp.where(lane >= 64 - w, roll(got[0], -w - at), v)
+                v = jnp.where((lane >= g.nz) & (lane < g.nz + w), roll(got[1], g.nz - at), v)
+                self.refs[k][rows, :] = v
+            zo += g.ny
 
 
 class Place:
@@ -376,7 +382,9 @@
         self.mine, self.got, self.sum, self.ss, self.rs = scratch
         n = place.sizes
         self.near = [(a, b) for a in range(n[0]) for b in range(n[1])][1:]
-        self.at = pl.ds(pl.multiple_of(GUARD + self.rows * place.me[2], 8), self.rows)
+        self.near.sort(key=lambda p: -far((p[0], p[1], 0), n))
+        self.line = sorted(range(1, n[2]), key=lambda c: -far((0, 0, c), n))
+        self.at = pl.ds(pl.multiple_of(GUARD3 + self.rows * place.me[2], 8), self.rows)
 
     def copy(self, src, dst, k, peer):
         return pltpu.make_async_remote_copy(
@@ -394,12 +402,12 @@
         for k in range(len(self.near)):
             total = total + self.got[k]
         self.sum[...] = total
-        for c in range(1, self.place.sizes[2]):
+        for c in self.line:
             self.copy(self.sum, self.whole.at[self.at, :], 1, self.place.beside(0, 0, c)).start()
         self.whole[self.at, :] = total
 
     def finish(self):
-        most = self.whole.at[pl.ds(GUARD, self.rows * (self.place.sizes[2] - 1)), :]
+        most = self.whole.at[pl.ds(GUARD3, self.rows * (self.place.sizes[2] - 1)), :]
         self.copy(most, most, 1, self.place.beside(1, 0, 0)).wait()
 
 
@@ -450,7 +458,7 @@
     n = min(rows, 384)
 
     def step(i, carry):
-        r = pl.multiple_of(GUARD + i * n, 8)
+        r = pl.multiple_of(GUARD3 + i * n, 8)
         ref[pl.ds(r, n), :] = body(r, n)
         return carry
 
@@ -466,7 +474,7 @@
 def restrict4(src, n, ny):
     total = None
     for k in range(3):
-        t = src[pl.ds(GUARD + k, n, stride=8), :] + src[pl.ds(GUARD + k + 4, n, stride=8), :]
+        t = src[pl.ds(GUARD3 + k, n, stride=8), :] + src[pl.ds(GUARD3 + k + 4, n, stride=8), :]
         part = mm(t, jnp.where(match4(k, (128, 128), 1, ny), 0.125, 0.0).astype(BF16))
         total = part if total is None else total + part
     return total
@@ -490,14 +498,15 @@
         now = dot_all(left, left)
         bent = dot_all(left, image)
         if it == 0:
-            step = now / bent
+            denom = bent
             direction, turned = left, image
         else:
-            ratio = now / before
-            step = now / (bent - ratio * now / step)
+            ratio = now * inv_before
+            denom = bent - ratio * ratio * denom
             direction = left + ratio * direction
             turned = image + ratio * turned
-        before = now
+        step = now / denom
+        inv_before = 1.0 / now
         estimate = estimate + step * direction
         if it < BOTTOM_ITERS - 1:
             left = left - step * turned
@@ -546,7 +555,7 @@
     def clear(ref):
         n = ref.shape[0]
         size = next(k for k in (128, 122 * 8, 80, 8) if n % k == 0) if n > 128 else n
-        size = {1808: 904, 976: 488}.get(n, size)
+        size = {1808: 904, 976: 488, 416: 208}.get(n, size)
 
         def step(i, carry):
             ref[pl.ds(pl.multiple_of(i * size, 8), size), :] = jnp.zeros((size, 128), F32)
@@ -562,9 +571,9 @@
     for ref in (guess, right, react, f1, s1, ea1, eb1, f2, s2, ea2, eb2, ea3, eb3, p4, square):
         clear(ref)
     spread[...] = jnp.zeros_like(spread)
-    for ref in (f3, s3):
-        for r in (0, GUARD + n3):
-            ref[pl.ds(r, GUARD), :] = jnp.zeros((GUARD, 128), F32)
+    for ref in (f3, s3, inv3):
+        for r in (0, GUARD3 + n3):
+            ref[pl.ds(r, GUARD3), :] = jnp.zeros((GUARD3, 128), F32)
 
     a = iota2((128, 128), 0)
     b = iota2((128, 128), 1)
@@ -613,6 +622,7 @@
 
     ex_a.unpack()
     ex_a.x_send()
+    ex_a.unpack_rest()
     planes(L0, 1, 23, start)
     ex_a.x_fill()
     planes(L0, -2, 1, start)
@@ -650,6 +660,7 @@
 
     ex_c.unpack()
     ex_c.x_send()
+    ex_c.unpack_rest()
     ga_s.finish()
     chunks3(n3, inv3, lambda r, n: inverse(s3[pl.ds(r, n), :], FACTOR3))
     s4[...] = restrict4(s3, n4, ny3)
@@ -678,18 +689,19 @@
     for k in range(3):
         u = mm(e4, jnp.where(match4(k, (128, 128), 0, ny3), 1.0, 0.0).astype(BF16))
         for q in (k, k + 4):
-            at = pl.ds(GUARD + q, n4, stride=8)
+            at = pl.ds(GUARD3 + q, n4, stride=8)
             eb3[at, :] = eb3[at, :] + u
-    relax3(eb3, ea3)
-    relax3(ea3, eb3)
-
-    slab[...] = eb3[pl.ds(pl.multiple_of(24 * gz, 8), 40), :]
+    for src, dst, n in ((eb3, ea3, 48), (ea3, slab, 40)):
+        r = pl.multiple_of(GUARD3 + 24 * gz - (n - 24) // 2, 4)
+        c, image = image3(src, s3, r, n)
+        at = pl.ds(r, n)
+        dst[at if n == 48 else pl.ds(0, n), :] = c + inv3[at, :] * (f3[at, :] - image)
     for k in range(3):
         v = slab[pl.ds(k, 10, stride=4), :]
         for h in range(2):
             for q in range(2):
                 spread[k, pl.ds(64 * h + q, 10, stride=2), :] = v
-    wide = [jnp.concatenate(p, axis=1) for p in zip(*[split3(spread[k]) for k in range(3)])]
+    wide = [jnp.concatenate(p, axis=1) for p in zip(*[split(spread[k]) for k in range(3)])]
     coarse = []
     for h in range(2):
         r = iota2((112, 384), 0)
@@ -699,7 +711,7 @@
         parts = [
             lax.dot_general(pick, p, (((1,), (1,)), ((), ())), preferred_element_type=F32) for p in wide
         ]
-        coarse.append(parts[0] + (parts[1] + parts[2]))
+        coarse.append(parts[0] + parts[1])
     fine = roll(jnp.where(lanes(112) < 64, coarse[0], coarse[1]), -4)
     for i in range(7):
         u = fine[16 * i : 16 * i + 10]
@@ -782,7 +794,7 @@
 
 def solution(mesh):
     sizes = tuple(mesh.shape[a] for a in ("gx", "gy", "gz"))
-    n3, n4 = 24 * sizes[2] + 2 * GUARD, 3 * sizes[2]
+    n3, n4 = 24 * sizes[2] + 2 * GUARD3, 3 * sizes[2]
     scratch = [pltpu.VMEM((48, 48, 48), F32)] * 3 + [pltpu.SemaphoreType.DMA((3,))]
     scratch += [pltpu.VMEM((L0.total, 128), F32)] * 4
     scratch += [pltpu.VMEM((L1.total, 128), F32)] * 6

time: 50.4 us -> 47.8 us (0.948)
  Pallas kernels: 49.7 us -> 47.1 us
    pallas_call x1, Pallas kernels: 48 us -> 45.4 us  [body(): pl.pallas_call(functools.partial(kernel, sizes, counts), out_shape=[whole...]
where the time goes in v5:
time: 47.8 us; the launch traced here: 47.7 us
  Pallas kernels  47.1 us (99%)
  between operations  0.64 us (1%)
    pallas_call x1, Pallas kernels, body(): pl.pallas_call(functools.partial(kernel, sizes, counts), out_shape=[whole...  45.4 us
    pallas_call x1, Pallas kernels, body(): pl.pallas_call(finish, out_shape=[shape, shape], in_specs=[vmem] * 5, out...  1.68 us

profile of v5, /device:TPU:1, one launch (start us, length us, event | category | flops | bytes accessed | tf_op | source)
XLA Modules:
  0.0 47.7 jit_solution(4241969766864691397)
XLA Ops:
  0.6 45.4 %shard_map.50 = (f32[1808,128]{1,0:T(8,128)S(1)}, f32[1808,128]{1,0:T(8,128)S(1)}, f32[1808,128]{1,0:T(8,128)S(1)}, f32[1808,128]{1,0:T(8,128)S(1)}, f32[8,128]{1,0:T(8,128)S(1)}) custom-call(f32[48,48,48]{2,1,0:T(8,128)} %right_in.1, f32[48,48,48]{2,1,0:T(8,128)} %guess_in.1, f32[48,48,48]{2,1,0:T(8,128)} %react_in.1), custom_call_target="tpu_custom_call" | custom-call | tf_op jit(solution)/shard_map/pallas_call | solution.py:819
  46.1 1.7 %shard_map.51 = (f32[48,48,48]{2,1,0:T(8,128)}, f32[48,48,48]{2,1,0:T(8,128)}) custom-call(f32[1808,128]{1,0:T(8,128)S(1)} %get-tuple-element.7.guess, f32[1808,128]{1,0:T(8,128)S(1)} %get-tuple-element.8.r0, f32[1808,128]{1,0:T(8,128)S(1)} %get-tuple-element.9.eb0, f32[1808,128]{1,0:T(8,128)S(1)} %get-tuple-element.10.left0, ...), custom_call_target="tpu_custom_call" | custom-call | tf_op jit(solution)/shard_map/pallas_call | solution.py:831

commit v6 on v5

--- a/solution.py
+++ b/solution.py
@@ -248,8 +248,12 @@
         for c in self.x_copies:
             c.start()
 
+    def settle(self):
+        self.copy(self.xr, self.xr, 0, self.partner).wait_send()
+        self.copy(self.sent, self.got, 1, self.partner).wait_send()
+
     def x_fill(self):
-        self.copy(self.xr, self.xr, 0, self.partner).wait()
+        self.copy(self.xr, self.xr, 0, self.partner).wait_recv()
         m0, m1 = self.place.x_masks
         o = 0
         for k, it in enumerate(self.plan.items):
@@ -264,31 +268,37 @@
             o += w * g.R
 
     def pack_send(self):
-        self.pack(True)
-        for c in self.d_copies + self.y_copies:
+        self.pack_sides()
+        for c in self.d_copies:
             c.start()
+        self.pack_z()
+        for c in self.z_copies + self.y_copies:
+            c.start()
+
+    def pack(self):
+        self.pack_sides()
+        self.pack_z()
 
     def send(self):
-        for c in self.z_copies + self.d_copies + self.y_copies:
+        for c in self.d_copies + self.z_copies + self.y_copies:
             c.start()
 
-    def pack(self, early=False):
+    def pack_z(self):
         zo = 0
         for g, _, slots in self.plan.tiles:
-            lane = lanes(g.ny) & 63
+            lane = lanes(g.ny)
             acc = [None, None]
             for k, x, at in slots:
                 w = self.plan.items[k].w
-                v = self.refs[k][pl.ds(g.row(x, 0), g.ny), :]
-                for q, z in enumerate((g.nz - w, 0)):
-                    moved = roll(v, at - z)
-                    acc[q] = moved if acc[q] is None else jnp.where(lane >= at, moved, acc[q])
+                moved = roll(self.refs[k][pl.ds(g.row(x, 0), g.ny), :], at)
+                for q, past in enumerate((g.nz - self.plan.items[k].w, 0)):
+                    here = ((lane - past) & 63 >= at) & ((lane - past) & 63 < at + w)
+                    acc[q] = moved if acc[q] is None else jnp.where(here, moved, acc[q])
             for q in range(2):
                 self.sent[pl.ds(self.plan.z0[q] + zo, g.ny), :] = acc[q]
             zo += g.ny
-        if early:
-            for c in self.z_copies:
-                c.start()
+
+    def pack_sides(self):
         yo, co = 0, 0
         corner = [None] * 4
         for k, it in enumerate(self.plan.items):
@@ -313,7 +323,7 @@
 
     def unpack(self):
         my, mz = self.place.y_masks, self.place.z_masks
-        self.copy(self.sent, self.got, 1, self.partner).wait()
+        self.copy(self.sent, self.got, 1, self.partner).wait_recv()
         yo, co = 0, 0
         for k, it in enumerate(self.plan.items):
             g, w, ref = it.g, it.w, self.refs[k]
@@ -347,7 +357,7 @@
                     continue
                 rows = pl.ds(g.row(x, 0), g.ny)
                 v = self.refs[k][rows, :]
-                v = jnp.where(lane >= 64 - w, roll(got[0], -w - at), v)
+                v = jnp.where(lane >= 64 - w, roll(got[0], -g.nz - at), v)
                 v = jnp.where((lane >= g.nz) & (lane < g.nz + w), roll(got[1], g.nz - at), v)
                 self.refs[k][rows, :] = v
             zo += g.ny
@@ -397,7 +407,7 @@
             self.copy(self.mine, self.got.at[k], 0, self.place.beside(a, b, 0)).start()
 
     def relay(self):
-        self.copy(self.got, self.got, 0, self.place.beside(1, 0, 0)).wait()
+        self.copy(self.got, self.got, 0, self.place.beside(1, 0, 0)).wait_recv()
         total = self.mine[...]
         for k in range(len(self.near)):
             total = total + self.got[k]
@@ -407,8 +417,15 @@
         self.whole[self.at, :] = total
 
     def finish(self):
+        self.most().wait_recv()
+
+    def most(self):
         most = self.whole.at[pl.ds(GUARD3, self.rows * (self.place.sizes[2] - 1)), :]
-        self.copy(most, most, 1, self.place.beside(1, 0, 0)).wait()
+        return self.copy(most, most, 1, self.place.beside(1, 0, 0))
+
+    def settle(self):
+        self.copy(self.got, self.got, 0, self.place.beside(1, 0, 0)).wait_send()
+        self.most().wait_send()
 
 
 def gather_scratch(sizes):
@@ -672,6 +689,8 @@
     ex_d.x_fill()
     first(L2, ea2, f2, inv2, -5, 11)
     relax(L2, ea2, eb2, f2, s2, inv2, -4, 10)
+    for e in (ex_a, ex_s, ex_b, ex_c, ex_d, ga_s):
+        e.settle()
     ga_f.finish()
 
     def relax3(src, dst):
@@ -758,6 +777,7 @@
 
     for p in peers:
         summed(own, own, p).start()
+    ga_f.settle()
     most = reduced.at[pl.ds(0, len(peers))]
     summed(most, most, peers[0]).wait()
     sums = [reduced[k] for k in range(8)]

time: 47.8 us -> 47.7 us (level)
  no operation moved by 1% of the time
where the time goes in v6:
time: 47.7 us; the launch traced here: 47.6 us
  Pallas kernels  47 us (99%)
  between operations  0.64 us (1%)
    pallas_call x1, Pallas kernels, body(): pl.pallas_call(functools.partial(kernel, sizes, counts), out_shape=[whole...  45.3 us
    pallas_call x1, Pallas kernels, body(): pl.pallas_call(finish, out_shape=[shape, shape], in_specs=[vmem] * 5, out...  1.68 us

profile of v6, /device:TPU:1, one launch (start us, length us, event | category | flops | bytes accessed | tf_op | source)
XLA Modules:
  0.0 47.6 jit_solution(8422738137407182314)
XLA Ops:
  0.6 45.3 %shard_map.50 = (f32[1808,128]{1,0:T(8,128)S(1)}, f32[1808,128]{1,0:T(8,128)S(1)}, f32[1808,128]{1,0:T(8,128)S(1)}, f32[1808,128]{1,0:T(8,128)S(1)}, f32[8,128]{1,0:T(8,128)S(1)}) custom-call(f32[48,48,48]{2,1,0:T(8,128)} %right_in.1, f32[48,48,48]{2,1,0:T(8,128)} %guess_in.1, f32[48,48,48]{2,1,0:T(8,128)} %react_in.1), custom_call_target="tpu_custom_call" | custom-call | tf_op jit(solution)/shard_map/pallas_call | solution.py:839
  45.9 1.7 %shard_map.51 = (f32[48,48,48]{2,1,0:T(8,128)}, f32[48,48,48]{2,1,0:T(8,128)}) custom-call(f32[1808,128]{1,0:T(8,128)S(1)} %get-tuple-element.7.guess, f32[1808,128]{1,0:T(8,128)S(1)} %get-tuple-element.8.r0, f32[1808,128]{1,0:T(8,128)S(1)} %get-tuple-element.9.eb0, f32[1808,128]{1,0:T(8,128)S(1)} %get-tuple-element.10.left0, ...), custom_call_target="tpu_custom_call" | custom-call | tf_op jit(solution)/shard_map/pallas_call | solution.py:851

commit v7 on v6

--- a/solution.py
+++ b/solution.py
@@ -166,13 +166,14 @@
 
 
 class Plan:
-    def __init__(self, items):
-        self.items = items
-        self.yrows = sum(it.g.nx * it.w for it in items)
+    def __init__(self, items, cross=False):
+        self.items, self.cross = items, cross
+        self.counts = [it.w if cross else it.g.nx for it in items]
+        self.yrows = sum(n * it.w for n, it in zip(self.counts, items))
         self.yrows = -(-self.yrows // 8) * 8
         self.tiles = []
         for k, it in enumerate(items):
-            for x in range(it.g.nx):
+            for x in range(self.counts[k]):
                 for t in self.tiles:
                     if t[0] is it.g and t[1] + it.w <= 64:
                         break
@@ -183,7 +184,7 @@
                 t[1] += it.w
         self.zrows = sum(t[0].ny for t in self.tiles)
         self.zrows = -(-self.zrows // 8) * 8
-        self.drows = max(it.g.nx for it in items)
+        self.drows = max(self.counts)
         self.drows = -(-self.drows // 8) * 8
         assert sum(it.w * it.w for it in items) <= 64
 
@@ -194,8 +195,8 @@
         self.xtotal = sum(it.w * it.g.R for it in items)
 
     def scratch(self):
-        return [
-            pltpu.VMEM((self.xtotal, 128), F32),
+        x = [] if self.cross else [pltpu.VMEM((self.xtotal, 128), F32)]
+        return x + [
             pltpu.VMEM((self.total, 128), F32),
             pltpu.VMEM((self.total, 128), F32),
             pltpu.SemaphoreType.DMA((2,)),
@@ -212,12 +213,23 @@
         self.x_copies = []
         o = 0
         for k, it in enumerate(plan.items):
-            g = it.g
-            start = jnp.where(gx == 0, g.nx - it.w, 0)
-            r = pl.multiple_of(GUARD + (g.halo + start) * g.R, 8)
-            n = it.w * g.R
+            r = pl.multiple_of(GUARD + (it.g.halo + self.edge(it)) * it.g.R, 8)
+            n = it.w * it.g.R
             self.x_copies.append(self.copy(refs[k].at[pl.ds(r, n), :], self.xr.at[pl.ds(o, n), :], 0, self.partner))
             o += n
+        self.segments(0)
+
+    def edge(self, it):
+        return jnp.where(self.place.me[0] == 0, it.g.nx - it.w, 0)
+
+    def source(self, k, x, y):
+        return self.plan.items[k].g.row(x, y)
+
+    def target(self, k, x, y):
+        return self.refs[k], self.plan.items[k].g.row(x, y)
+
+    def segments(self, dx):
+        plan = self.plan
         at = {}
         for d in range(2):
             at[1 - 2 * d, 0] = plan.y0[d]
@@ -226,14 +238,14 @@
                 at[1 - 2 * d, 1 - 2 * e] = plan.d0[2 * d + e]
         self.y_copies, self.z_copies, self.d_copies = [], [], []
         for d in (1, -1):
-            self.y_copies.append(self.segment(at, d, 0, plan.yrows))
-            self.z_copies.append(self.segment(at, 0, d, plan.zrows))
+            self.y_copies.append(self.segment(at, dx, d, 0, plan.yrows))
+            self.z_copies.append(self.segment(at, dx, 0, d, plan.zrows))
             for e in (1, -1):
-                self.d_copies.append(self.segment(at, d, e, plan.drows))
-
-    def segment(self, at, dy, dz, n):
+                self.d_copies.append(self.segment(at, dx, d, e, plan.drows))
+
+    def segment(self, at, dx, dy, dz, n):
         there = self.place.exists(dy, dz)
-        peer = self.place.beside(0, dy, dz)
+        peer = self.place.beside(dx, dy, dz)
         peer = tuple(jnp.where(there, p, q) for p, q in zip(peer, self.partner))
         target = pl.multiple_of(jnp.where(there, at[dy, dz], at[-dy, -dz]), 8)
         return self.copy(self.sent.at[pl.ds(at[dy, dz], n), :], self.got.at[pl.ds(target, n), :], 1, peer)
@@ -248,12 +260,18 @@
         for c in self.x_copies:
             c.start()
 
-    def settle(self):
+    def settle(self, x=True):
+        if x:
+            self.x_sent()
+        self.copy(self.sent, self.got, 1, self.partner).wait_send()
+
+    def x_sent(self):
         self.copy(self.xr, self.xr, 0, self.partner).wait_send()
-        self.copy(self.sent, self.got, 1, self.partner).wait_send()
+
+    def x_wait(self):
+        self.copy(self.xr, self.xr, 0, self.partner).wait_recv()
 
     def x_fill(self):
-        self.copy(self.xr, self.xr, 0, self.partner).wait_recv()
         m0, m1 = self.place.x_masks
         o = 0
         for k, it in enumerate(self.plan.items):
@@ -290,7 +308,7 @@
             acc = [None, None]
             for k, x, at in slots:
                 w = self.plan.items[k].w
-                moved = roll(self.refs[k][pl.ds(g.row(x, 0), g.ny), :], at)
+                moved = roll(self.refs[k][pl.ds(self.source(k, x, 0), g.ny), :], at)
                 for q, past in enumerate((g.nz - self.plan.items[k].w, 0)):
                     here = ((lane - past) & 63 >= at) & ((lane - past) & 63 < at + w)
                     acc[q] = moved if acc[q] is None else jnp.where(here, moved, acc[q])
@@ -303,12 +321,12 @@
         corner = [None] * 4
         for k, it in enumerate(self.plan.items):
             g, w, ref = it.g, it.w, self.refs[k]
-            n = g.nx
+            n = self.plan.counts[k]
             lane = lanes(self.plan.drows) & 63
             for d in range(1, w + 1):
                 at = co + (d - 1) * w
                 for e, y in enumerate((g.ny - d, d - 1)):
-                    v = ref[pl.ds(g.row(0, y), n, stride=g.R), :]
+                    v = ref[pl.ds(self.source(k, 0, y), n, stride=g.R), :]
                     self.sent[pl.ds(self.plan.y0[e] + yo, n), :] = v
                     if n < self.plan.drows:
                         v = jnp.concatenate([v, jnp.zeros((self.plan.drows - n, 128), F32)], axis=0)
@@ -326,8 +344,8 @@
         self.copy(self.sent, self.got, 1, self.partner).wait_recv()
         yo, co = 0, 0
         for k, it in enumerate(self.plan.items):
-            g, w, ref = it.g, it.w, self.refs[k]
-            n = g.nx
+            g, w = it.g, it.w
+            n = self.plan.counts[k]
             lane = lanes(n) & 63
             into = (lane >= 64 - w, (lane >= g.nz) & (lane < g.nz + w))
             for d in range(1, w + 1):
@@ -337,7 +355,8 @@
                     for q, z in enumerate((-w, g.nz)):
                         got = self.got[pl.ds(self.plan.d0[2 * e + q], n), :] * mz[q]
                         v = jnp.where(into[q], roll(got, z - at), v)
-                    ref[pl.ds(g.row(0, y), n, stride=g.R), :] = v * my[e]
+                    ref, r = self.target(k, 0, y)
+                    ref[pl.ds(r, n, stride=g.R), :] = v * my[e]
                 yo += n
             co += w * w
         self.unpack_z(True)
@@ -355,12 +374,30 @@
                 w = self.plan.items[k].w
                 if (x < w or x >= g.nx - w) != edge:
                     continue
-                rows = pl.ds(g.row(x, 0), g.ny)
-                v = self.refs[k][rows, :]
+                ref, r = self.target(k, x, 0)
+                rows = pl.ds(r, g.ny)
+                v = ref[rows, :]
                 v = jnp.where(lane >= 64 - w, roll(got[0], -g.nz - at), v)
                 v = jnp.where((lane >= g.nz) & (lane < g.nz + w), roll(got[1], g.nz - at), v)
-                self.refs[k][rows, :] = v
+                ref[rows, :] = v
             zo += g.ny
+
+
+class Cross(Exchange):
+    def __init__(self, plan, main, scratch, place):
+        self.plan, self.main, self.refs, self.place = plan, main, main.refs, place
+        self.sent, self.got, self.ss, self.rs = scratch
+        self.partner = main.partner
+        self.segments(1)
+
+    def source(self, k, x, y):
+        it = self.plan.items[k]
+        return GUARD + (it.g.halo + self.edge(it) + x) * it.g.R + it.g.y0 + y
+
+    def target(self, k, x, y):
+        o = sum(it.w * it.g.R for it in self.plan.items[:k])
+        g = self.plan.items[k].g
+        return self.main.xr, o + x * g.R + g.y0 + y
 
 
 class Place:
@@ -533,9 +570,10 @@
 PLAN_A = Plan([Item(L0, 3), Item(L0, 2), Item(L0, 2)])
 PLAN_S = Plan([Item(L1, 6), Item(L2, 5)])
 PLAN_B = Plan([Item(L1, 6)])
+PLAN_BX = Plan([Item(L1, 6)], True)
 PLAN_C = Plan([Item(L0, 3)])
 PLAN_D = Plan([Item(L2, 5)])
-PLANS = (PLAN_A, PLAN_S, PLAN_B, PLAN_C, PLAN_D)
+PLANS = (PLAN_A, PLAN_S, PLAN_B, PLAN_C, PLAN_D, PLAN_BX)
 
 
 def far(p, sizes):
@@ -614,9 +652,10 @@
     ex_b = Exchange(PLAN_B, (f1,), scr[2], place)
     ex_c = Exchange(PLAN_C, (eb0,), scr[3], place)
     ex_d = Exchange(PLAN_D, (f2,), scr[4], place)
-    ga_s = Gather(place, scr[5], s3)
-    ga_f = Gather(place, scr[6], f3)
-    reduced, red_send, red_recv = scr[7]
+    cx_b = Cross(PLAN_BX, ex_b, scr[5], place)
+    ga_s = Gather(place, scr[6], s3)
+    ga_f = Gather(place, scr[7], f3)
+    reduced, red_send, red_recv = scr[8]
 
     ex_a.pack()
     pl.semaphore_wait(barrier, len(peers))
@@ -641,6 +680,7 @@
     ex_a.x_send()
     ex_a.unpack_rest()
     planes(L0, 1, 23, start)
+    ex_a.x_wait()
     ex_a.x_fill()
     planes(L0, -2, 1, start)
     planes(L0, 23, 26, start)
@@ -648,19 +688,24 @@
     leftover(L0, eb0, left0, r0, react, 0, 24)
     restrict(left0, L0, f1, L1, 0, 12, 0, 24, down_m, tmp)
     ex_b.pack_send()
+    cx_b.pack_send()
+    ex_b.x_send()
 
     ex_s.unpack()
     ex_s.x_send()
     ex_c.pack_send()
+    ex_s.x_wait()
     ex_s.x_fill()
     for g, sh, inv in ((L1, s1, inv1), (L2, s2, inv2)):
         planes(g, -g.halo, g.nx + g.halo, lambda r: [(inv, inverse(sh[pl.ds(r, g.R), :], g.factor))])
     ga_s.relay()
 
+    ex_b.x_sent()
     ex_b.unpack()
-    ex_b.x_send()
     first(L1, ea1, f1, inv1, 0, 12)
     relax(L1, ea1, eb1, f1, s1, inv1, 1, 11)
+    ex_b.x_wait()
+    cx_b.unpack()
     ex_b.x_fill()
     first(L1, ea1, f1, inv1, -6, 0)
     first(L1, ea1, f1, inv1, 12, 18)
@@ -685,12 +730,16 @@
     ga_f.relay()
     ex_d.unpack()
     ex_d.x_send()
+    ex_c.x_wait()
     ex_c.x_fill()
+    ex_d.x_wait()
     ex_d.x_fill()
     first(L2, ea2, f2, inv2, -5, 11)
     relax(L2, ea2, eb2, f2, s2, inv2, -4, 10)
-    for e in (ex_a, ex_s, ex_b, ex_c, ex_d, ga_s):
+    for e in (ex_a, ex_s, ex_c, ex_d, ga_s):
         e.settle()
+    for e in (ex_b, cx_b):
+        e.settle(False)
     ga_f.finish()
 
     def relax3(src, dst):

time: 47.7 us -> 47.2 us (0.990)
  Pallas kernels: 47 us -> 46.4 us
    pallas_call x1, Pallas kernels: 45.3 us -> 44.7 us  [body(): pl.pallas_call(functools.partial(kernel, sizes, counts), out_shape=[whole...]
where the time goes in v7:
time: 47.2 us; the launch traced here: 47.1 us
  Pallas kernels  46.4 us (98%)
  between operations  0.64 us (1%)
    pallas_call x1, Pallas kernels, body(): pl.pallas_call(functools.partial(kernel, sizes, counts), out_shape=[whole...  44.7 us
    pallas_call x1, Pallas kernels, body(): pl.pallas_call(finish, out_shape=[shape, shape], in_specs=[vmem] * 5, out...  1.68 us

profile of v7, /device:TPU:1, one launch (start us, length us, event | category | flops | bytes accessed | tf_op | source)
XLA Modules:
  0.0 47.1 jit_solution(13397672684619859774)
XLA Ops:
  0.6 44.7 %shard_map.50 = (f32[1808,128]{1,0:T(8,128)S(1)}, f32[1808,128]{1,0:T(8,128)S(1)}, f32[1808,128]{1,0:T(8,128)S(1)}, f32[1808,128]{1,0:T(8,128)S(1)}, f32[8,128]{1,0:T(8,128)S(1)}) custom-call(f32[48,48,48]{2,1,0:T(8,128)} %right_in.1, f32[48,48,48]{2,1,0:T(8,128)} %guess_in.1, f32[48,48,48]{2,1,0:T(8,128)} %react_in.1), custom_call_target="tpu_custom_call" | custom-call | tf_op jit(solution)/shard_map/pallas_call | solution.py:888
  45.4 1.7 %shard_map.51 = (f32[48,48,48]{2,1,0:T(8,128)}, f32[48,48,48]{2,1,0:T(8,128)}) custom-call(f32[1808,128]{1,0:T(8,128)S(1)} %get-tuple-element.7.guess, f32[1808,128]{1,0:T(8,128)S(1)} %get-tuple-element.8.r0, f32[1808,128]{1,0:T(8,128)S(1)} %get-tuple-element.9.eb0, f32[1808,128]{1,0:T(8,128)S(1)} %get-tuple-element.10.left0, ...), custom_call_target="tpu_custom_call" | custom-call | tf_op jit(solution)/shard_map/pallas_call | solution.py:900

commit v8 on v7

--- a/solution.py
+++ b/solution.py
@@ -620,8 +620,11 @@
 
     peers = [(a, b, c) for a in range(sizes[0]) for b in range(sizes[1]) for c in range(sizes[2])][1:]
     peers.sort(key=lambda p: -far(p, sizes))
+    beside = {(a, b % sizes[1], c % sizes[2]) for a in range(2) for b in (1, -1) for c in (1, -1)}
+    beside |= {(1, 0, c % sizes[2]) for c in (1, -1)}
+    greeted = [p for p in peers if p[2] == 0 or p[:2] == (0, 0) or p in beside]
     barrier = pltpu.get_barrier_semaphore()
-    for p in peers:
+    for p in greeted:
         pl.semaphore_signal(barrier, inc=1, device_id=place.beside(*p), device_id_type=MESH)
     for ref in (guess, right, react, f1, s1, ea1, eb1, f2, s2, ea2, eb2, ea3, eb3, p4, square):
         clear(ref)
@@ -658,7 +661,7 @@
     reduced, red_send, red_recv = scr[8]
 
     ex_a.pack()
-    pl.semaphore_wait(barrier, len(peers))
+    pl.semaphore_wait(barrier, len(greeted))
     ex_a.send()
 
     restrict(react, L0, s1, L1, 0, 12, 0, 24, down_m, tmp)

time: 47.2 us -> 46.4 us (0.983)
  Pallas kernels: 46.4 us -> 45.6 us
    pallas_call x1, Pallas kernels: 44.7 us -> 44 us  [body(): pl.pallas_call(functools.partial(kernel, sizes, counts), out_shape=[whole...]
where the time goes in v8:
time: 46.4 us; the launch traced here: 46.3 us
  Pallas kernels  45.6 us (98%)
  between operations  0.64 us (1%)
    pallas_call x1, Pallas kernels, body(): pl.pallas_call(functools.partial(kernel, sizes, counts), out_shape=[whole...  44 us
    pallas_call x1, Pallas kernels, body(): pl.pallas_call(finish, out_shape=[shape, shape], in_specs=[vmem] * 5, out...  1.68 us

profile of v8, /device:TPU:1, one launch (start us, length us, event | category | flops | bytes accessed | tf_op | source)
XLA Modules:
  0.0 46.3 jit_solution(10184441396322220419)
XLA Ops:
  0.6 44.0 %shard_map.50 = (f32[1808,128]{1,0:T(8,128)S(1)}, f32[1808,128]{1,0:T(8,128)S(1)}, f32[1808,128]{1,0:T(8,128)S(1)}, f32[1808,128]{1,0:T(8,128)S(1)}, f32[8,128]{1,0:T(8,128)S(1)}) custom-call(f32[48,48,48]{2,1,0:T(8,128)} %right_in.1, f32[48,48,48]{2,1,0:T(8,128)} %guess_in.1, f32[48,48,48]{2,1,0:T(8,128)} %react_in.1), custom_call_target="tpu_custom_call" | custom-call | tf_op jit(solution)/shard_map/pallas_call | solution.py:891
  44.6 1.7 %shard_map.51 = (f32[48,48,48]{2,1,0:T(8,128)}, f32[48,48,48]{2,1,0:T(8,128)}) custom-call(f32[1808,128]{1,0:T(8,128)S(1)} %get-tuple-element.7.guess, f32[1808,128]{1,0:T(8,128)S(1)} %get-tuple-element.8.r0, f32[1808,128]{1,0:T(8,128)S(1)} %get-tuple-element.9.eb0, f32[1808,128]{1,0:T(8,128)S(1)} %get-tuple-element.10.left0, ...), custom_call_target="tpu_custom_call" | custom-call | tf_op jit(solution)/shard_map/pallas_call | solution.py:903

commit v9 on v8

--- a/solution.py
+++ b/solution.py
@@ -666,11 +666,10 @@
 
     restrict(react, L0, s1, L1, 0, 12, 0, 24, down_m, tmp)
     restrict(s1, L1, s2, L2, 0, 6, 0, 12, down_m, tmp)
-    ex_s.pack_send()
+    ex_s.pack()
     ga_s.mine[...] = jnp.zeros((24, 128), F32)
     ga_f.mine[...] = jnp.zeros((24, 128), F32)
     to_level3(s2, ga_s.mine, square, turned, place)
-    ga_s.send()
 
     def start(r):
         at = pl.ds(r, L0.R)
@@ -681,6 +680,8 @@
 
     ex_a.unpack()
     ex_a.x_send()
+    ex_s.send()
+    ga_s.send()
     ex_a.unpack_rest()
     planes(L0, 1, 23, start)
     ex_a.x_wait()
@@ -694,9 +695,9 @@
     cx_b.pack_send()
     ex_b.x_send()
 
+    ex_c.pack()
     ex_s.unpack()
     ex_s.x_send()
-    ex_c.pack_send()
     ex_s.x_wait()
     ex_s.x_fill()
     for g, sh, inv in ((L1, s1, inv1), (L2, s2, inv2)):
@@ -705,6 +706,7 @@
 
     ex_b.x_sent()
     ex_b.unpack()
+    ex_c.send()
     first(L1, ea1, f1, inv1, 0, 12)
     relax(L1, ea1, eb1, f1, s1, inv1, 1, 11)
     ex_b.x_wait()
@@ -726,10 +728,6 @@
     ex_c.unpack()
     ex_c.x_send()
     ex_c.unpack_rest()
-    ga_s.finish()
-    chunks3(n3, inv3, lambda r, n: inverse(s3[pl.ds(r, n), :], FACTOR3))
-    s4[...] = restrict4(s3, n4, ny3)
-
     ga_f.relay()
     ex_d.unpack()
     ex_d.x_send()
@@ -739,6 +737,9 @@
     ex_d.x_fill()
     first(L2, ea2, f2, inv2, -5, 11)
     relax(L2, ea2, eb2, f2, s2, inv2, -4, 10)
+    ga_s.finish()
+    chunks3(n3, inv3, lambda r, n: inverse(s3[pl.ds(r, n), :], FACTOR3))
+    s4[...] = restrict4(s3, n4, ny3)
     for e in (ex_a, ex_s, ex_c, ex_d, ga_s):
         e.settle()
     for e in (ex_b, cx_b):

time: 46.4 us -> 45.2 us (0.974)
  Pallas kernels: 45.6 us -> 44.4 us
    pallas_call x1, Pallas kernels: 44 us -> 42.7 us  [body(): pl.pallas_call(functools.partial(kernel, sizes, counts), out_shape=[whole...]
where the time goes in v9:
time: 45.2 us; the launch traced here: 45 us
  Pallas kernels  44.4 us (98%)
  between operations  0.64 us (1%)
    pallas_call x1, Pallas kernels, body(): pl.pallas_call(functools.partial(kernel, sizes, counts), out_shape=[whole...  42.7 us
    pallas_call x1, Pallas kernels, body(): pl.pallas_call(finish, out_shape=[shape, shape], in_specs=[vmem] * 5, out...  1.68 us

profile of v9, /device:TPU:1, one launch (start us, length us, event | category | flops | bytes accessed | tf_op | source)
XLA Modules:
  0.0 45.0 jit_solution(11601393481652922592)
XLA Ops:
  0.6 42.7 %shard_map.50 = (f32[1808,128]{1,0:T(8,128)S(1)}, f32[1808,128]{1,0:T(8,128)S(1)}, f32[1808,128]{1,0:T(8,128)S(1)}, f32[1808,128]{1,0:T(8,128)S(1)}, f32[8,128]{1,0:T(8,128)S(1)}) custom-call(f32[48,48,48]{2,1,0:T(8,128)} %right_in.1, f32[48,48,48]{2,1,0:T(8,128)} %guess_in.1, f32[48,48,48]{2,1,0:T(8,128)} %react_in.1), custom_call_target="tpu_custom_call" | custom-call | tf_op jit(solution)/shard_map/pallas_call | solution.py:892
  43.4 1.7 %shard_map.51 = (f32[48,48,48]{2,1,0:T(8,128)}, f32[48,48,48]{2,1,0:T(8,128)}) custom-call(f32[1808,128]{1,0:T(8,128)S(1)} %get-tuple-element.7.guess, f32[1808,128]{1,0:T(8,128)S(1)} %get-tuple-element.8.r0, f32[1808,128]{1,0:T(8,128)S(1)} %get-tuple-element.9.eb0, f32[1808,128]{1,0:T(8,128)S(1)} %get-tuple-element.10.left0, ...), custom_call_target="tpu_custom_call" | custom-call | tf_op jit(solution)/shard_map/pallas_call | solution.py:904

commit v10 on v9

--- a/solution.py
+++ b/solution.py
@@ -286,58 +286,57 @@
             o += w * g.R
 
     def pack_send(self):
-        self.pack_sides()
-        for c in self.d_copies:
-            c.start()
-        self.pack_z()
-        for c in self.z_copies + self.y_copies:
-            c.start()
+        self.pack()
+        self.send()
 
     def pack(self):
-        self.pack_sides()
-        self.pack_z()
+        for k in range(len(self.refs)):
+            self.pack_item(k)
 
     def send(self):
         for c in self.d_copies + self.z_copies + self.y_copies:
             c.start()
 
-    def pack_z(self):
+    def pack_item(self, k):
+        if k == 0:
+            self.yo, self.co, self.corner = 0, 0, [None] * 4
+        it = self.plan.items[k]
+        g, w, ref = it.g, it.w, self.refs[k]
+        n = self.plan.counts[k]
+        lane = lanes(self.plan.drows) & 63
+        for d in range(1, w + 1):
+            at = self.co + (d - 1) * w
+            for e, y in enumerate((g.ny - d, d - 1)):
+                v = ref[pl.ds(self.source(k, 0, y), n, stride=g.R), :]
+                self.sent[pl.ds(self.plan.y0[e] + self.yo, n), :] = v
+                if n < self.plan.drows:
+                    v = jnp.concatenate([v, jnp.zeros((self.plan.drows - n, 128), F32)], axis=0)
+                for q, z in enumerate((g.nz - w, 0)):
+                    moved = roll(v, at - z)
+                    old = self.corner[2 * e + q]
+                    self.corner[2 * e + q] = moved if old is None else jnp.where(lane >= at, moved, old)
+            self.yo += n
+        self.co += w * w
+        if k == len(self.refs) - 1:
+            for q in range(4):
+                self.sent[pl.ds(self.plan.d0[q], self.plan.drows), :] = self.corner[q]
         zo = 0
-        for g, _, slots in self.plan.tiles:
-            lane = lanes(g.ny)
-            acc = [None, None]
-            for k, x, at in slots:
-                w = self.plan.items[k].w
-                moved = roll(self.refs[k][pl.ds(self.source(k, x, 0), g.ny), :], at)
-                for q, past in enumerate((g.nz - self.plan.items[k].w, 0)):
-                    here = ((lane - past) & 63 >= at) & ((lane - past) & 63 < at + w)
-                    acc[q] = moved if acc[q] is None else jnp.where(here, moved, acc[q])
-            for q in range(2):
-                self.sent[pl.ds(self.plan.z0[q] + zo, g.ny), :] = acc[q]
-            zo += g.ny
-
-    def pack_sides(self):
-        yo, co = 0, 0
-        corner = [None] * 4
-        for k, it in enumerate(self.plan.items):
-            g, w, ref = it.g, it.w, self.refs[k]
-            n = self.plan.counts[k]
-            lane = lanes(self.plan.drows) & 63
-            for d in range(1, w + 1):
-                at = co + (d - 1) * w
-                for e, y in enumerate((g.ny - d, d - 1)):
-                    v = ref[pl.ds(self.source(k, 0, y), n, stride=g.R), :]
-                    self.sent[pl.ds(self.plan.y0[e] + yo, n), :] = v
-                    if n < self.plan.drows:
-                        v = jnp.concatenate([v, jnp.zeros((self.plan.drows - n, 128), F32)], axis=0)
-                    for q, z in enumerate((g.nz - w, 0)):
-                        moved = roll(v, at - z)
-                        old = corner[2 * e + q]
-                        corner[2 * e + q] = moved if old is None else jnp.where(lane >= at, moved, old)
-                yo += n
-            co += w * w
-        for q in range(4):
-            self.sent[pl.ds(self.plan.d0[q], self.plan.drows), :] = corner[q]
+        for t, _, slots in self.plan.tiles:
+            if slots[-1][0] == k:
+                self.pack_tile(t, slots, zo)
+            zo += t.ny
+
+    def pack_tile(self, g, slots, zo):
+        lane = lanes(g.ny)
+        acc = [None, None]
+        for k, x, at in slots:
+            w = self.plan.items[k].w
+            moved = roll(self.refs[k][pl.ds(self.source(k, x, 0), g.ny), :], at)
+            for q, past in enumerate((g.nz - w, 0)):
+                here = ((lane - past) & 63 >= at) & ((lane - past) & 63 < at + w)
+                acc[q] = moved if acc[q] is None else jnp.where(here, moved, acc[q])
+        for q in range(2):
+            self.sent[pl.ds(self.plan.z0[q] + zo, g.ny), :] = acc[q]
 
     def unpack(self):
         my, mz = self.place.y_masks, self.place.z_masks
@@ -643,13 +642,6 @@
     hit = a == ((base(b) + (zb >> 1)) & 127)
     up_m[...] = jnp.where(hit, 1.0, 0.0).astype(BF16)
 
-    for k, dst in enumerate((guess, right, react)):
-        pltpu.make_async_copy(inputs[k], raw[k], in_sems.at[k]).wait()
-
-        for i in range(24):
-            dst[pl.ds(L0.row(i, 0), 48), 0:48] = raw[k][i]
-            dst[pl.ds(L0.row(i, 0), 48), 64:112] = raw[k][i + 24]
-
     ex_a = Exchange(PLAN_A, (guess, right, react), scr[0], place)
     ex_s = Exchange(PLAN_S, (s1, s2), scr[1], place)
     ex_b = Exchange(PLAN_B, (f1,), scr[2], place)
@@ -658,9 +650,16 @@
     cx_b = Cross(PLAN_BX, ex_b, scr[5], place)
     ga_s = Gather(place, scr[6], s3)
     ga_f = Gather(place, scr[7], f3)
+    for k, dst in enumerate((guess, right, react)):
+        pltpu.make_async_copy(inputs[k], raw[k], in_sems.at[k]).wait()
+
+        for i in range(24):
+            dst[pl.ds(L0.row(i, 0), 48), 0:48] = raw[k][i]
+            dst[pl.ds(L0.row(i, 0), 48), 64:112] = raw[k][i + 24]
+        ex_a.pack_item(k)
+
     reduced, red_send, red_recv = scr[8]
 
-    ex_a.pack()
     pl.semaphore_wait(barrier, len(greeted))
     ex_a.send()
 
@@ -698,10 +697,11 @@
     ex_c.pack()
     ex_s.unpack()
     ex_s.x_send()
-    ex_s.x_wait()
-    ex_s.x_fill()
-    for g, sh, inv in ((L1, s1, inv1), (L2, s2, inv2)):
-        planes(g, -g.halo, g.nx + g.halo, lambda r: [(inv, inverse(sh[pl.ds(r, g.R), :], g.factor))])
+
+    def inverse_of(g, sh, inv, first_plane, end):
+        planes(g, first_plane, end, lambda r: [(inv, inverse(sh[pl.ds(r, g.R), :], g.factor))])
+
+    inverse_of(L1, s1, inv1, 0, 12)
     ga_s.relay()
 
     ex_b.x_sent()
@@ -709,6 +709,11 @@
     ex_c.send()
     first(L1, ea1, f1, inv1, 0, 12)
     relax(L1, ea1, eb1, f1, s1, inv1, 1, 11)
+    ex_s.x_wait()
+    ex_s.x_fill()
+    inverse_of(L1, s1, inv1, -6, 0)
+    inverse_of(L1, s1, inv1, 12, 18)
+    inverse_of(L2, s2, inv2, -5, 11)
     ex_b.x_wait()
     cx_b.unpack()
     ex_b.x_fill()
@@ -725,10 +730,10 @@
     ga_f.send()
     ex_d.pack_send()
 
+    ga_f.relay()
     ex_c.unpack()
     ex_c.x_send()
     ex_c.unpack_rest()
-    ga_f.relay()
     ex_d.unpack()
     ex_d.x_send()
     ex_c.x_wait()

time: 45.2 us -> 46.2 us (1.022)
  Pallas kernels: 44.4 us -> 45.5 us
    pallas_call x1, Pallas kernels: 42.7 us -> 43.8 us  [body(): pl.pallas_call(functools.partial(kernel, sizes, counts), out_shape=[whole...]
where the time goes in v10:
time: 46.2 us; the launch traced here: 46.1 us
  Pallas kernels  45.5 us (98%)
  between operations  0.64 us (1%)
    pallas_call x1, Pallas kernels, body(): pl.pallas_call(functools.partial(kernel, sizes, counts), out_shape=[whole...  43.8 us
    pallas_call x1, Pallas kernels, body(): pl.pallas_call(finish, out_shape=[shape, shape], in_specs=[vmem] * 5, out...  1.68 us

profile of v10, /device:TPU:1, one launch (start us, length us, event | category | flops | bytes accessed | tf_op | source)
XLA Modules:
  0.0 46.1 jit_solution(5767178216701189257)
XLA Ops:
  0.6 43.8 %shard_map.50 = (f32[1808,128]{1,0:T(8,128)S(1)}, f32[1808,128]{1,0:T(8,128)S(1)}, f32[1808,128]{1,0:T(8,128)S(1)}, f32[1808,128]{1,0:T(8,128)S(1)}, f32[8,128]{1,0:T(8,128)S(1)}) custom-call(f32[48,48,48]{2,1,0:T(8,128)} %right_in.1, f32[48,48,48]{2,1,0:T(8,128)} %guess_in.1, f32[48,48,48]{2,1,0:T(8,128)} %react_in.1), custom_call_target="tpu_custom_call" | custom-call | tf_op jit(solution)/shard_map/pallas_call | solution.py:897
  44.4 1.7 %shard_map.51 = (f32[48,48,48]{2,1,0:T(8,128)}, f32[48,48,48]{2,1,0:T(8,128)}) custom-call(f32[1808,128]{1,0:T(8,128)S(1)} %get-tuple-element.7.guess, f32[1808,128]{1,0:T(8,128)S(1)} %get-tuple-element.8.r0, f32[1808,128]{1,0:T(8,128)S(1)} %get-tuple-element.9.eb0, f32[1808,128]{1,0:T(8,128)S(1)} %get-tuple-element.10.left0, ...), custom_call_target="tpu_custom_call" | custom-call | tf_op jit(solution)/shard_map/pallas_call | solution.py:909

commit v11 on v10

--- a/solution.py
+++ b/solution.py
@@ -702,7 +702,6 @@
         planes(g, first_plane, end, lambda r: [(inv, inverse(sh[pl.ds(r, g.R), :], g.factor))])
 
     inverse_of(L1, s1, inv1, 0, 12)
-    ga_s.relay()
 
     ex_b.x_sent()
     ex_b.unpack()
@@ -729,6 +728,7 @@
     to_level3(left2, ga_f.mine, square, turned, place)
     ga_f.send()
     ex_d.pack_send()
+    ga_s.relay()
 
     ga_f.relay()
     ex_c.unpack()

time: 46.2 us -> 45.2 us (0.978)
  Pallas kernels: 45.5 us -> 44.4 us
    pallas_call x1, Pallas kernels: 43.8 us -> 42.7 us  [body(): pl.pallas_call(functools.partial(kernel, sizes, counts), out_shape=[whole...]
where the time goes in v11:
time: 45.2 us; the launch traced here: 45 us
  Pallas kernels  44.4 us (98%)
  between operations  0.64 us (1%)
    pallas_call x1, Pallas kernels, body(): pl.pallas_call(functools.partial(kernel, sizes, counts), out_shape=[whole...  42.7 us
    pallas_call x1, Pallas kernels, body(): pl.pallas_call(finish, out_shape=[shape, shape], in_specs=[vmem] * 5, out...  1.68 us

profile of v11, /device:TPU:1, one launch (start us, length us, event | category | flops | bytes accessed | tf_op | source)
XLA Modules:
  0.0 45.0 jit_solution(233566799309767428)
XLA Ops:
  0.6 42.7 %shard_map.50 = (f32[1808,128]{1,0:T(8,128)S(1)}, f32[1808,128]{1,0:T(8,128)S(1)}, f32[1808,128]{1,0:T(8,128)S(1)}, f32[1808,128]{1,0:T(8,128)S(1)}, f32[8,128]{1,0:T(8,128)S(1)}) custom-call(f32[48,48,48]{2,1,0:T(8,128)} %right_in.1, f32[48,48,48]{2,1,0:T(8,128)} %guess_in.1, f32[48,48,48]{2,1,0:T(8,128)} %react_in.1), custom_call_target="tpu_custom_call" | custom-call | tf_op jit(solution)/shard_map/pallas_call | solution.py:897
  43.4 1.7 %shard_map.51 = (f32[48,48,48]{2,1,0:T(8,128)}, f32[48,48,48]{2,1,0:T(8,128)}) custom-call(f32[1808,128]{1,0:T(8,128)S(1)} %get-tuple-element.7.guess, f32[1808,128]{1,0:T(8,128)S(1)} %get-tuple-element.8.r0, f32[1808,128]{1,0:T(8,128)S(1)} %get-tuple-element.9.eb0, f32[1808,128]{1,0:T(8,128)S(1)} %get-tuple-element.10.left0, ...), custom_call_target="tpu_custom_call" | custom-call | tf_op jit(solution)/shard_map/pallas_call | solution.py:909

commit v12 on v11

--- a/solution.py
+++ b/solution.py
@@ -474,9 +474,18 @@
     ]
 
 
-def to_level3(src, mine, square, turned, place):
+def spread_to_level3(place):
+    gx, gy, gz = place.me
+    r = iota2((128, 384), 0)
+    l = iota2((128, 384), 1)
+    x = 6 * gx + 3 * (r >> 6) + ((r & 63) >> 3)
+    y = 6 * gy + (r & 7)
+    hit = (x == (l >> 5)) & (y == (l & 31)) & ((r & 7) < 6) & ((r & 63) < 24)
+    return jnp.where(hit, 1.0, 0.0).astype(BF16)
+
+
+def to_level3(src, mine, square, turned, chosen):
     g = L2
-    gx, gy, gz = place.me
     for i in range(3):
         r = g.row(2 * i, 0)
         t = src[pl.ds(r, 6, stride=2), :] + src[pl.ds(r + 1, 6, stride=2), :]
@@ -487,12 +496,7 @@
     a = turned[pl.ds(0, 8, stride=2), :] + turned[pl.ds(1, 8, stride=2), :]
     b = turned[pl.ds(64, 8, stride=2), :] + turned[pl.ds(65, 8, stride=2), :]
     a = (a + roll(b, 64)) * 0.125
-    r = iota2((128, 384), 0)
-    l = iota2((128, 384), 1)
-    x = 6 * gx + 3 * (r >> 6) + ((r & 63) >> 3)
-    y = 6 * gy + (r & 7)
-    hit = (x == (l >> 5)) & (y == (l & 31)) & ((r & 7) < 6) & ((r & 63) < 24)
-    out = mm(a, jnp.where(hit, 1.0, 0.0).astype(BF16))
+    out = mm(a, chosen[...])
     for k in range(3):
         mine[pl.ds(k, 6, stride=4), :] = out[0:6, 128 * k : 128 * k + 128]
 
@@ -524,11 +528,11 @@
     return ((c >> 4) == 2 * k + (l >> 6)) & ((c & 15) == ((l & 31) >> 1)) & ((l & 31) < ny)
 
 
-def restrict4(src, n, ny):
+def restrict4(src, n, matrix):
     total = None
     for k in range(3):
         t = src[pl.ds(GUARD3 + k, n, stride=8), :] + src[pl.ds(GUARD3 + k + 4, n, stride=8), :]
-        part = mm(t, jnp.where(match4(k, (128, 128), 1, ny), 0.125, 0.0).astype(BF16))
+        part = mm(t, matrix[k])
         total = part if total is None else total + part
     return total
 
@@ -595,6 +599,7 @@
     f2, s2, inv2, ea2, eb2, left2 = take(6)
     f3, s3, inv3, ea3, eb3, left3 = take(6)
     s4, p4, down_m, up_m, tmp, square, turned, spread, slab = take(9)
+    chosen, picks, down4, up4 = take(4)
     scr = [take(n) for n in counts]
     place = Place(sizes)
     gx, gy, gz = place.me
@@ -668,7 +673,17 @@
     ex_s.pack()
     ga_s.mine[...] = jnp.zeros((24, 128), F32)
     ga_f.mine[...] = jnp.zeros((24, 128), F32)
-    to_level3(s2, ga_s.mine, square, turned, place)
+    chosen[...] = spread_to_level3(place)
+    to_level3(s2, ga_s.mine, square, turned, chosen)
+    for h in range(2):
+        r = iota2((112, 384), 0)
+        l = iota2((112, 384), 1)
+        hit = (6 * gx + 3 * h + (r >> 4) - 2 == (l >> 5)) & (6 * gy + (r & 15) - 2 == (l & 31)) & ((r & 15) < 10)
+        picks[h] = jnp.where(hit, 1.0, 0.0).astype(BF16)
+    for k in range(3):
+        down4[k] = jnp.where(match4(k, (128, 128), 1, ny3), 0.125, 0.0).astype(BF16)
+        up4[k] = jnp.where(match4(k, (128, 128), 0, ny3), 1.0, 0.0).astype(BF16)
+
 
     def start(r):
         at = pl.ds(r, L0.R)
@@ -725,7 +740,7 @@
     first(L2, ea2, f2, inv2, -2, 8)
     relax(L2, ea2, eb2, f2, s2, inv2, -1, 7)
     leftover(L2, eb2, left2, f2, s2, 0, 6)
-    to_level3(left2, ga_f.mine, square, turned, place)
+    to_level3(left2, ga_f.mine, square, turned, chosen)
     ga_f.send()
     ex_d.pack_send()
     ga_s.relay()
@@ -744,7 +759,7 @@
     relax(L2, ea2, eb2, f2, s2, inv2, -4, 10)
     ga_s.finish()
     chunks3(n3, inv3, lambda r, n: inverse(s3[pl.ds(r, n), :], FACTOR3))
-    s4[...] = restrict4(s3, n4, ny3)
+    s4[...] = restrict4(s3, n4, down4)
     for e in (ex_a, ex_s, ex_c, ex_d, ga_s):
         e.settle()
     for e in (ex_b, cx_b):
@@ -762,9 +777,9 @@
     chunks3(n3, ea3, lambda r, n: inv3[pl.ds(r, n), :] * f3[pl.ds(r, n), :])
     relax3(ea3, eb3)
     chunks3(n3, left3, lambda r, n: f3[pl.ds(r, n), :] - image3(eb3, s3, r, n)[1])
-    e4 = bottom(restrict4(left3, n4, ny3), s4, p4, n4, ny3 // 2)
+    e4 = bottom(restrict4(left3, n4, down4), s4, p4, n4, ny3 // 2)
     for k in range(3):
-        u = mm(e4, jnp.where(match4(k, (128, 128), 0, ny3), 1.0, 0.0).astype(BF16))
+        u = mm(e4, up4[k])
         for q in (k, k + 4):
             at = pl.ds(GUARD3 + q, n4, stride=8)
             eb3[at, :] = eb3[at, :] + u
@@ -781,10 +796,7 @@
     wide = [jnp.concatenate(p, axis=1) for p in zip(*[split(spread[k]) for k in range(3)])]
     coarse = []
     for h in range(2):
-        r = iota2((112, 384), 0)
-        l = iota2((112, 384), 1)
-        hit = (6 * gx + 3 * h + (r >> 4) - 2 == (l >> 5)) & (6 * gy + (r & 15) - 2 == (l & 31)) & ((r & 15) < 10)
-        pick = jnp.where(hit, 1.0, 0.0).astype(BF16)
+        pick = picks[h]
         parts = [
             lax.dot_general(pick, p, (((1,), (1,)), ((), ())), preferred_element_type=F32) for p in wide
         ]
@@ -882,6 +894,8 @@
     scratch += [pltpu.VMEM((128, 128), BF16)] * 2 + [pltpu.VMEM((16 * 56, 128), F32)]
     scratch += [pltpu.VMEM((128, 128), F32)] * 2
     scratch += [pltpu.VMEM((3, 128, 128), F32), pltpu.VMEM((40, 128), F32)]
+    scratch += [pltpu.VMEM((128, 384), BF16), pltpu.VMEM((2, 112, 384), BF16)]
+    scratch += [pltpu.VMEM((3, 128, 128), BF16)] * 2
     groups = [p.scratch() for p in PLANS] + [gather_scratch(sizes)] * 2
     devices = sizes[0] * sizes[1] * sizes[2]
     groups += [[pltpu.VMEM((devices, 1, 128), F32)] + [pltpu.SemaphoreType.DMA((1,))] * 2]

time: 45.2 us -> 45.1 us (level)
  no operation moved by 1% of the time
where the time goes in v12:
time: 45.1 us; the launch traced here: 45 us
  Pallas kernels  44.4 us (98%)
  between operations  0.64 us (1%)
    pallas_call x1, Pallas kernels, body(): pl.pallas_call(functools.partial(kernel, sizes, counts), out_shape=[whole...  42.7 us
    pallas_call x1, Pallas kernels, body(): pl.pallas_call(finish, out_shape=[shape, shape], in_specs=[vmem] * 5, out...  1.68 us

profile of v12, /device:TPU:1, one launch (start us, length us, event | category | flops | bytes accessed | tf_op | source)
XLA Modules:
  0.0 45.0 jit_solution(17418730318787859020)
XLA Ops:
  0.6 42.7 %shard_map.50 = (f32[1808,128]{1,0:T(8,128)S(1)}, f32[1808,128]{1,0:T(8,128)S(1)}, f32[1808,128]{1,0:T(8,128)S(1)}, f32[1808,128]{1,0:T(8,128)S(1)}, f32[8,128]{1,0:T(8,128)S(1)}) custom-call(f32[48,48,48]{2,1,0:T(8,128)} %right_in.1, f32[48,48,48]{2,1,0:T(8,128)} %guess_in.1, f32[48,48,48]{2,1,0:T(8,128)} %react_in.1), custom_call_target="tpu_custom_call" | custom-call | tf_op jit(solution)/shard_map/pallas_call | solution.py:911
  43.3 1.7 %shard_map.51 = (f32[48,48,48]{2,1,0:T(8,128)}, f32[48,48,48]{2,1,0:T(8,128)}) custom-call(f32[1808,128]{1,0:T(8,128)S(1)} %get-tuple-element.7.guess, f32[1808,128]{1,0:T(8,128)S(1)} %get-tuple-element.8.r0, f32[1808,128]{1,0:T(8,128)S(1)} %get-tuple-element.9.eb0, f32[1808,128]{1,0:T(8,128)S(1)} %get-tuple-element.10.left0, ...), custom_call_target="tpu_custom_call" | custom-call | tf_op jit(solution)/shard_map/pallas_call | solution.py:923

commit v13 on v12

--- a/solution.py
+++ b/solution.py
@@ -718,9 +718,9 @@
 
     inverse_of(L1, s1, inv1, 0, 12)
 
+    ex_c.send()
     ex_b.x_sent()
     ex_b.unpack()
-    ex_c.send()
     first(L1, ea1, f1, inv1, 0, 12)
     relax(L1, ea1, eb1, f1, s1, inv1, 1, 11)
     ex_s.x_wait()

time: 45.1 us -> 45.3 us (level)
  no operation moved by 1% of the time
where the time goes in v13:
time: 45.3 us; the launch traced here: 45.2 us
  Pallas kernels  44.5 us (98%)
  between operations  0.64 us (1%)
    pallas_call x1, Pallas kernels, body(): pl.pallas_call(functools.partial(kernel, sizes, counts), out_shape=[whole...  42.8 us
    pallas_call x1, Pallas kernels, body(): pl.pallas_call(finish, out_shape=[shape, shape], in_specs=[vmem] * 5, out...  1.68 us

profile of v13, /device:TPU:1, one launch (start us, length us, event | category | flops | bytes accessed | tf_op | source)
XLA Modules:
  0.0 45.2 jit_solution(17074744263044606447)
XLA Ops:
  0.6 42.8 %shard_map.50 = (f32[1808,128]{1,0:T(8,128)S(1)}, f32[1808,128]{1,0:T(8,128)S(1)}, f32[1808,128]{1,0:T(8,128)S(1)}, f32[1808,128]{1,0:T(8,128)S(1)}, f32[8,128]{1,0:T(8,128)S(1)}) custom-call(f32[48,48,48]{2,1,0:T(8,128)} %right_in.1, f32[48,48,48]{2,1,0:T(8,128)} %guess_in.1, f32[48,48,48]{2,1,0:T(8,128)} %react_in.1), custom_call_target="tpu_custom_call" | custom-call | tf_op jit(solution)/shard_map/pallas_call | solution.py:911
  43.5 1.7 %shard_map.51 = (f32[48,48,48]{2,1,0:T(8,128)}, f32[48,48,48]{2,1,0:T(8,128)}) custom-call(f32[1808,128]{1,0:T(8,128)S(1)} %get-tuple-element.7.guess, f32[1808,128]{1,0:T(8,128)S(1)} %get-tuple-element.8.r0, f32[1808,128]{1,0:T(8,128)S(1)} %get-tuple-element.9.eb0, f32[1808,128]{1,0:T(8,128)S(1)} %get-tuple-element.10.left0, ...), custom_call_target="tpu_custom_call" | custom-call | tf_op jit(solution)/shard_map/pallas_call | solution.py:923

commit v14 on v12

--- a/solution.py
+++ b/solution.py
@@ -425,7 +425,7 @@
 
     def __init__(self, place, scratch, whole):
         self.place, self.whole = place, whole
-        self.mine, self.got, self.sum, self.ss, self.rs = scratch
+        self.mine, self.got, self.sum, self.parts, self.ss, self.rs = scratch
         n = place.sizes
         self.near = [(a, b) for a in range(n[0]) for b in range(n[1])][1:]
         self.near.sort(key=lambda p: -far((p[0], p[1], 0), n))
@@ -444,13 +444,28 @@
 
     def relay(self):
         self.copy(self.got, self.got, 0, self.place.beside(1, 0, 0)).wait_recv()
-        total = self.mine[...]
-        for k in range(len(self.near)):
-            total = total + self.got[k]
-        self.sum[...] = total
+        gx, gy, gz = self.place.me
+        ny = self.place.sizes[1]
+        lane = lanes(8)
+        sums = [[], []], [[], []]
+        for k, (a, b) in enumerate([(0, 0)] + self.near):
+            tile = self.mine[...] if k == 0 else self.got[k - 1]
+            start = 6 * lax.rem(gy + ny - b, ny)
+            for h in range(2):
+                y = (lane - 16 * h) & 31
+                sums[a][h].append(jnp.where((y >= start) & (y < start + 6), tile, 0.0))
+        for h in range(2):
+            own, other = (roll(tree(sums[a][h]), -16 * h) for a in range(2))
+            self.parts[pl.ds(16 * h, 8), :] = jnp.where(gx == 0, own, other)
+            self.parts[pl.ds(16 * h + 8, 8), :] = jnp.where(gx == 0, other, own)
+        for h in range(2):
+            r = 16 * h
+            self.sum[pl.ds(12 * h, 3, stride=4), :] = self.parts[pl.ds(r, 3), :]
+            self.sum[pl.ds(12 * h + 1, 3, stride=4), :] = self.parts[pl.ds(r + 4, 3), :] + self.parts[pl.ds(r + 8, 3), :]
+            self.sum[pl.ds(12 * h + 2, 3, stride=4), :] = self.parts[pl.ds(r + 12, 3), :]
         for c in self.line:
             self.copy(self.sum, self.whole.at[self.at, :], 1, self.place.beside(0, 0, c)).start()
-        self.whole[self.at, :] = total
+        self.whole[self.at, :] = self.sum[...]
 
     def finish(self):
         self.most().wait_recv()
@@ -466,9 +481,10 @@
 
 def gather_scratch(sizes):
     return [
+        pltpu.VMEM((8, 128), F32),
+        pltpu.VMEM((sizes[0] * sizes[1] - 1, 8, 128), F32),
         pltpu.VMEM((24, 128), F32),
-        pltpu.VMEM((sizes[0] * sizes[1] - 1, 24, 128), F32),
-        pltpu.VMEM((24, 128), F32),
+        pltpu.VMEM((32, 128), F32),
         pltpu.SemaphoreType.DMA((2,)),
         pltpu.SemaphoreType.DMA((2,)),
     ]
@@ -476,11 +492,11 @@
 
 def spread_to_level3(place):
     gx, gy, gz = place.me
-    r = iota2((128, 384), 0)
-    l = iota2((128, 384), 1)
+    r = iota2((128, 256), 0)
+    l = iota2((128, 256), 1)
     x = 6 * gx + 3 * (r >> 6) + ((r & 63) >> 3)
     y = 6 * gy + (r & 7)
-    hit = (x == (l >> 5)) & (y == (l & 31)) & ((r & 7) < 6) & ((r & 63) < 24)
+    hit = (x == (l >> 5) + 4 * gx) & (y == (l & 31)) & ((r & 7) < 6) & ((r & 63) < 24)
     return jnp.where(hit, 1.0, 0.0).astype(BF16)
 
 
@@ -497,8 +513,10 @@
     b = turned[pl.ds(64, 8, stride=2), :] + turned[pl.ds(65, 8, stride=2), :]
     a = (a + roll(b, 64)) * 0.125
     out = mm(a, chosen[...])
-    for k in range(3):
-        mine[pl.ds(k, 6, stride=4), :] = out[0:6, 128 * k : 128 * k + 128]
+    for k in range(2):
+        turned[pl.ds(8 * k, 8), :] = out[:, 128 * k : 128 * k + 128]
+    for k in range(2):
+        mine[pl.ds(4 * k, 3), :] = turned[pl.ds(8 * k, 3), :] + roll(turned[pl.ds(8 * k + 3, 3), :], 16)
 
 
 def image3(ref, s_ref, r, n):
@@ -671,8 +689,9 @@
     restrict(react, L0, s1, L1, 0, 12, 0, 24, down_m, tmp)
     restrict(s1, L1, s2, L2, 0, 6, 0, 12, down_m, tmp)
     ex_s.pack()
-    ga_s.mine[...] = jnp.zeros((24, 128), F32)
-    ga_f.mine[...] = jnp.zeros((24, 128), F32)
+    for e in (ga_s, ga_f):
+        e.mine[...] = jnp.zeros((8, 128), F32)
+        e.sum[...] = jnp.zeros((24, 128), F32)
     chosen[...] = spread_to_level3(place)
     to_level3(s2, ga_s.mine, square, turned, chosen)
     for h in range(2):
@@ -894,7 +913,7 @@
     scratch += [pltpu.VMEM((128, 128), BF16)] * 2 + [pltpu.VMEM((16 * 56, 128), F32)]
     scratch += [pltpu.VMEM((128, 128), F32)] * 2
     scratch += [pltpu.VMEM((3, 128, 128), F32), pltpu.VMEM((40, 128), F32)]
-    scratch += [pltpu.VMEM((128, 384), BF16), pltpu.VMEM((2, 112, 384), BF16)]
+    scratch += [pltpu.VMEM((128, 256), BF16), pltpu.VMEM((2, 112, 384), BF16)]
     scratch += [pltpu.VMEM((3, 128, 128), BF16)] * 2
     groups = [p.scratch() for p in PLANS] + [gather_scratch(sizes)] * 2
     devices = sizes[0] * sizes[1] * sizes[2]

time: 45.1 us -> 45 us (level)
  no operation moved by 1% of the time
where the time goes in v14:
time: 45 us; the launch traced here: 44.9 us
  Pallas kernels  44.2 us (98%)
  between operations  0.64 us (1%)
    pallas_call x1, Pallas kernels, body(): pl.pallas_call(functools.partial(kernel, sizes, counts), out_shape=[whole...  42.5 us
    pallas_call x1, Pallas kernels, body(): pl.pallas_call(finish, out_shape=[shape, shape], in_specs=[vmem] * 5, out...  1.68 us

profile of v14, /device:TPU:1, one launch (start us, length us, event | category | flops | bytes accessed | tf_op | source)
XLA Modules:
  0.0 44.9 jit_solution(12040399243113234591)
XLA Ops:
  0.6 42.5 %shard_map.50 = (f32[1808,128]{1,0:T(8,128)S(1)}, f32[1808,128]{1,0:T(8,128)S(1)}, f32[1808,128]{1,0:T(8,128)S(1)}, f32[1808,128]{1,0:T(8,128)S(1)}, f32[8,128]{1,0:T(8,128)S(1)}) custom-call(f32[48,48,48]{2,1,0:T(8,128)} %right_in.1, f32[48,48,48]{2,1,0:T(8,128)} %guess_in.1, f32[48,48,48]{2,1,0:T(8,128)} %react_in.1), custom_call_target="tpu_custom_call" | custom-call | tf_op jit(solution)/shard_map/pallas_call | solution.py:930
  43.2 1.7 %shard_map.51 = (f32[48,48,48]{2,1,0:T(8,128)}, f32[48,48,48]{2,1,0:T(8,128)}) custom-call(f32[1808,128]{1,0:T(8,128)S(1)} %get-tuple-element.7.guess, f32[1808,128]{1,0:T(8,128)S(1)} %get-tuple-element.8.r0, f32[1808,128]{1,0:T(8,128)S(1)} %get-tuple-element.9.eb0, f32[1808,128]{1,0:T(8,128)S(1)} %get-tuple-element.10.left0, ...), custom_call_target="tpu_custom_call" | custom-call | tf_op jit(solution)/shard_map/pallas_call | solution.py:942

commit v15 on v14

--- a/solution.py
+++ b/solution.py
@@ -648,22 +648,8 @@
     barrier = pltpu.get_barrier_semaphore()
     for p in greeted:
         pl.semaphore_signal(barrier, inc=1, device_id=place.beside(*p), device_id_type=MESH)
-    for ref in (guess, right, react, f1, s1, ea1, eb1, f2, s2, ea2, eb2, ea3, eb3, p4, square):
-        clear(ref)
-    spread[...] = jnp.zeros_like(spread)
-    for ref in (f3, s3, inv3):
-        for r in (0, GUARD3 + n3):
-            ref[pl.ds(r, GUARD3), :] = jnp.zeros((GUARD3, 128), F32)
-
-    a = iota2((128, 128), 0)
-    b = iota2((128, 128), 1)
-    signed = lambda v: ((v + 8) & 63) - 8
-    base = lambda v: ((v + 8) & 127) & 64
-    zb = signed(b)
-    hit = ((a == ((base(b) + 2 * zb) & 127)) | (a == ((base(b) + 2 * zb + 1) & 127))) & (zb >= -8) & (zb < 24)
-    down_m[...] = jnp.where(hit, 0.125, 0.0).astype(BF16)
-    hit = a == ((base(b) + (zb >> 1)) & 127)
-    up_m[...] = jnp.where(hit, 1.0, 0.0).astype(BF16)
+    for ref in (guess, right, react):
+        ref[...] = jnp.zeros_like(ref)
 
     ex_a = Exchange(PLAN_A, (guess, right, react), scr[0], place)
     ex_s = Exchange(PLAN_S, (s1, s2), scr[1], place)
@@ -685,6 +671,24 @@
 
     pl.semaphore_wait(barrier, len(greeted))
     ex_a.send()
+
+    for ref in (f1, s1, ea1, eb1, f2, s2, ea2, eb2, ea3, eb3, p4, square):
+        clear(ref)
+    spread[...] = jnp.zeros_like(spread)
+    for ref in (f3, s3, inv3):
+        for r in (0, GUARD3 + n3):
+            ref[pl.ds(r, GUARD3), :] = jnp.zeros((GUARD3, 128), F32)
+
+    a = iota2((128, 128), 0)
+    b = iota2((128, 128), 1)
+    signed = lambda v: ((v + 8) & 63) - 8
+    base = lambda v: ((v + 8) & 127) & 64
+    zb = signed(b)
+    hit = ((a == ((base(b) + 2 * zb) & 127)) | (a == ((base(b) + 2 * zb + 1) & 127))) & (zb >= -8) & (zb < 24)
+    down_m[...] = jnp.where(hit, 0.125, 0.0).astype(BF16)
+    hit = a == ((base(b) + (zb >> 1)) & 127)
+    up_m[...] = jnp.where(hit, 1.0, 0.0).astype(BF16)
+
 
     restrict(react, L0, s1, L1, 0, 12, 0, 24, down_m, tmp)
     restrict(s1, L1, s2, L2, 0, 6, 0, 12, down_m, tmp)

time: 45 us -> 45 us (level)
  no operation moved by 1% of the time
where the time goes in v15:
time: 45 us; the launch traced here: 44.9 us
  Pallas kernels  44.2 us (98%)
  between operations  0.64 us (1%)
    pallas_call x1, Pallas kernels, body(): pl.pallas_call(functools.partial(kernel, sizes, counts), out_shape=[whole...  42.5 us
    pallas_call x1, Pallas kernels, body(): pl.pallas_call(finish, out_shape=[shape, shape], in_specs=[vmem] * 5, out...  1.68 us

profile of v15, /device:TPU:1, one launch (start us, length us, event | category | flops | bytes accessed | tf_op | source)
XLA Modules:
  0.0 44.9 jit_solution(7600659774646531264)
XLA Ops:
  0.6 42.5 %shard_map.50 = (f32[1808,128]{1,0:T(8,128)S(1)}, f32[1808,128]{1,0:T(8,128)S(1)}, f32[1808,128]{1,0:T(8,128)S(1)}, f32[1808,128]{1,0:T(8,128)S(1)}, f32[8,128]{1,0:T(8,128)S(1)}) custom-call(f32[48,48,48]{2,1,0:T(8,128)} %right_in.1, f32[48,48,48]{2,1,0:T(8,128)} %guess_in.1, f32[48,48,48]{2,1,0:T(8,128)} %react_in.1), custom_call_target="tpu_custom_call" | custom-call | tf_op jit(solution)/shard_map/pallas_call | solution.py:934
  43.2 1.7 %shard_map.51 = (f32[48,48,48]{2,1,0:T(8,128)}, f32[48,48,48]{2,1,0:T(8,128)}) custom-call(f32[1808,128]{1,0:T(8,128)S(1)} %get-tuple-element.7.guess, f32[1808,128]{1,0:T(8,128)S(1)} %get-tuple-element.8.r0, f32[1808,128]{1,0:T(8,128)S(1)} %get-tuple-element.9.eb0, f32[1808,128]{1,0:T(8,128)S(1)} %get-tuple-element.10.left0, ...), custom_call_target="tpu_custom_call" | custom-call | tf_op jit(solution)/shard_map/pallas_call | solution.py:946

commit v16 on v15

--- a/solution.py
+++ b/solution.py
@@ -163,6 +163,7 @@
 class Item:
     def __init__(self, geo, w):
         self.g, self.w = geo, w
+        self.deep = w - 1 if geo is L0 else w
 
 
 class Plan:
@@ -309,6 +310,8 @@
             for e, y in enumerate((g.ny - d, d - 1)):
                 v = ref[pl.ds(self.source(k, 0, y), n, stride=g.R), :]
                 self.sent[pl.ds(self.plan.y0[e] + self.yo, n), :] = v
+                if d > it.deep:
+                    continue
                 if n < self.plan.drows:
                     v = jnp.concatenate([v, jnp.zeros((self.plan.drows - n, 128), F32)], axis=0)
                 for q, z in enumerate((g.nz - w, 0)):
@@ -351,7 +354,7 @@
                 at = co + (d - 1) * w
                 for e, y in enumerate((-d, g.ny + d - 1)):
                     v = self.got[pl.ds(self.plan.y0[e] + yo, n), :]
-                    for q, z in enumerate((-w, g.nz)):
+                    for q, z in enumerate((-w, g.nz) if d <= it.deep else ()):
                         got = self.got[pl.ds(self.plan.d0[2 * e + q], n), :] * mz[q]
                         v = jnp.where(into[q], roll(got, z - at), v)
                     ref, r = self.target(k, 0, y)

time: 45 us -> 45 us (level)
  no operation moved by 1% of the time
where the time goes in v16:
time: 45 us; the launch traced here: 44.8 us
  Pallas kernels  44.2 us (98%)
  between operations  0.64 us (1%)
    pallas_call x1, Pallas kernels, body(): pl.pallas_call(functools.partial(kernel, sizes, counts), out_shape=[whole...  42.5 us
    pallas_call x1, Pallas kernels, body(): pl.pallas_call(finish, out_shape=[shape, shape], in_specs=[vmem] * 5, out...  1.68 us

profile of v16, /device:TPU:1, one launch (start us, length us, event | category | flops | bytes accessed | tf_op | source)
XLA Modules:
  0.0 44.8 jit_solution(10321078953744300341)
XLA Ops:
  0.6 42.5 %shard_map.50 = (f32[1808,128]{1,0:T(8,128)S(1)}, f32[1808,128]{1,0:T(8,128)S(1)}, f32[1808,128]{1,0:T(8,128)S(1)}, f32[1808,128]{1,0:T(8,128)S(1)}, f32[8,128]{1,0:T(8,128)S(1)}) custom-call(f32[48,48,48]{2,1,0:T(8,128)} %right_in.1, f32[48,48,48]{2,1,0:T(8,128)} %guess_in.1, f32[48,48,48]{2,1,0:T(8,128)} %react_in.1), custom_call_target="tpu_custom_call" | custom-call | tf_op jit(solution)/shard_map/pallas_call | solution.py:937
  43.1 1.7 %shard_map.51 = (f32[48,48,48]{2,1,0:T(8,128)}, f32[48,48,48]{2,1,0:T(8,128)}) custom-call(f32[1808,128]{1,0:T(8,128)S(1)} %get-tuple-element.7.guess, f32[1808,128]{1,0:T(8,128)S(1)} %get-tuple-element.8.r0, f32[1808,128]{1,0:T(8,128)S(1)} %get-tuple-element.9.eb0, f32[1808,128]{1,0:T(8,128)S(1)} %get-tuple-element.10.left0, ...), custom_call_target="tpu_custom_call" | custom-call | tf_op jit(solution)/shard_map/pallas_call | solution.py:949

commit v17 on v15

--- a/solution.py
+++ b/solution.py
@@ -555,8 +555,17 @@
     return total
 
 
-def dot_all(a, b):
-    return jnp.sum(jnp.sum(a * b, axis=0, keepdims=True), axis=1, keepdims=True)
+def both_sums(a, b):
+    fold = lambda v: tree([v[k : k + 8] for k in range(0, v.shape[0], 8)])
+    rest = jnp.concatenate([fold(a), fold(b)], axis=0)
+    ones = jnp.ones((128, 128), BF16)
+    parts = []
+    for _ in range(3):
+        part = rest.astype(BF16)
+        rest = rest - part.astype(F32)
+        parts.append(jnp.dot(part, ones, preferred_element_type=F32))
+    total = parts[0] + (parts[1] + parts[2])
+    return jnp.sum(total[0:8], axis=0, keepdims=True), jnp.sum(total[8:16], axis=0, keepdims=True)
 
 
 def bottom(source, s4, p4, n, ny):
@@ -570,8 +579,7 @@
         b = b + (roll(left, 1) + roll(left, -1))
         b = b + (roll(left, 16) + roll(left, -16))
         image = shifted * left - FACTOR4 * jnp.where(inside, b, 0.0)
-        now = dot_all(left, left)
-        bent = dot_all(left, image)
+        now, bent = both_sums(left * left, left * image)
         if it == 0:
             denom = bent
             direction, turned = left, image

time: 45 us -> 45.5 us (1.011)
  Pallas kernels: 44.2 us -> 44.7 us
    pallas_call x1, Pallas kernels: 42.5 us -> 43 us  [body(): pl.pallas_call(functools.partial(kernel, sizes, counts), out_shape=[whole...]
where the time goes in v17:
time: 45.5 us; the launch traced here: 45.3 us
  Pallas kernels  44.7 us (98%)
  between operations  0.64 us (1%)
    pallas_call x1, Pallas kernels, body(): pl.pallas_call(functools.partial(kernel, sizes, counts), out_shape=[whole...  43 us
    pallas_call x1, Pallas kernels, body(): pl.pallas_call(finish, out_shape=[shape, shape], in_specs=[vmem] * 5, out...  1.68 us

profile of v17, /device:TPU:1, one launch (start us, length us, event | category | flops | bytes accessed | tf_op | source)
XLA Modules:
  0.0 45.3 jit_solution(413504046354776392)
XLA Ops:
  0.6 43.0 %shard_map.50 = (f32[1808,128]{1,0:T(8,128)S(1)}, f32[1808,128]{1,0:T(8,128)S(1)}, f32[1808,128]{1,0:T(8,128)S(1)}, f32[1808,128]{1,0:T(8,128)S(1)}, f32[8,128]{1,0:T(8,128)S(1)}) custom-call(f32[48,48,48]{2,1,0:T(8,128)} %right_in.1, f32[48,48,48]{2,1,0:T(8,128)} %guess_in.1, f32[48,48,48]{2,1,0:T(8,128)} %react_in.1), custom_call_target="tpu_custom_call" | custom-call | tf_op jit(solution)/shard_map/pallas_call | solution.py:942
  43.7 1.7 %shard_map.51 = (f32[48,48,48]{2,1,0:T(8,128)}, f32[48,48,48]{2,1,0:T(8,128)}) custom-call(f32[1808,128]{1,0:T(8,128)S(1)} %get-tuple-element.7.guess, f32[1808,128]{1,0:T(8,128)S(1)} %get-tuple-element.8.r0, f32[1808,128]{1,0:T(8,128)S(1)} %get-tuple-element.9.eb0, f32[1808,128]{1,0:T(8,128)S(1)} %get-tuple-element.10.left0, ...), custom_call_target="tpu_custom_call" | custom-call | tf_op jit(solution)/shard_map/pallas_call | solution.py:954

commit v18 on v15

--- a/solution.py
+++ b/solution.py
@@ -884,8 +884,7 @@
 
 def finish(guess, r0, eb0, left0, step_ref, field_out, resid_out, field, resid, sems):
     step = step_ref[0:1, :]
-    copies = []
-    parts, size = 4, 6
+    parts, size = 6, 4
     for p in range(parts):
         for x in range(p * size, p * size + size):
             at = pl.ds(L0.row(x, 0), 48)
@@ -898,11 +897,9 @@
         for q, (src, dst) in enumerate(((field, field_out), (resid, resid_out))):
             for h in range(2):
                 at = pl.ds(p * size + 24 * h, size)
-                c = pltpu.make_async_copy(src.at[at], dst.at[at], sems.at[4 * p + 2 * q + h])
-                c.start()
-                copies.append(c)
-    for c in copies:
-        c.wait()
+                pltpu.make_async_copy(src.at[at], dst.at[at], sems.at[q]).start()
+    for q, (src, dst) in enumerate(((field, field_out), (resid, resid_out))):
+        pltpu.make_async_copy(src, dst, sems.at[q]).wait()
 
 
 def solution(mesh):
@@ -948,7 +945,7 @@
                 out_shape=[shape, shape],
                 in_specs=[vmem] * 5,
                 out_specs=[anywhere] * 2,
-                scratch_shapes=[pltpu.VMEM(right_side.shape, F32)] * 2 + [pltpu.SemaphoreType.DMA((16,))],
+                scratch_shapes=[pltpu.VMEM(right_side.shape, F32)] * 2 + [pltpu.SemaphoreType.DMA((2,))],
                 compiler_params=pltpu.CompilerParams(vmem_limit_bytes=16 * 2**20),
             )(*parts)
         )

time: 45 us -> 44.8 us (level)
  no operation moved by 1% of the time
where the time goes in v18:
time: 44.8 us; the launch traced here: 44.7 us
  Pallas kernels  44.1 us (98%)
  between operations  0.64 us (1%)
    pallas_call x1, Pallas kernels, body(): pl.pallas_call(functools.partial(kernel, sizes, counts), out_shape=[whole...  42.5 us
    pallas_call x1, Pallas kernels, body(): pl.pallas_call(finish, out_shape=[shape, shape], in_specs=[vmem] * 5, out...  1.52 us

profile of v18, /device:TPU:1, one launch (start us, length us, event | category | flops | bytes accessed | tf_op | source)
XLA Modules:
  0.0 44.7 jit_solution(11138382669668256152)
XLA Ops:
  0.6 42.5 %shard_map.50 = (f32[1808,128]{1,0:T(8,128)S(1)}, f32[1808,128]{1,0:T(8,128)S(1)}, f32[1808,128]{1,0:T(8,128)S(1)}, f32[1808,128]{1,0:T(8,128)S(1)}, f32[8,128]{1,0:T(8,128)S(1)}) custom-call(f32[48,48,48]{2,1,0:T(8,128)} %right_in.1, f32[48,48,48]{2,1,0:T(8,128)} %guess_in.1, f32[48,48,48]{2,1,0:T(8,128)} %react_in.1), custom_call_target="tpu_custom_call" | custom-call | tf_op jit(solution)/shard_map/pallas_call | solution.py:931
  43.2 1.5 %shard_map.51 = (f32[48,48,48]{2,1,0:T(8,128)}, f32[48,48,48]{2,1,0:T(8,128)}) custom-call(f32[1808,128]{1,0:T(8,128)S(1)} %get-tuple-element.7.guess, f32[1808,128]{1,0:T(8,128)S(1)} %get-tuple-element.8.r0, f32[1808,128]{1,0:T(8,128)S(1)} %get-tuple-element.9.eb0, f32[1808,128]{1,0:T(8,128)S(1)} %get-tuple-element.10.left0, ...), custom_call_target="tpu_custom_call" | custom-call | tf_op jit(solution)/shard_map/pallas_call | solution.py:943

commit v19 on v18

--- a/solution.py
+++ b/solution.py
@@ -163,6 +163,7 @@
 class Item:
     def __init__(self, geo, w):
         self.g, self.w = geo, w
+        self.deep = w - 1 if geo is L0 else w
 
 
 class Plan:
@@ -309,6 +310,8 @@
             for e, y in enumerate((g.ny - d, d - 1)):
                 v = ref[pl.ds(self.source(k, 0, y), n, stride=g.R), :]
                 self.sent[pl.ds(self.plan.y0[e] + self.yo, n), :] = v
+                if d > it.deep:
+                    continue
                 if n < self.plan.drows:
                     v = jnp.concatenate([v, jnp.zeros((self.plan.drows - n, 128), F32)], axis=0)
                 for q, z in enumerate((g.nz - w, 0)):
@@ -351,7 +354,7 @@
                 at = co + (d - 1) * w
                 for e, y in enumerate((-d, g.ny + d - 1)):
                     v = self.got[pl.ds(self.plan.y0[e] + yo, n), :]
-                    for q, z in enumerate((-w, g.nz)):
+                    for q, z in enumerate((-w, g.nz) if d <= it.deep else ()):
                         got = self.got[pl.ds(self.plan.d0[2 * e + q], n), :] * mz[q]
                         v = jnp.where(into[q], roll(got, z - at), v)
                     ref, r = self.target(k, 0, y)

time: 44.8 us -> 44.8 us (level)
  no operation moved by 1% of the time
where the time goes in v19:
time: 44.8 us; the launch traced here: 44.7 us
  Pallas kernels  44 us (98%)
  between operations  0.64 us (1%)
    pallas_call x1, Pallas kernels, body(): pl.pallas_call(functools.partial(kernel, sizes, counts), out_shape=[whole...  42.5 us
    pallas_call x1, Pallas kernels, body(): pl.pallas_call(finish, out_shape=[shape, shape], in_specs=[vmem] * 5, out...  1.52 us

profile of v19, /device:TPU:1, one launch (start us, length us, event | category | flops | bytes accessed | tf_op | source)
XLA Modules:
  0.0 44.7 jit_solution(17698870030735175259)
XLA Ops:
  0.6 42.5 %shard_map.50 = (f32[1808,128]{1,0:T(8,128)S(1)}, f32[1808,128]{1,0:T(8,128)S(1)}, f32[1808,128]{1,0:T(8,128)S(1)}, f32[1808,128]{1,0:T(8,128)S(1)}, f32[8,128]{1,0:T(8,128)S(1)}) custom-call(f32[48,48,48]{2,1,0:T(8,128)} %right_in.1, f32[48,48,48]{2,1,0:T(8,128)} %guess_in.1, f32[48,48,48]{2,1,0:T(8,128)} %react_in.1), custom_call_target="tpu_custom_call" | custom-call | tf_op jit(solution)/shard_map/pallas_call | solution.py:934
  43.1 1.5 %shard_map.51 = (f32[48,48,48]{2,1,0:T(8,128)}, f32[48,48,48]{2,1,0:T(8,128)}) custom-call(f32[1808,128]{1,0:T(8,128)S(1)} %get-tuple-element.7.guess, f32[1808,128]{1,0:T(8,128)S(1)} %get-tuple-element.8.r0, f32[1808,128]{1,0:T(8,128)S(1)} %get-tuple-element.9.eb0, f32[1808,128]{1,0:T(8,128)S(1)} %get-tuple-element.10.left0, ...), custom_call_target="tpu_custom_call" | custom-call | tf_op jit(solution)/shard_map/pallas_call | solution.py:946
